TPU v7x, 32 devices: a whole 2x2x4 slice. The times are simulated.
32 devices in a mesh: depth: 2 (over y), azim: 16 (over z, x, core).
Axes of the slice: x: 2, y: 2, z: 4, core: 2. Of those that a mesh axis runs over, the one named last changes fastest.
Arguments:
- cotangent: bfloat16 [128, 4096, 256], P('depth', 'azim'), may hold values from -6 to 6
- pre_second: bfloat16 [128, 4096, 256], P('depth', 'azim'), may hold values from -6 to 6
- pre_first: bfloat16 [128, 4096, 256], P('depth', 'azim'), may hold values from -6 to 6
- kernel_first: bfloat16 [3, 3, 3, 32, 32], replicated, may hold values from -0.21875 to 0.21875
- kernel_second: bfloat16 [3, 3, 3, 32, 32], replicated, may hold values from -0.21875 to 0.21875
- row_resample: float32 [4, 128, 8, 8], P(None, 'depth'), may hold values from -0.1875 to 0.1875
- col_taps: float32 [4, 128, 8], P(None, 'depth'), may hold values from 0.1 to 1
- band_width: int32 [4, 128], P(None, 'depth'), may hold values from 1 to 8
- col_offset: int32 [4, 128], P(None, 'depth'), may hold values from -24 to 24, as said below
Outputs:
- cam_grad: float32 [8, 4096, 128], P('depth', 'azim')
Inputs may be any that keep to these rules, and one draw needn't show every extreme that they name: `col_offset`: some entry equals -24 and some entry equals 24.
All inputs are finite; a program needn't handle non-finite values.
Results may differ from a plain program's by a relative error of at most 0.0048.
Values may be sent and summed in bfloat16 or wider, within the bound.
No kernel may reach another device: no remote copies, remote signals or barrier semaphores. Data moves between devices by JAX's collectives and lax.ppermute only.
A program may use at most 256 MiB of HBM per device.

v0:
```python
import jax
import jax.numpy as jnp
from jax import lax
from jax.sharding import PartitionSpec as P

TAPS = 8
SHIFT = 24


def padded_2(block, sides, width):
    for axis, dim in sides:
        count = lax.axis_size(axis)
        forward = [(i, i + 1) for i in range(count - 1)]
        forward.append((count - 1, 0))
        backward = [(target, source) for source, target in forward]
        low = lax.ppermute(
            lax.slice_in_dim(block, block.shape[dim] - width, None, axis=dim), axis, forward
        )
        high = lax.ppermute(lax.slice_in_dim(block, 0, width, axis=dim), axis, backward)
        block = jnp.concatenate([low, block, high], axis=dim)
    return block


def row_mixers(kernel, row_count):
    channels = kernel.shape[3]
    row_in = lax.broadcasted_iota(jnp.int32, (row_count, 1, row_count, 1), 0)
    row_out = lax.broadcasted_iota(jnp.int32, (row_count, 1, row_count, 1), 2)
    mixers = []
    for depth_tap in range(3):
        group = []
        for column_tap in range(3):
            mixed = jnp.zeros((row_count, channels, row_count, channels), jnp.bfloat16)
            for row_tap in range(3):
                block = kernel[depth_tap, column_tap, row_tap].T[None, :, None, :]
                mixed = mixed + jnp.where(
                    row_in == row_out + 1 - row_tap, block, jnp.zeros((), jnp.bfloat16)
                )
            group.append(mixed.reshape(row_count * channels, row_count * channels))
        mixers.append(group)
    return mixers


def transpose_conv(padded, mixers):
    sphere_span, column_span, merged = padded.shape
    out_spheres = sphere_span - 2
    out_columns = column_span - 2
    accumulated = jnp.zeros((out_spheres * out_columns, merged), jnp.float32)
    for depth_tap in range(3):
        for column_tap in range(3):
            slab = padded[
                2 - depth_tap : 2 - depth_tap + out_spheres,
                2 - column_tap : 2 - column_tap + out_columns,
            ]
            accumulated = accumulated + jnp.dot(
                slab.reshape(-1, merged),
                mixers[depth_tap][column_tap],
                preferred_element_type=jnp.float32,
            )
    return accumulated.reshape(out_spheres, out_columns, merged)


def clear_rims(extended, width, sphere_dim):
    device_index = lax.axis_index("depth")
    last_device = lax.axis_size("depth") - 1
    extent = extended.shape[sphere_dim]
    position = lax.broadcasted_iota(jnp.int32, (extent,), 0)
    outside = (position < width) & (device_index == 0) | (position >= extent - width) & (
        device_index == last_device
    )
    layout = [1] * extended.ndim
    layout[sphere_dim] = extent
    return jnp.where(outside.reshape(layout), jnp.zeros_like(extended), extended)


def faces_once(volume):
    extended = padded_2(volume, (("depth", 0), ("azim", 1)), 1)
    return clear_rims(extended, 1, 0)


def band_matrix(taps_camera, offsets_camera, big_count, small_count, margin, direction):
    tap_count = taps_camera.shape[1]
    big_index = lax.broadcasted_iota(jnp.int32, (1, big_count, 1, 1), 1)
    small_index = lax.broadcasted_iota(jnp.int32, (1, 1, small_count, 1), 2)
    tap_index = lax.broadcasted_iota(jnp.int32, (1, 1, 1, tap_count), 3)
    target = small_index + margin + direction * (offsets_camera[:, None, None, None] + tap_index)
    chosen = jnp.where(
        big_index == target, taps_camera[:, None, None, :], jnp.zeros((), jnp.bfloat16)
    )
    return jnp.sum(chosen, axis=3, dtype=jnp.bfloat16)


def camera_terms(
    source,
    row_resample,
    band_taps,
    col_offset,
    big_count,
    small_count,
    margin,
    direction,
    row_count,
    channels,
):
    sphere_count = source.shape[0]
    pieces = []
    for camera in range(band_taps.shape[0]):
        matrix = band_matrix(
            band_taps[camera], col_offset[camera], big_count, small_count, margin, direction
        )
        pulled = jnp.einsum("sbw,sbx->swx", matrix, source, preferred_element_type=jnp.float32)
        pulled = pulled.reshape(sphere_count, -1, row_count, channels)
        pieces.append(
            jnp.einsum(
                "shg,swhc->gwc", row_resample[camera], pulled, precision=lax.Precision.HIGHEST
            )
        )
    return jnp.concatenate(pieces, axis=-1)


def body(
    cotangent,
    pre_second,
    pre_first,
    kernel_first,
    kernel_second,
    row_resample,
    col_taps,
    band_width,
    col_offset,
):
    sphere_count, column_count, merged = cotangent.shape
    channels = kernel_first.shape[3]
    row_count = merged // channels
    mixers_second = row_mixers(kernel_second, row_count)
    mixers_first = row_mixers(kernel_first, row_count)
    second_grad = jnp.where(pre_second > 0, cotangent, jnp.zeros_like(cotangent))
    hidden_grad = transpose_conv(faces_once(second_grad), mixers_second)
    first_grad = (hidden_grad * (pre_first > 0).astype(jnp.float32)).astype(jnp.bfloat16)
    volume_grad = transpose_conv(faces_once(first_grad), mixers_first).astype(jnp.bfloat16)
    margin = SHIFT + TAPS
    band_keep = lax.broadcasted_iota(jnp.int32, col_taps.shape, 2) < band_width[:, :, None]
    band_taps = jnp.where(band_keep, col_taps, jnp.zeros_like(col_taps)).astype(jnp.bfloat16)
    extended = padded_2(volume_grad, (("azim", 1),), margin)
    partial_value = camera_terms(
        extended,
        row_resample,
        band_taps,
        col_offset,
        column_count + 2 * margin,
        column_count,
        margin,
        1,
        row_count,
        channels,
    )
    return lax.psum_scatter(partial_value, "depth", scatter_dimension=0, tiled=True)


def solution(mesh):
    placed = (
        P("depth", "azim", None),
        P("depth", "azim", None),
        P("depth", "azim", None),
        P(),
        P(),
        P(None, "depth", None, None),
        P(None, "depth", None),
        P(None, "depth"),
        P(None, "depth"),
    )
    return jax.shard_map(
        body, mesh=mesh, in_specs=placed, out_specs=P("depth", "azim", None), check_vma=False
    )
```

profile of v0, /device:TPU:0, one launch (start us, length us, event | category | flops | bytes accessed | tf_op | source)
XLA Modules:
  0.0 1039.6 jit_solution(9617606342221660304)
XLA Ops:
  31.5 106.6 %fusion.7 = bf16[64,320,256]{2,1,0:T(8,128)(2,1)} fusion(s32[64,256,8]{1,2,0:T(8,128)S(1)} %get-tuple-element.113, bf16[64,8]{1,0:T(8,128)(2,1)S(1)} %copy.136), kind=kLoop, calls=%fused_computation.11 | loop fusion | flops 120586240 | bytes 11011072 | tf_op jit(solution)/shard_map/reduce_sum | solution.py:89
  138.1 107.1 %fusion.6 = bf16[64,320,256]{2,1,0:T(8,128)(2,1)} fusion(s32[64,256,8]{1,2,0:T(8,128)S(1)} %get-tuple-element.114, bf16[64,8]{1,0:T(8,128)(2,1)S(1)} %copy.192), kind=kLoop, calls=%fused_computation.10 | loop fusion | flops 120586240 | bytes 11011072 | tf_op jit(solution)/shard_map/reduce_sum | solution.py:89
  281.1 26.6 %fusion.42 = (bf16[64,256,256]{2,1,0:T(8,128)(2,1)}, bf16[64,256,256]{2,1,0:T(8,128)(2,1)}, bf16[64,256,256]{2,1,0:T(8,128)(2,1)}, bf16[64,256,256]{2,1,0:T(8,12...) fusion(bf16[66,258,256]{2,1,0:T(8,128)(2,1)S(1)} %maximum_selec, ...), kind=kLoop, calls=%fused_computation.163 | loop fusion | bytes 150994944 | tf_op jit(solution)/shard_map/slice | solution.py:50
  319.5 16.5 %convolution_add_fusion.15 = f32[16384,256]{1,0:T(8,128)} fusion(f32[16384,256]{1,0:T(8,128)} %fusion.46, bf16[16384,256]{1,0:T(8,128)(2,1)} %bitcast.397, bf16[256,256]{1,0:T(8,128)(2,1)S(1)} %copy-done.20), kind=kOutput, calls=%fused_computation.28 | convolution fusion | flops 2151677952 | bytes 42074112 | tf_op jit(solution)/shard_map/dot_general | solution.py:54
  336.0 13.9 %convolution_add_fusion.14 = f32[16384,256]{1,0:T(8,128)} fusion(f32[16384,256]{1,0:T(8,128)} %convolution_add_fusion.15, bf16[16384,256]{1,0:T(8,128)(2,1)S(1)} %bitcast.393, bf16[256,256]{1,0:T(8,128)(2,1)S(1)} %add.767), kind=kOutput, calls=%fused_computation.27 | convolution fusion | flops 2151677952 | bytes 42074112 | tf_op jit(solution)/shard_map/dot_general | solution.py:54
  349.9 16.5 %convolution_add_fusion.13 = f32[16384,256]{1,0:T(8,128)} fusion(f32[16384,256]{1,0:T(8,128)} %convolution_add_fusion.14, bf16[16384,256]{1,0:T(8,128)(2,1)} %bitcast.389, bf16[256,256]{1,0:T(8,128)(2,1)S(1)} %add.771), kind=kOutput, calls=%fused_computation.26 | convolution fusion | flops 2151677952 | bytes 42074112 | tf_op jit(solution)/shard_map/dot_general | solution.py:54
  366.4 16.5 %convolution_add_fusion.12 = f32[16384,256]{1,0:T(8,128)} fusion(f32[16384,256]{1,0:T(8,128)} %convolution_add_fusion.13, bf16[16384,256]{1,0:T(8,128)(2,1)} %bitcast.387, bf16[256,256]{1,0:T(8,128)(2,1)S(1)} %copy-done.17), kind=kOutput, calls=%fused_computation.25 | convolution fusion | flops 2151677952 | bytes 42074112 | tf_op jit(solution)/shard_map/dot_general | solution.py:54
  382.9 14.5 %convolution_add_fusion.11 = f32[16384,256]{1,0:T(8,128)} fusion(f32[16384,256]{1,0:T(8,128)} %convolution_add_fusion.12, bf16[16384,256]{1,0:T(8,128)(2,1)S(1)} %bitcast.383, bf16[256,256]{1,0:T(8,128)(2,1)S(1)} %copy-done.15), kind=kOutput, calls=%fused_computation.24 | convolution fusion | flops 2151677952 | bytes 42074112 | tf_op jit(solution)/shard_map/dot_general | solution.py:54
  397.4 16.5 %convolution_add_fusion.10 = f32[16384,256]{1,0:T(8,128)} fusion(f32[16384,256]{1,0:T(8,128)} %convolution_add_fusion.11, bf16[16384,256]{1,0:T(8,128)(2,1)} %bitcast.379, bf16[256,256]{1,0:T(8,128)(2,1)S(1)} %copy-done.13), kind=kOutput, calls=%fused_computation.23 | convolution fusion | flops 2151677952 | bytes 42074112 | tf_op jit(solution)/shard_map/dot_general | solution.py:54
  413.8 14.0 %convolution_add_fusion.9 = f32[16384,256]{1,0:T(8,128)} fusion(f32[16384,256]{1,0:T(8,128)} %convolution_add_fusion.10, bf16[16384,256]{1,0:T(8,128)(2,1)S(1)} %bitcast.375, bf16[256,256]{1,0:T(8,128)(2,1)S(1)} %add.787), kind=kOutput, calls=%fused_computation.22 | convolution fusion | flops 2151677952 | bytes 42074112 | tf_op jit(solution)/shard_map/dot_general | solution.py:54
  427.8 13.7 %convolution_add_fusion.8 = bf16[16384,256]{1,0:T(8,128)(2,1)} fusion(f32[16384,256]{1,0:T(8,128)} %convolution_add_fusion.9, bf16[16384,256]{1,0:T(8,128)(2,1)} %bitcast.368, bf16[256,256]{1,0:T(8,128)(2,1)S(1)} %copy-done.9), kind=kOutput, calls=%fused_computation.21 | convolution fusion | flops 2155872256 | bytes 33685504 | tf_op jit(solution)/shard_map/dot_general | solution.py:54
  454.5 106.7 %fusion.5 = bf16[64,320,256]{2,1,0:T(8,128)(2,1)} fusion(s32[64,256,8]{1,2,0:T(8,128)S(1)} %copy-done.7, bf16[64,8]{1,0:T(8,128)(2,1)S(1)} %copy-done.24), kind=kLoop, calls=%fused_computation.9 | loop fusion | flops 120586240 | bytes 11011072 | tf_op jit(solution)/shard_map/reduce_sum | solution.py:89
  583.0 13.0 %maximum_select_fusion.1 = bf16[66,258,256]{2,1,0:T(8,128)(2,1)S(1)} fusion(bf16[66,1,256]{2,1,0:T(2,128)(2,1)} %collective-permute-done.7, bf16[1,256,256]{2,1,0:T(8,128)(2,1)S(1)} %collective-permute-done.5, bf16[64,256,256]{2,1,0:T(8,128)(2,1)} %copy-done.1, bf16[1,256,256]{2,1,0:T(8,128)(2,1)S(1)} %collective-permute-done.4, ...), kind=kLoop, calls=%fused_computation.41 | loop fusion | flops 47950848 | bytes 17436738 | tf_op jit(solution)/shard_map/jit(_where)/select_n | solution.py:72
  596.0 26.9 %fusion.41 = (bf16[64,256,256]{2,1,0:T(8,128)(2,1)}, bf16[64,256,256]{2,1,0:T(8,128)(2,1)}, bf16[64,256,256]{2,1,0:T(8,128)(2,1)}, bf16[64,256,256]{2,1,0:T(8,12...) fusion(bf16[66,258,256]{2,1,0:T(8,128)(2,1)S(1)} %maximum_selec, ...), kind=kLoop, calls=%fused_computation.162 | loop fusion | bytes 150994944 | tf_op jit(solution)/shard_map/slice | solution.py:50
  634.7 16.5 %convolution_add_fusion.7 = f32[16384,256]{1,0:T(8,128)} fusion(f32[16384,256]{1,0:T(8,128)} %fusion.47, bf16[16384,256]{1,0:T(8,128)(2,1)} %bitcast.398, bf16[256,256]{1,0:T(8,128)(2,1)S(1)} %copy-done.18), kind=kOutput, calls=%fused_computation.20 | convolution fusion | flops 2151677952 | bytes 42074112 | tf_op jit(solution)/shard_map/dot_general | solution.py:54
  651.2 14.0 %convolution_add_fusion.6 = f32[16384,256]{1,0:T(8,128)} fusion(f32[16384,256]{1,0:T(8,128)} %convolution_add_fusion.7, bf16[16384,256]{1,0:T(8,128)(2,1)S(1)} %bitcast.396, bf16[256,256]{1,0:T(8,128)(2,1)S(1)} %copy-done.16), kind=kOutput, calls=%fused_computation.19 | convolution fusion | flops 2151677952 | bytes 42074112 | tf_op jit(solution)/shard_map/dot_general | solution.py:54
  665.2 16.5 %convolution_add_fusion.5 = f32[16384,256]{1,0:T(8,128)} fusion(f32[16384,256]{1,0:T(8,128)} %convolution_add_fusion.6, bf16[16384,256]{1,0:T(8,128)(2,1)} %bitcast.390, bf16[256,256]{1,0:T(8,128)(2,1)S(1)} %copy-done.14), kind=kOutput, calls=%fused_computation.18 | convolution fusion | flops 2151677952 | bytes 42074112 | tf_op jit(solution)/shard_map/dot_general | solution.py:54
  681.6 16.5 %convolution_add_fusion.4 = f32[16384,256]{1,0:T(8,128)} fusion(f32[16384,256]{1,0:T(8,128)} %convolution_add_fusion.5, bf16[16384,256]{1,0:T(8,128)(2,1)} %bitcast.388, bf16[256,256]{1,0:T(8,128)(2,1)S(1)} %copy-done.12), kind=kOutput, calls=%fused_computation.17 | convolution fusion | flops 2151677952 | bytes 42074112 | tf_op jit(solution)/shard_map/dot_general | solution.py:54
  698.1 14.3 %convolution_add_fusion.3 = f32[16384,256]{1,0:T(8,128)} fusion(f32[16384,256]{1,0:T(8,128)} %convolution_add_fusion.4, bf16[16384,256]{1,0:T(8,128)(2,1)S(1)} %bitcast.386, bf16[256,256]{1,0:T(8,128)(2,1)S(1)} %copy-done.11), kind=kOutput, calls=%fused_computation.16 | convolution fusion | flops 2151677952 | bytes 42074112 | tf_op jit(solution)/shard_map/dot_general | solution.py:54
  712.4 16.5 %convolution_add_fusion.2 = f32[16384,256]{1,0:T(8,128)} fusion(f32[16384,256]{1,0:T(8,128)} %convolution_add_fusion.3, bf16[16384,256]{1,0:T(8,128)(2,1)} %bitcast.380, bf16[256,256]{1,0:T(8,128)(2,1)S(1)} %copy-done.10), kind=kOutput, calls=%fused_computation.15 | convolution fusion | flops 2151677952 | bytes 42074112 | tf_op jit(solution)/shard_map/dot_general | solution.py:54
  728.9 14.0 %convolution_add_fusion.1 = f32[16384,256]{1,0:T(8,128)} fusion(f32[16384,256]{1,0:T(8,128)} %convolution_add_fusion.2, bf16[16384,256]{1,0:T(8,128)(2,1)S(1)} %bitcast.378, bf16[256,256]{1,0:T(8,128)(2,1)S(1)} %add.822), kind=kOutput, calls=%fused_computation.14 | convolution fusion | flops 2151677952 | bytes 42074112 | tf_op jit(solution)/shard_map/dot_general | solution.py:54
  742.9 13.8 %fusion.8 = bf16[16384,256]{1,0:T(8,128)(2,1)} fusion(f32[16384,256]{1,0:T(8,128)} %convolution_add_fusion.1, bf16[16384,256]{1,0:T(8,128)(2,1)} %bitcast.369, bf16[256,256]{1,0:T(8,128)(2,1)S(1)} %copy-done.8), kind=kOutput, calls=%fused_computation.13 | convolution fusion | flops 2155872256 | bytes 33685504 | tf_op jit(solution)/shard_map/dot_general | solution.py:54
  763.1 106.8 %fusion.4 = bf16[64,320,256]{2,1,0:T(8,128)(2,1)} fusion(s32[64,256,8]{1,2,0:T(8,128)S(1)} %copy-done.6, bf16[64,8]{1,0:T(8,128)(2,1)S(1)} %copy-done.25), kind=kLoop, calls=%fused_computation.8 | loop fusion | flops 120586240 | bytes 11011072 | tf_op jit(solution)/shard_map/reduce_sum | solution.py:89
  870.9 13.1 %fusion.40 = f32[64,256,256]{1,2,0:T(8,128)} fusion(bf16[64,320,256]{2,1,0:T(8,128)(2,1)} %fusion.7, bf16[64,32,256]{2,1,0:T(8,128)(2,1)} %collective-permute-done.9, bf16[64,256,256]{2,1,0:T(8,128)(2,1)S(1)} %bitcast.402, bf16[64,32,256]{2,1,0:T(8,128)(2,1)} %copy-done.60), kind=kOutput, calls=%fused_computation.161 | convolution fusion | flops 2715811840 | bytes 37748736 | tf_op jit(solution)/shard_map/sbw,sbx->swx/dot_general | solution.py:110
  884.0 22.1 %fusion.17 = f32[8,256,32]{1,0,2:T(8,128)S(1)} fusion(f32[64,256,8,32]{1,3,2,0:T(8,128)} %bitcast.407, f32[4,64,8,8]{1,3,2,0:T(8,128)S(1)} %copy-done.23), kind=kOutput, calls=%fused_computation.42 | convolution fusion | flops 402653184 | bytes 17072128 | tf_op jit(solution)/shard_map/shg,swhc->gwc/dot_general | solution.py:113
  906.1 13.6 %fusion.39 = f32[64,256,256]{1,2,0:T(8,128)} fusion(bf16[64,320,256]{2,1,0:T(8,128)(2,1)} %fusion.6, bf16[64,32,256]{2,1,0:T(8,128)(2,1)} %collective-permute-done.9, bf16[64,256,256]{2,1,0:T(8,128)(2,1)S(1)} %bitcast.403, bf16[64,32,256]{2,1,0:T(8,128)(2,1)} %copy-done.60), kind=kOutput, calls=%fused_computation.160 | convolution fusion | flops 2715811840 | bytes 37748736 | tf_op jit(solution)/shard_map/sbw,sbx->swx/dot_general | solution.py:110
  919.7 22.1 %fusion.20 = f32[8,256,32]{1,0,2:T(8,128)S(1)} fusion(f32[64,256,8,32]{1,3,2,0:T(8,128)} %bitcast.408, f32[4,64,8,8]{1,3,2,0:T(8,128)S(1)} %copy-done.23), kind=kOutput, calls=%fused_computation.43 | convolution fusion | flops 402653184 | bytes 17072128 | tf_op jit(solution)/shard_map/shg,swhc->gwc/dot_general | solution.py:113
  941.8 13.1 %fusion.38 = f32[64,256,256]{1,2,0:T(8,128)} fusion(bf16[64,320,256]{2,1,0:T(8,128)(2,1)} %fusion.5, bf16[64,32,256]{2,1,0:T(8,128)(2,1)} %collective-permute-done.9, bf16[64,256,256]{2,1,0:T(8,128)(2,1)S(1)} %bitcast.404, bf16[64,32,256]{2,1,0:T(8,128)(2,1)} %copy-done.60), kind=kOutput, calls=%fused_computation.159 | convolution fusion | flops 2715811840 | bytes 37748736 | tf_op jit(solution)/shard_map/sbw,sbx->swx/dot_general | solution.py:110
  955.0 22.3 %fusion.23 = f32[8,256,32]{1,0,2:T(8,128)S(1)} fusion(f32[64,256,8,32]{1,3,2,0:T(8,128)} %bitcast.409, f32[4,64,8,8]{1,3,2,0:T(8,128)S(1)} %copy-done.23), kind=kOutput, calls=%fused_computation.44 | convolution fusion | flops 402653184 | bytes 17072128 | tf_op jit(solution)/shard_map/shg,swhc->gwc/dot_general | solution.py:113
  977.3 13.1 %fusion.37 = f32[64,256,256]{1,2,0:T(8,128)} fusion(bf16[64,320,256]{2,1,0:T(8,128)(2,1)} %fusion.4, bf16[64,32,256]{2,1,0:T(8,128)(2,1)} %collective-permute-done.9, bf16[64,256,256]{2,1,0:T(8,128)(2,1)S(1)} %bitcast.405, bf16[64,32,256]{2,1,0:T(8,128)(2,1)} %copy-done.60), kind=kOutput, calls=%fused_computation.158 | convolution fusion | flops 2715811840 | bytes 37748736 | tf_op jit(solution)/shard_map/sbw,sbx->swx/dot_general | solution.py:110
  990.4 22.3 %fusion.26 = f32[8,256,32]{1,0,2:T(8,128)S(1)} fusion(f32[64,256,8,32]{1,3,2,0:T(8,128)} %bitcast.406, f32[4,64,8,8]{1,3,2,0:T(8,128)S(1)} %copy-done.23), kind=kOutput, calls=%fused_computation.45 | convolution fusion | flops 402653184 | bytes 17072128 | tf_op jit(solution)/shard_map/shg,swhc->gwc/dot_general | solution.py:113
  1014.2 18.3 %reduce-scatter.2.cloned.1.call-done = f32[4,256,128]{2,1,0:T(8,128)} async-done(((f32[8,256,128]{2,1,0:T(8,128)}), f32[4,256,128]{2,1,0:T(8,128)}) %reduce-scatter.2.cloned.1.call-update) | async-done | bytes 524304 | tf_op jit(solution)/shard_map/reduce_scatter | solution.py:156
  (287 shorter events, 127.6 us)
Async XLA Ops:
  6.5 1026.0 %reduce-scatter.2.cloned.1.call-start = ((), (), s32[]{:S(2)}) async-start(), calls=%async_computation.1 | async-start | bytes 1572864 | tf_op jit(solution)/shard_map/reduce_scatter | solution.py:156
  17.1 233.7 %collective-permute-start = (bf16[1,256,256]{2,1,0:T(8,128)(2,1)}, bf16[1,256,256]{2,1,0:T(8,128)(2,1)S(1)}, u32[]{:S(2)}, u32[]{:S(2)}) collective-permute-start(bf16[1,256,256]{2,1,0:T(8,128)(2,1)} %get-tuple-element.31), channel_id=1, source_target_pairs={{0,16},{16,0},{1,17},{17,1},{2,18},{18,2},{3,19},{19,3},{4,20},{20... | collective-permute-start | bytes 393224 | tf_op jit(solution)/shard_map/ppermute | solution.py:16
  20.1 230.7 %collective-permute-start.1 = (bf16[1,256,256]{2,1,0:T(8,128)(2,1)S(1)}, bf16[1,256,256]{2,1,0:T(8,128)(2,1)S(1)}, u32[]{:S(2)}, u32[]{:S(2)}) collective-permute-start(bf16[1,256,256]{2,1,0:T(8,128)(2,1)S(1)} %get-tuple-element.32), channel_id=1, source_target_pairs={{16,0},{0,16},{17,1},{1,17},{18,2},{2,18},{19,3},{3,19},{20,4},{4,... | collective-permute-start | bytes 393224 | tf_op jit(solution)/shard_map/ppermute | solution.py:19
  22.9 223.9 %copy-start.48 = (pred[8,8]{1,0:T(8,128)(4,1)}, pred[8,8]{1,0:T(8,128)(4,1)S(1)}, u32[]{:S(2)}) copy-start(pred[8,8]{1,0:T(8,128)(4,1)S(1)} %get-tuple-element.121) | copy-start | bytes 196
  22.9 223.9 %copy-start.50 = (pred[8,8]{1,0:T(8,128)(4,1)}, pred[8,8]{1,0:T(8,128)(4,1)S(1)}, u32[]{:S(2)}) copy-start(pred[8,8]{1,0:T(8,128)(4,1)S(1)} %get-tuple-element.122) | copy-start | bytes 196
  22.9 223.9 %copy-start.53 = (pred[8,8]{1,0:T(8,128)(4,1)}, pred[8,8]{1,0:T(8,128)(4,1)S(1)}, u32[]{:S(2)}) copy-start(pred[8,8]{1,0:T(8,128)(4,1)S(1)} %iota_compare_fusion.7) | copy-start | bytes 196
  138.0 110.7 %copy-start.26 = (bf16[32,32]{1,0:T(8,128)(2,1)S(1)}, bf16[32,32]{1,0:T(8,128)(2,1)}, u32[]{:S(2)}) copy-start(bf16[32,32]{1,0:T(8,128)(2,1)} %copy.178) | copy-start | bytes 6148
  138.0 110.7 %copy-start.27 = (bf16[32,32]{1,0:T(8,128)(2,1)S(1)}, bf16[32,32]{1,0:T(8,128)(2,1)}, u32[]{:S(2)}) copy-start(bf16[32,32]{1,0:T(8,128)(2,1)} %copy.179) | copy-start | bytes 6148
  138.0 110.7 %copy-start.28 = (bf16[32,32]{1,0:T(8,128)(2,1)S(1)}, bf16[32,32]{1,0:T(8,128)(2,1)}, u32[]{:S(2)}) copy-start(bf16[32,32]{1,0:T(8,128)(2,1)} %copy.180) | copy-start | bytes 6148
  138.0 110.7 %copy-start.29 = (bf16[32,32]{1,0:T(8,128)(2,1)S(1)}, bf16[32,32]{1,0:T(8,128)(2,1)}, u32[]{:S(2)}) copy-start(bf16[32,32]{1,0:T(8,128)(2,1)} %copy.181) | copy-start | bytes 6148
  138.0 110.7 %copy-start.30 = (bf16[32,32]{1,0:T(8,128)(2,1)S(1)}, bf16[32,32]{1,0:T(8,128)(2,1)}, u32[]{:S(2)}) copy-start(bf16[32,32]{1,0:T(8,128)(2,1)} %copy.137) | copy-start | bytes 6148
  138.1 110.7 %copy-start.31 = (bf16[32,32]{1,0:T(8,128)(2,1)S(1)}, bf16[32,32]{1,0:T(8,128)(2,1)}, u32[]{:S(2)}) copy-start(bf16[32,32]{1,0:T(8,128)(2,1)} %copy.138) | copy-start | bytes 6148
  138.1 110.7 %copy-start.32 = (bf16[32,32]{1,0:T(8,128)(2,1)S(1)}, bf16[32,32]{1,0:T(8,128)(2,1)}, u32[]{:S(2)}) copy-start(bf16[32,32]{1,0:T(8,128)(2,1)} %copy.139) | copy-start | bytes 6148
  252.6 15.6 %collective-permute-start.2 = (bf16[66,1,256]{2,1,0:T(2,128)(2,1)}, bf16[66,1,256]{2,1,0:T(2,128)(2,1)}, u32[]{:S(2)}, u32[]{:S(2)}) collective-permute-start(bf16[66,1,256]{2,1,0:T(2,128)(2,1)} %get-tuple-element.25), channel_id=1, source_target_pairs={{0,1},{1,2},{2,3},{3,4},{4,5},{5,6},{6,7},{7,8},{8,9},{9,10},{10,1... | collective-permute-start | bytes 101384 | tf_op jit(solution)/shard_map/ppermute | solution.py:16
  252.6 15.6 %collective-permute-start.3 = (bf16[66,1,256]{2,1,0:T(2,128)(2,1)}, bf16[66,1,256]{2,1,0:T(2,128)(2,1)}, u32[]{:S(2)}, u32[]{:S(2)}) collective-permute-start(bf16[66,1,256]{2,1,0:T(2,128)(2,1)} %get-tuple-element.26), channel_id=1, source_target_pairs={{1,0},{2,1},{3,2},{4,3},{5,4},{6,5},{7,6},{8,7},{9,8},{10,9},{11,1... | collective-permute-start | bytes 101384 | tf_op jit(solution)/shard_map/ppermute | solution.py:19
  452.2 109.9 %copy-start.38 = (bf16[32,32]{0,1:T(8,128)(2,1)S(1)}, bf16[32,32]{0,1:T(8,128)(2,1)}, u32[]{:S(2)}) copy-start(bf16[32,32]{0,1:T(8,128)(2,1)} %get-tuple-element.57) | copy-start | bytes 6148
  452.2 110.0 %copy-start.36 = (bf16[32,32]{0,1:T(8,128)(2,1)S(1)}, bf16[32,32]{0,1:T(8,128)(2,1)}, u32[]{:S(2)}) copy-start(bf16[32,32]{0,1:T(8,128)(2,1)} %get-tuple-element.56) | copy-start | bytes 6148
  452.2 110.1 %copy-start.35 = (bf16[32,32]{0,1:T(8,128)(2,1)S(1)}, bf16[32,32]{0,1:T(8,128)(2,1)}, u32[]{:S(2)}) copy-start(bf16[32,32]{0,1:T(8,128)(2,1)} %get-tuple-element.55) | copy-start | bytes 6148
  452.2 110.2 %copy-start.34 = (bf16[32,32]{0,1:T(8,128)(2,1)S(1)}, bf16[32,32]{0,1:T(8,128)(2,1)}, u32[]{:S(2)}) copy-start(bf16[32,32]{0,1:T(8,128)(2,1)} %get-tuple-element.54) | copy-start | bytes 6148
  452.2 110.2 %copy-start.33 = (bf16[32,32]{0,1:T(8,128)(2,1)S(1)}, bf16[32,32]{0,1:T(8,128)(2,1)}, u32[]{:S(2)}) copy-start(bf16[32,32]{0,1:T(8,128)(2,1)} %get-tuple-element.53) | copy-start | bytes 6148
  452.2 116.6 %copy-start.49 = (pred[8,8]{1,0:T(8,128)(4,1)S(1)}, pred[8,8]{1,0:T(8,128)(4,1)}, u32[]{:S(2)}) copy-start(pred[8,8]{1,0:T(8,128)(4,1)} %copy-done.48) | copy-start | bytes 196
  452.2 116.6 %copy-start.51 = (pred[8,8]{1,0:T(8,128)(4,1)S(1)}, pred[8,8]{1,0:T(8,128)(4,1)}, u32[]{:S(2)}) copy-start(pred[8,8]{1,0:T(8,128)(4,1)} %copy-done.50) | copy-start | bytes 196
  452.2 116.6 %copy-start.54 = (pred[8,8]{1,0:T(8,128)(4,1)S(1)}, pred[8,8]{1,0:T(8,128)(4,1)}, u32[]{:S(2)}) copy-start(pred[8,8]{1,0:T(8,128)(4,1)} %copy-done.53) | copy-start | bytes 196
  452.3 110.3 %collective-permute-start.4 = (bf16[1,256,256]{2,1,0:T(8,128)(2,1)S(1)}, bf16[1,256,256]{2,1,0:T(8,128)(2,1)S(1)}, u32[]{:S(2)}, u32[]{:S(2)}) collective-permute-start(bf16[1,256,256]{2,1,0:T(8,128)(2,1)S(1)} %get-tuple-element.29), channel_id=1, source_target_pairs={{0,16},{16,0},{1,17},{17,1},{2,18},{18,2},{3,19},{19,3},{4,20},{20... | collective-permute-start | bytes 393224 | tf_op jit(solution)/shard_map/ppermute | solution.py:16
  454.4 108.2 %collective-permute-start.5 = (bf16[1,256,256]{2,1,0:T(8,128)(2,1)S(1)}, bf16[1,256,256]{2,1,0:T(8,128)(2,1)S(1)}, u32[]{:S(2)}, u32[]{:S(2)}) collective-permute-start(bf16[1,256,256]{2,1,0:T(8,128)(2,1)S(1)} %get-tuple-element.30), channel_id=1, source_target_pairs={{16,0},{0,16},{17,1},{1,17},{18,2},{2,18},{19,3},{3,19},{20,4},{4,... | collective-permute-start | bytes 393224 | tf_op jit(solution)/shard_map/ppermute | solution.py:19
  454.5 123.4 %copy-start.3 = (bf16[8,32,8,32]{3,2,1,0:T(8,128)(2,1)S(1)}, bf16[8,32,8,32]{3,2,1,0:T(8,128)(2,1)}, u32[]{:S(2)}) copy-start(bf16[8,32,8,32]{3,2,1,0:T(8,128)(2,1)} %get-tuple-element.107) | copy-start | bytes 393220
  454.5 124.4 %copy-start.2 = (bf16[8,32,8,32]{3,2,1,0:T(8,128)(2,1)S(1)}, bf16[8,32,8,32]{3,2,1,0:T(8,128)(2,1)}, u32[]{:S(2)}) copy-start(bf16[8,32,8,32]{3,2,1,0:T(8,128)(2,1)} %get-tuple-element.106) | copy-start | bytes 393220
  564.4 18.6 %collective-permute-start.6 = (bf16[66,1,256]{2,1,0:T(2,128)(2,1)}, bf16[66,1,256]{2,1,0:T(2,128)(2,1)}, u32[]{:S(2)}, u32[]{:S(2)}) collective-permute-start(bf16[66,1,256]{2,1,0:T(2,128)(2,1)} %get-tuple-element.23), channel_id=1, source_target_pairs={{0,1},{1,2},{2,3},{3,4},{4,5},{5,6},{6,7},{7,8},{8,9},{9,10},{10,1... | collective-permute-start | bytes 101384 | tf_op jit(solution)/shard_map/ppermute | solution.py:16
  564.4 18.6 %collective-permute-start.7 = (bf16[66,1,256]{2,1,0:T(2,128)(2,1)}, bf16[66,1,256]{2,1,0:T(2,128)(2,1)}, u32[]{:S(2)}, u32[]{:S(2)}) collective-permute-start(bf16[66,1,256]{2,1,0:T(2,128)(2,1)} %get-tuple-element.24), channel_id=1, source_target_pairs={{1,0},{2,1},{3,2},{4,3},{5,4},{6,5},{7,6},{8,7},{9,8},{10,9},{11,1... | collective-permute-start | bytes 101384 | tf_op jit(solution)/shard_map/ppermute | solution.py:19
  756.7 114.2 %slice-start.12 = ((s8[8388608]{0:T(1024)(128)(4,1)}), s8[4194304]{0:T(1024)(128)(4,1)S(1)}, s32[]{:S(2)}) async-start(s8[8388608]{0:T(1024)(128)(4,1)} %bitcast.400), calls=%async_computation.14 | async-start | bytes 8388608
  758.6 111.3 %collective-permute-start.8 = (bf16[64,32,256]{2,1,0:T(8,128)(2,1)S(1)}, bf16[64,32,256]{2,1,0:T(8,128)(2,1)S(1)}, u32[]{:S(2)}, u32[]{:S(2)}) collective-permute-start(bf16[64,32,256]{2,1,0:T(8,128)(2,1)S(1)} %get-tuple-element.27), channel_id=1, source_target_pairs={{0,1},{1,2},{2,3},{3,4},{4,5},{5,6},{6,7},{7,8},{8,9},{9,10},{10,1... | collective-permute-start | bytes 3145736 | tf_op jit(solution)/shard_map/ppermute | solution.py:16
  758.6 112.2 %collective-permute-start.9 = (bf16[64,32,256]{2,1,0:T(8,128)(2,1)S(1)}, bf16[64,32,256]{2,1,0:T(8,128)(2,1)}, u32[]{:S(2)}, u32[]{:S(2)}) collective-permute-start(bf16[64,32,256]{2,1,0:T(8,128)(2,1)S(1)} %get-tuple-element.28), channel_id=1, source_target_pairs={{1,0},{2,1},{3,2},{4,3},{5,4},{6,5},{7,6},{8,7},{9,8},{10,9},{11,1... | collective-permute-start | bytes 3145736 | tf_op jit(solution)/shard_map/ppermute | solution.py:19
  (54 other events, 1978.7 us)
Sparse Core Ops, SparseCore 0:
  1014.4 18.1 reduce-scatter.1
where the time goes:
time: 1050 us; the launch traced here: 1040 us
  other arithmetic  479 us (46%)
  matrix products  409 us (39%)
  local copies, waits for them, and re-layouts  100 us (10%)
  starting transfers between devices  18.6 us (2%)
  waiting for transfers between devices  18.3 us (2%)
  between operations  14.3 us (1%)
    reduce_sum x4, other arithmetic, band_matrix(): return jnp.sum(chosen, axis=3, dtype=jnp.bfloat16)  427 us
    dot_general x18, matrix products, transpose_conv(): jnp.dot(slab.reshape(-1, merged), mixers[depth_tap][column_tap], preferre...  267 us
    dot_general x4, matrix products, camera_terms(): jnp.einsum('shg,swhc->gwc', row_resample[camera], pulled, precision=lax.P...  88.8 us
    slice x2, local copies, waits for them, and re-layouts, transpose_conv(): padded[2 - depth_tap:2 - depth_tap + out_spheres, 2 - column_tap:2 - colu...  53.6 us
    dot_general x4, matrix products, camera_terms(): jnp.einsum('sbw,sbx->swx', matrix, source, preferred_element_type=jnp.flo...  53 us
    select_n x2, other arithmetic, clear_rims(): jnp.where(outside.reshape(layout), jnp.zeros_like(extended), extended)  25.9 us
    add x18, local copies, waits for them, and re-layouts, row_mixers(): mixed + jnp.where(row_in == row_out + 1 - row_tap, block, jnp.zeros((), j...  21.4 us
  transfers between devices with their start and end apart: 11, of which 1 were waited for; matrix products, arithmetic and copies ran while one was open for 45% of the time, Pallas kernels for 0%

commit v1 on v0

v1 whole, which is shorter than its diff:
```python
import functools

import jax
import jax.numpy as jnp
from jax import lax
from jax.experimental import pallas as pl
from jax.experimental.pallas import tpu as pltpu
from jax.sharding import PartitionSpec as P

TAPS = 8
SHIFT = 24
MARGIN = SHIFT + TAPS
GROUP = 4
VBLOCK = 64
BF16 = jnp.bfloat16
F32 = jnp.float32


def sweep_kernel(
    sphere_rim,
    column_rim,
    cot_a,
    cot_b,
    cot_zero,
    second_a,
    second_b,
    second_zero,
    first_a,
    first_b,
    first_c,
    first_d,
    first_zero,
    mixer_second,
    mixer_first,
    resample,
    bands,
    out_ref,
    taps_one,
    taps_two,
    padded_one,
    padded_two,
    volume,
    mixed,
    total,
):
    step = pl.program_id(0)
    steps = pl.num_programs(0)
    last = step == steps - 1
    columns, merged = cot_a.shape[1:]
    cameras, row_count = resample.shape[1:3]
    channels = merged // row_count
    wide = columns + 16
    blocks = columns // VBLOCK
    window = VBLOCK + 2 * MARGIN

    def store_taps(source, target, slot, rows):
        for tap in range(3):
            target[slot, :, tap * merged : (tap + 1) * merged] = source[
                9 - tap : 9 - tap + rows
            ].astype(BF16)

    def gate_second(grad, index, sphere, slot):
        padded = padded_one.at[index]
        padded[16 : 16 + columns] = grad.astype(F32)
        padded[8:16] = column_rim[sphere, 0:8].astype(F32)
        padded[16 + columns : 24 + columns] = column_rim[sphere, 8:16].astype(F32)
        store_taps(padded, taps_one, slot, wide)

    def masked(cot, saved):
        return jnp.where(saved > 0, cot, jnp.zeros_like(cot))

    def conv(source, mixers, slots):
        lhs = lambda depth: jnp.concatenate(
            [source[slot + 2 - depth] for slot in slots], axis=0
        )
        value = jnp.dot(lhs(2), mixers[2], preferred_element_type=F32)
        value = value + jnp.dot(lhs(1), mixers[1], preferred_element_type=F32)
        return value + jnp.dot(lhs(0), mixers[0], preferred_element_type=F32)

    def gate_first(hidden, saved, index, sphere, slot):
        low = column_rim[sphere, 16:24].astype(F32)
        high = column_rim[sphere, 24:32].astype(F32)
        keep = jnp.concatenate([low, saved.astype(F32), high], axis=0) > 0
        padded_two[index] = jnp.where(keep, hidden, 0.0)
        store_taps(padded_two.at[index], taps_two, slot, columns)

    lane = lax.broadcasted_iota(jnp.int32, (channels, merged), 1)
    diagonal = lax.rem(lane, channels) == lax.broadcasted_iota(
        jnp.int32, (channels, merged), 0
    )

    def mix_rows(group):
        for camera in range(cameras):
            for sphere in range(GROUP):
                rows = resample[group * GROUP + sphere, camera]
                weights = jnp.concatenate(
                    [jnp.where(diagonal, rows[r : r + 1], 0.0) for r in range(row_count)],
                    axis=0,
                ).astype(BF16)
                value = jnp.dot(
                    volume[sphere], weights, preferred_element_type=F32
                ).astype(BF16)
                for block in range(blocks):
                    mixed[camera, block, sphere * VBLOCK : (sphere + 1) * VBLOCK] = value[
                        block * VBLOCK : (block + 1) * VBLOCK
                    ]

    width = GROUP * VBLOCK
    distance = (
        lax.rem(lax.broadcasted_iota(jnp.int32, (window, width), 1), VBLOCK)
        - lax.broadcasted_iota(jnp.int32, (window, width), 0)
        + MARGIN
    ).astype(F32)

    def warp_columns(group):
        for camera in range(cameras):
            rows = bands[camera, group]
            tap_of = distance - rows[TAPS : TAPS + 1]
            matrix = jnp.zeros((window, width), F32)
            for tap in range(TAPS):
                matrix = jnp.where(tap_of == float(tap), rows[tap : tap + 1], matrix)
            matrix = matrix.astype(BF16)
            for block in range(blocks):
                place = slice(block * VBLOCK, block * VBLOCK + window)
                total[camera, place] = total[camera, place] + jnp.dot(
                    matrix, mixed[camera, block], preferred_element_type=F32
                )

    @pl.when(step == 0)
    def _():
        total[...] = jnp.zeros_like(total)
        volume[...] = jnp.zeros_like(volume)
        gate_second(sphere_rim[0], 0, 0, 2)
        gate_second(sphere_rim[1], 1, 1, 3)
        gate_second(masked(cot_zero[0], second_zero[0]), 2, 2, 0)
        gate_second(masked(cot_zero[1], second_zero[1]), 3, 3, 1)
        order = (2, 3, 0, 1)
        for index in range(2):
            hidden = jnp.zeros((wide, merged), F32)
            for depth in range(3):
                hidden = hidden + jnp.dot(
                    taps_one[order[index + 2 - depth]],
                    mixer_second[depth],
                    preferred_element_type=F32,
                )
            saved = sphere_rim[2] if index == 0 else first_zero[0]
            gate_first(hidden, saved, index, index + 1, index)

    base = step * GROUP
    before = jnp.maximum(step - 1, 0)

    gate_second(masked(cot_a[0], second_a[0]), 0, base + 4, 2)
    gate_second(masked(cot_a[1], second_a[1]), 1, base + 5, 3)
    hidden = conv(taps_one, mixer_second, (0, 1))
    gate_first(hidden[:wide], first_a[0], 0, base + 3, 2)
    gate_first(hidden[wide:], first_b[0], 1, base + 4, 3)
    for index in range(2):
        grad = masked(cot_b[index], second_b[index])
        grad = jnp.where(last, sphere_rim[3 + index], grad)
        gate_second(grad, 2 + index, base + 6 + index, 4 + index)
    mix_rows(before)
    hidden = conv(taps_one, mixer_second, (2, 3))
    gate_first(hidden[:wide], first_c[0], 2, base + 5, 4)
    gate_first(
        hidden[wide:], jnp.where(last, sphere_rim[5], first_d[0]), 3, base + 6, 5
    )
    for pair in range(2):
        value = conv(taps_two, mixer_first, (2 * pair, 2 * pair + 1)).astype(BF16)
        volume[2 * pair] = value[:columns]
        volume[2 * pair + 1] = value[columns:]
        if pair == 0:
            warp_columns(before)
    for slot in range(2):
        taps_one[slot] = taps_one[slot + 4]
        taps_two[slot] = taps_two[slot + 4]

    @pl.when(last)
    def _():
        mix_rows(step)
        warp_columns(step)
        for row in range(row_count):
            out_ref[row] = jnp.concatenate(
                [
                    total[camera, :, row * channels : (row + 1) * channels]
                    for camera in range(cameras)
                ],
                axis=1,
            )


def sweep(sphere_rim, column_rim, cot, second, first, mixer_second, mixer_first, resample, bands):
    spheres, columns, merged = cot.shape
    cameras, row_count = resample.shape[1:3]
    channels = merged // row_count
    wide = columns + 16
    blocks = columns // VBLOCK
    window = VBLOCK + 2 * MARGIN
    pairs = spheres // 2

    def whole(array):
        zeros = (0,) * array.ndim
        return pl.BlockSpec(
            array.shape, lambda g: zeros, pipeline_mode=pl.Buffered(buffer_count=1)
        )

    pair_a = pl.BlockSpec((2, columns, merged), lambda g: (2 * g + 1, 0, 0))
    pair_b = pl.BlockSpec(
        (2, columns, merged), lambda g: (jnp.minimum(2 * g + 2, pairs - 1), 0, 0)
    )
    pair_zero = pl.BlockSpec(
        (2, columns, merged), lambda g: (0, 0, 0), pipeline_mode=pl.Buffered(buffer_count=1)
    )
    single = lambda ahead: pl.BlockSpec(
        (1, columns, merged),
        lambda g: (jnp.minimum(GROUP * g + ahead, spheres - 1), 0, 0),
    )
    single_zero = pl.BlockSpec(
        (1, columns, merged), lambda g: (0, 0, 0), pipeline_mode=pl.Buffered(buffer_count=1)
    )
    extended = columns + 2 * MARGIN
    out_shape = (row_count, extended, cameras * channels)
    flops = 2 * spheres * columns * merged * merged * (18 + cameras + cameras // 2)
    return pl.pallas_call(
        sweep_kernel,
        grid=(spheres // GROUP,),
        in_specs=[
            whole(sphere_rim),
            whole(column_rim),
            pair_a,
            pair_b,
            pair_zero,
            pair_a,
            pair_b,
            pair_zero,
            single(1),
            single(2),
            single(3),
            single(4),
            single_zero,
            whole(mixer_second),
            whole(mixer_first),
            whole(resample),
            whole(bands),
        ],
        out_specs=pl.BlockSpec(
            out_shape, lambda g: (0, 0, 0), pipeline_mode=pl.Buffered(buffer_count=1)
        ),
        out_shape=jax.ShapeDtypeStruct(out_shape, F32),
        scratch_shapes=[
            pltpu.VMEM((6, wide, 3 * merged), BF16),
            pltpu.VMEM((6, columns, 3 * merged), BF16),
            pltpu.VMEM((4, columns + 32, merged), F32),
            pltpu.VMEM((4, wide, merged), F32),
            pltpu.VMEM((GROUP, columns, merged), BF16),
            pltpu.VMEM((cameras, blocks, GROUP * VBLOCK, merged), BF16),
            pltpu.VMEM((cameras, extended, merged), F32),
        ],
        compiler_params=pltpu.CompilerParams(
            dimension_semantics=("arbitrary",), vmem_limit_bytes=56 * 2**20
        ),
        cost_estimate=pl.CostEstimate(
            flops=flops, bytes_accessed=3 * cot.size * 2, transcendentals=0
        ),
        name="sweep",
    )(
        sphere_rim,
        column_rim,
        cot,
        cot,
        cot,
        second,
        second,
        second,
        first,
        first,
        first,
        first,
        first,
        mixer_second,
        mixer_first,
        resample,
        bands,
    )


def row_mixers(kernel, row_count):
    channels = kernel.shape[3]
    strip = jnp.transpose(kernel, (0, 1, 4, 2, 3)).reshape(9, channels, 3 * channels)
    merged = row_count * channels
    strip = jnp.pad(strip, ((0, 0), (0, 0), (merged, merged)))
    rows = [
        lax.slice_in_dim(
            strip, merged - (row - 1) * channels, 2 * merged - (row - 1) * channels, axis=2
        )
        for row in range(row_count)
    ]
    return jnp.stack(rows, axis=1).reshape(3, 3 * merged, merged)


def steps_along(axis, offset):
    count = lax.axis_size(axis)
    return [(i, i + offset) for i in range(count) if 0 <= i + offset < count]


def ring_along(axis, offset):
    count = lax.axis_size(axis)
    return [(i, (i + offset) % count) for i in range(count)]


def joint(depth_pairs, azim_pairs):
    width = lax.axis_size("azim")
    return [
        (d0 * width + a0, d1 * width + a1)
        for d0, d1 in depth_pairs
        for a0, a1 in azim_pairs
    ]


def body(cot, second, first, kernel_first, kernel_second, row_resample, col_taps, band_width, col_offset):
    spheres, columns, merged = cot.shape
    cameras, _, row_count, _ = row_resample.shape
    channels = merged // row_count
    gate = lambda where: jnp.where(second[where] > 0, cot[where], jnp.zeros((), BF16))
    everything = slice(None)

    def edge(sphere_slice, column_slice, sphere_first, column_first, axis):
        return jnp.concatenate(
            [gate((sphere_slice, column_slice)), first[sphere_first, column_first]], axis=axis
        )

    left = edge(everything, slice(0, 2), everything, slice(0, 1), 1)
    right = edge(everything, slice(columns - 2, None), everything, slice(columns - 1, None), 1)
    low = edge(slice(0, 2), everything, slice(0, 1), everything, 0)
    high = edge(slice(spheres - 2, None), everything, slice(spheres - 1, None), everything, 0)
    forward, backward = ring_along("azim", 1), ring_along("azim", -1)
    up, down = steps_along("depth", 1), steps_along("depth", -1)
    both = ("depth", "azim")
    from_left = lax.ppermute(right, "azim", forward)
    from_right = lax.ppermute(left, "azim", backward)
    from_low = lax.ppermute(high, "depth", up)
    from_high = lax.ppermute(low, "depth", down)

    def corner(side):
        return jnp.concatenate([side[:2], side[spheres - 2 :]], axis=0)

    corners = {}
    for name, source, azim_pairs in (("left", right, forward), ("right", left, backward)):
        below = lax.ppermute(source[spheres - 2 :], both, joint(up, azim_pairs))
        above = lax.ppermute(source[:2], both, joint(down, azim_pairs))
        corners[name] = (below, above)
    side_left = jnp.concatenate([corners["left"][0], from_left, corners["left"][1]], axis=0)
    side_right = jnp.concatenate([corners["right"][0], from_right, corners["right"][1]], axis=0)
    blank = lambda rows: jnp.zeros((spheres + 4, rows, merged), BF16)
    column_rim = jnp.concatenate(
        [
            blank(6),
            side_left[:, :2],
            side_right[:, :2],
            blank(6),
            blank(7),
            side_left[:, 2:],
            side_right[:, 2:],
            blank(7),
        ],
        axis=1,
    )
    sphere_rim = jnp.concatenate([from_low, from_high], axis=0)

    mixer_second = row_mixers(kernel_second, row_count)
    mixer_first = row_mixers(kernel_first, row_count)
    resample = jnp.repeat(jnp.transpose(row_resample, (1, 0, 2, 3)), channels, axis=3)
    keep = lax.broadcasted_iota(jnp.int32, col_taps.shape, 2) < band_width[:, :, None]
    taps = jnp.where(keep, col_taps, 0.0).astype(BF16).astype(F32)
    table = jnp.concatenate([taps, col_offset[:, :, None].astype(F32)], axis=2)
    table = jnp.transpose(
        table.reshape(cameras, spheres // GROUP, GROUP, TAPS + 1), (0, 1, 3, 2)
    )
    table = jnp.repeat(table, VBLOCK, axis=3)
    bands = jnp.pad(table, ((0, 0), (0, 0), (0, 7), (0, 0)))

    partial = sweep(
        sphere_rim, column_rim, cot, second, first, mixer_second, mixer_first, resample, bands
    )

    spill_left = lax.ppermute(partial[:, :MARGIN], "azim", backward)
    spill_right = lax.ppermute(partial[:, columns + MARGIN :], "azim", forward)
    inner = partial[:, MARGIN : columns + MARGIN]
    inner = inner.at[:, columns - MARGIN :].add(spill_left)
    inner = inner.at[:, :MARGIN].add(spill_right)
    return lax.psum_scatter(inner, "depth", scatter_dimension=0, tiled=True)


def solution(mesh):
    placed = (
        P("depth", "azim", None),
        P("depth", "azim", None),
        P("depth", "azim", None),
        P(),
        P(),
        P(None, "depth", None, None),
        P(None, "depth", None),
        P(None, "depth"),
        P(None, "depth"),
    )
    return jax.shard_map(
        body, mesh=mesh, in_specs=placed, out_specs=P("depth", "azim", None), check_vma=False
    )
```

time: 1050 us -> 162 us (0.15); the launches traced: 1040 us -> 162 us
  other arithmetic: 479 us -> 4.27 us
  matrix products: 409 us -> 0 us
  local copies, waits for them, and re-layouts: 100 us -> 23.9 us
  Pallas kernels: 0 us -> 69.1 us
    reduce_sum x4 -> x0, other arithmetic: 427 us -> none  [band_matrix(): return jnp.sum(chosen, axis=3, dtype=jnp.bfloat16)]
    dot_general x26 -> x0, matrix products: 409 us -> none  [the longest x18 267 us: transpose_conv(): jnp.dot(slab.reshape(-1, merged), mixers[depth_tap][column_tap], preferre...]
    pallas_call x0 -> x1, Pallas kernels: none -> 69.1 us  [sweep(): pl.pallas_call(sweep_kernel, grid=(spheres // GROUP,), in_specs=[whole(sp...]
    slice x5 -> x9, local copies, waits for them, and re-layouts: 56.1 us -> 3.52 us  [the longest x2 2.17 us: edge(): first[sphere_first, column_first]]
    select_n x3 -> x2, other arithmetic: 32.4 us -> 2.68 us  [body(): jnp.where(second[where] > 0, cot[where], jnp.zeros((), BF16))]
    add x19 -> x0, local copies, waits for them, and re-layouts: 21.4 us -> none  [the longest x18 21.4 us: row_mixers(): mixed + jnp.where(row_in == row_out + 1 - row_tap, block, jnp.zeros((), j...]
    ppermute x10, waiting for transfers between devices: 0.04 us -> 11.2 us  [the longest x1 4.6 us: body(): spill_right = lax.ppermute(partial[:, columns + MARGIN:], 'azim', forward)]
  transfers between devices with their start and end apart: 11 -> 11, of which waited for: 1 -> 5; matrix products, arithmetic and copies ran while one was open for 45% -> 13% of each run, Pallas kernels for 0% -> 0%
where the time goes in v1:
time: 162 us
  Pallas kernels  69.1 us (43%)
  waiting for transfers between devices  27.7 us (17%)
  local copies, waits for them, and re-layouts  23.9 us (15%)
  starting transfers between devices  23.3 us (14%)
  between operations  13.9 us (9%)
  other arithmetic  4.27 us (3%)
    pallas_call x1, Pallas kernels, sweep(): pl.pallas_call(sweep_kernel, grid=(spheres // GROUP,), in_specs=[whole(sp...  69.1 us
    reduce_scatter x1, waiting for transfers between devices, body(): return lax.psum_scatter(inner, 'depth', scatter_dimension=0, tiled=True)  16.4 us
    ppermute x2, starting transfers between devices, body(): below = lax.ppermute(source[spheres - 2:], both, joint(up, azim_pairs))  12.3 us
    concatenate x1, local copies, waits for them, and re-layouts, body(): jnp.concatenate([blank(6), side_left[:, :2], side_right[:, :2], blank(6),...  6.07 us
    ppermute x1, starting transfers between devices, body(): from_low = lax.ppermute(high, 'depth', up)  4.63 us
    ppermute x1, waiting for transfers between devices, body(): spill_right = lax.ppermute(partial[:, columns + MARGIN:], 'azim', forward)  4.6 us
    reshape x1, local copies, waits for them, and re-layouts, body(): jnp.repeat(jnp.transpose(row_resample, (1, 0, 2, 3)), channels, axis=3)  4.24 us
    ppermute x1, waiting for transfers between devices, body(): from_high = lax.ppermute(low, 'depth', down)  4.16 us
  transfers between devices with their start and end apart: 11, of which 5 were waited for; matrix products, arithmetic and copies ran while one was open for 13% of the time, Pallas kernels for 0%

profile of v1, /device:TPU:0, one launch (start us, length us, event | category | flops | bytes accessed | tf_op | source)
XLA Modules:
  0.0 162.1 jit_solution(38282967748227276)
XLA Ops:
  6.5 1.1 fusion.39
  7.7 1.4 compare_select_fusion.2
  9.1 4.3 %collective-permute-start.2 = (bf16[2,3,256]{2,1,0:T(4,128)(2,1)S(1)}, bf16[2,3,256]{2,1,0:T(4,128)(2,1)S(1)}, u32[]{:S(2)}, u32[]{:S(2)}) collective-permute-start(bf16[2,3,256]{2,1,0:T(4,128)(2,1)S(1)} %get-tuple-element.42), channel_id=1, source_target_pairs={{0,17},{1,18},{2,19},{3,20},{4,21},{5,22},{6,23},{7,24},{8,25},{9,... | collective-permute-start | bytes 9224 | tf_op jit(solution)/shard_map/ppermute | solution.py:348
  13.6 1.7 %collective-permute-start.3 = (bf16[64,3,256]{2,1,0:T(4,128)(2,1)S(1)}, bf16[64,3,256]{2,1,0:T(4,128)(2,1)S(1)}, u32[]{:S(2)}, u32[]{:S(2)}) collective-permute-start(bf16[64,3,256]{2,1,0:T(4,128)(2,1)S(1)} %pad_maximum_fusion.3), channel_id=1, source_target_pairs={{0,1},{1,2},{2,3},{3,4},{4,5},{5,6},{6,7},{7,8},{8,9},{9,10},{10,1... | collective-permute-start | bytes 294920 | tf_op jit(solution)/shard_map/ppermute | solution.py:338
  15.3 1.3 collective-permute-start.4
  16.6 8.0 %collective-permute-start.5 = (bf16[2,3,256]{2,1,0:T(4,128)(2,1)S(1)}, bf16[2,3,256]{2,1,0:T(4,128)(2,1)S(1)}, u32[]{:S(2)}, u32[]{:S(2)}) collective-permute-start(bf16[2,3,256]{2,1,0:T(4,128)(2,1)S(1)} %get-tuple-element.40), channel_id=1, source_target_pairs={{0,31},{1,16},{2,17},{3,18},{4,19},{5,20},{6,21},{7,22},{8,23},{9,... | collective-permute-start | bytes 9224 | tf_op jit(solution)/shard_map/ppermute | solution.py:348
  24.8 1.3 compare_select_fusion.1
  26.1 1.0 fusion.40
  28.9 1.0 copy-done.6
  30.0 0.2 concatenate.51
  30.5 0.3 copy-done.4
  30.8 2.3 %broadcast_in_dim.18 = f32[64,4,8,8,32]{0,4,3,2,1:T(8,128)} broadcast(f32[64,4,8,8]{0,3,2,1:T(8,128)S(1)} %bitcast.111), dimensions={0,1,2,3} | broadcast | bytes 2162688 | tf_op jit(solution)/shard_map/broadcast_in_dim | solution.py:371
  33.1 4.2 %copy.49.resample = f32[64,4,8,256]{3,2,1,0:T(8,128)} copy(f32[64,4,8,256]{0,3,2,1:T(8,128)} %bitcast.107) | data formatting | bytes 4194304 | tf_op jit(solution)/shard_map/reshape | solution.py:371
  37.3 0.5 copy.47
  37.8 0.8 broadcast_in_dim.20
  38.6 0.7 reshape.90
  39.3 0.4 copy.48
  39.6 1.1 pad.17.bands
  40.7 1.3 collective-permute-start.7
  42.0 4.6 %collective-permute-start = (bf16[3,256,256]{2,1,0:T(8,128)(2,1)S(1)}, bf16[3,256,256]{2,1,0:T(8,128)(2,1)S(1)}, u32[]{:S(2)}, u32[]{:S(2)}) collective-permute-start(bf16[3,256,256]{2,1,0:T(8,128)(2,1)S(1)} %pad_maximum_fusion.1), channel_id=1, source_target_pairs={{0,16},{1,17},{2,18},{3,19},{4,20},{5,21},{6,22},{7,23},{8,24},{9,... | collective-permute-start | bytes 1179656 | tf_op jit(solution)/shard_map/ppermute | solution.py:340
  46.7 1.5 collective-permute-start.1
  48.7 6.1 %concatenate.45.column_rim = bf16[68,32,256]{2,1,0:T(8,128)(2,1)} concatenate(bf16[68,6,256]{2,1,0:T(8,128)(2,1)S(1)} %broadcast.58, bf16[68,2,256]{2,1,0:T(2,128)(2,1)S(1)} %slice.211, bf16[68,2,256]{2,1,0:T(2,128)(2,1)S(1)} %slice.216, bf16[68,6,256]{2,1,0:T(8,128)(2,1)S(1)} %broadcast.58, bf16[68,7,256]{2,1,0:T(8,128)(2,1)S(1)} %broadcast.60, bf16[68,1,256]{2,1,0:T(2,128)(2,1)S(1)} %slice.217, ...), dimensions={1} | concatenate | bytes 2228224 | tf_op jit(solution)/shard_map/concatenate | solution.py:354
  54.8 0.4 collective-permute-done
  55.2 4.2 %collective-permute-done.1 = bf16[3,256,256]{2,1,0:T(8,128)(2,1)S(1)} collective-permute-done((bf16[3,256,256]{2,1,0:T(8,128)(2,1)S(1)}, bf16[3,256,256]{2,1,0:T(8,128)(2,1)S(1)}, u32[]{:S(2)}, u32[]{:S(2)}) %collective-permute-start.1) | collective-permute-done | bytes 393248 | tf_op jit(solution)/shard_map/ppermute | solution.py:341
  59.4 1.0 pad_maximum_fusion.sphere_rim
  60.4 69.1 %sweep.1 = f32[8,320,128]{2,1,0:T(8,128)} custom-call(bf16[6,256,256]{2,1,0:T(8,128)(2,1)} %pad_maximum_fusion.sphere_rim, bf16[68,32,256]{2,1,0:T(8,128)(2,1)} %concatenate.45.column_rim, bf16[64,256,256]{2,1,0:T(8,128)(2,1)} %cot_zero.1, bf16[64,256,256]{2,1,0:T(8,128)(2,1)} %cot_zero.1, bf16[64,256,256]{2,1,0:T(8,128)(2,1)} %cot_zero.1, ...), custom_call_target="tpu_custom_call" | custom-call | flops 51539607552 | bytes 25165824 | tf_op jit(solution)/shard_map/sweep/pallas_call | solution.py:223
  129.4 1.1 fusion.41
  130.6 0.5 collective-permute-start.9
  131.1 2.0 %collective-permute-done.8 = f32[8,32,128]{2,1,0:T(8,128)S(1)} collective-permute-done((f32[8,32,128]{2,1,0:T(8,128)S(1)}, f32[8,32,128]{2,1,0:T(8,128)S(1)}, u32[]{:S(2)}, u32[]{:S(2)}) %collective-permute-start.8) | collective-permute-done | bytes 131104 | tf_op jit(solution)/shard_map/ppermute | solution.py:385
  133.2 4.6 %collective-permute-done.9 = f32[8,32,128]{2,1,0:T(8,128)S(1)} collective-permute-done((f32[8,32,128]{2,1,0:T(8,128)S(1)}, f32[8,32,128]{2,1,0:T(8,128)S(1)}, u32[]{:S(2)}, u32[]{:S(2)}) %collective-permute-start.9) | collective-permute-done | bytes 131104 | tf_op jit(solution)/shard_map/ppermute | solution.py:386
  137.8 1.0 copy-done.1
  138.8 16.4 %reduce-scatter.2.cloned.1.call-done = f32[4,256,128]{2,1,0:T(8,128)} async-done(((f32[8,256,128]{2,1,0:T(8,128)}), f32[4,256,128]{2,1,0:T(8,128)}) %reduce-scatter.2.cloned.1.call-update) | async-done | bytes 524304 | tf_op jit(solution)/shard_map/reduce_scatter | solution.py:390
  (71 shorter events, 2.9 us)
Async XLA Ops:
  6.5 148.7 %reduce-scatter.2.cloned.1.call-start = ((), (), s32[]{:S(2)}) async-start(), calls=%async_computation.1 | async-start | bytes 1572864 | tf_op jit(solution)/shard_map/reduce_scatter | solution.py:390
  9.1 31.6 %collective-permute-start.2 = (bf16[2,3,256]{2,1,0:T(4,128)(2,1)S(1)}, bf16[2,3,256]{2,1,0:T(4,128)(2,1)S(1)}, u32[]{:S(2)}, u32[]{:S(2)}) collective-permute-start(bf16[2,3,256]{2,1,0:T(4,128)(2,1)S(1)} %get-tuple-element.42), channel_id=1, source_target_pairs={{0,17},{1,18},{2,19},{3,20},{4,21},{5,22},{6,23},{7,24},{8,25},{9,... | collective-permute-start | bytes 9224 | tf_op jit(solution)/shard_map/ppermute | solution.py:348
  13.6 33.1 %collective-permute-start.3 = (bf16[64,3,256]{2,1,0:T(4,128)(2,1)S(1)}, bf16[64,3,256]{2,1,0:T(4,128)(2,1)S(1)}, u32[]{:S(2)}, u32[]{:S(2)}) collective-permute-start(bf16[64,3,256]{2,1,0:T(4,128)(2,1)S(1)} %pad_maximum_fusion.3), channel_id=1, source_target_pairs={{0,1},{1,2},{2,3},{3,4},{4,5},{5,6},{6,7},{7,8},{8,9},{9,10},{10,1... | collective-permute-start | bytes 294920 | tf_op jit(solution)/shard_map/ppermute | solution.py:338
  15.3 33.0 %collective-permute-start.4 = (bf16[2,3,256]{2,1,0:T(4,128)(2,1)S(1)}, bf16[2,3,256]{2,1,0:T(4,128)(2,1)S(1)}, u32[]{:S(2)}, u32[]{:S(2)}) collective-permute-start(bf16[2,3,256]{2,1,0:T(4,128)(2,1)S(1)} %get-tuple-element.41), channel_id=1, source_target_pairs={{16,1},{17,2},{18,3},{19,4},{20,5},{21,6},{22,7},{23,8},{24,9},{25... | collective-permute-start | bytes 9224 | tf_op jit(solution)/shard_map/ppermute | solution.py:349
  16.6 10.5 %copy-start.2 = (bf16[3,3,3,32,32]{4,3,2,1,0:T(8,128)(2,1)S(1)}, bf16[3,3,3,32,32]{4,3,2,1,0:T(8,128)(2,1)}, u32[]{:S(2)}) copy-start(bf16[3,3,3,32,32]{4,3,2,1,0:T(8,128)(2,1)} %param.17) | copy-start | bytes 165892
  16.6 25.4 %collective-permute-start.5 = (bf16[2,3,256]{2,1,0:T(4,128)(2,1)S(1)}, bf16[2,3,256]{2,1,0:T(4,128)(2,1)S(1)}, u32[]{:S(2)}, u32[]{:S(2)}) collective-permute-start(bf16[2,3,256]{2,1,0:T(4,128)(2,1)S(1)} %get-tuple-element.40), channel_id=1, source_target_pairs={{0,31},{1,16},{2,17},{3,18},{4,19},{5,20},{6,21},{7,22},{8,23},{9,... | collective-permute-start | bytes 9224 | tf_op jit(solution)/shard_map/ppermute | solution.py:348
  24.8 23.5 %collective-permute-start.6 = (bf16[64,3,256]{2,1,0:T(4,128)(2,1)S(1)}, bf16[64,3,256]{2,1,0:T(4,128)(2,1)S(1)}, u32[]{:S(2)}, u32[]{:S(2)}) collective-permute-start(bf16[64,3,256]{2,1,0:T(4,128)(2,1)S(1)} %pad_maximum_fusion.4), channel_id=1, source_target_pairs={{0,15},{1,0},{2,1},{3,2},{4,3},{5,4},{6,5},{7,6},{8,7},{9,8},{10,9... | collective-permute-start | bytes 294920 | tf_op jit(solution)/shard_map/ppermute | solution.py:339
  26.1 1.9 %copy-start.3 = (bf16[3,3,3,32,32]{4,3,2,1,0:T(8,128)(2,1)S(1)}, bf16[3,3,3,32,32]{4,3,2,1,0:T(8,128)(2,1)}, u32[]{:S(2)}) copy-start(bf16[3,3,3,32,32]{4,3,2,1,0:T(8,128)(2,1)} %param.16) | copy-start | bytes 165892
  27.9 2.0 %copy-start.7 = (f32[4,64,8]{1,2,0:T(8,128)S(1)}, f32[4,64,8]{1,2,0:T(8,128)}, u32[]{:S(2)}) copy-start(f32[4,64,8]{1,2,0:T(8,128)} %param.19) | copy-start | bytes 24580
  27.9 2.0 %copy-start.8 = (s32[4,64]{1,0:T(4,128)S(1)}, s32[4,64]{1,0:T(4,128)}, u32[]{:S(2)}) copy-start(s32[4,64]{1,0:T(4,128)} %param.20) | copy-start | bytes 3076
  27.9 2.1 %copy-start.9 = (s32[4,64]{1,0:T(4,128)S(1)}, s32[4,64]{1,0:T(4,128)}, u32[]{:S(2)}) copy-start(s32[4,64]{1,0:T(4,128)} %param.21) | copy-start | bytes 3076
  28.0 2.2 %copy-start.5 = (bf16[9,8,32,256]{3,2,1,0:T(8,128)(2,1)}, bf16[9,8,32,256]{3,2,1,0:T(8,128)(2,1)S(1)}, u32[]{:S(2)}) copy-start(bf16[9,8,32,256]{3,2,1,0:T(8,128)(2,1)S(1)} %fusion.15) | copy-start | bytes 3538948
  28.9 1.0 copy-start.6
  29.9 0.9 copy-start.4
  40.7 7.8 %collective-permute-start.7 = (bf16[2,3,256]{2,1,0:T(4,128)(2,1)S(1)}, bf16[2,3,256]{2,1,0:T(4,128)(2,1)S(1)}, u32[]{:S(2)}, u32[]{:S(2)}) collective-permute-start(bf16[2,3,256]{2,1,0:T(4,128)(2,1)S(1)} %get-tuple-element.39), channel_id=1, source_target_pairs={{16,15},{17,0},{18,1},{19,2},{20,3},{21,4},{22,5},{23,6},{24,7},{2... | collective-permute-start | bytes 9224 | tf_op jit(solution)/shard_map/ppermute | solution.py:349
  42.0 13.2 %collective-permute-start = (bf16[3,256,256]{2,1,0:T(8,128)(2,1)S(1)}, bf16[3,256,256]{2,1,0:T(8,128)(2,1)S(1)}, u32[]{:S(2)}, u32[]{:S(2)}) collective-permute-start(bf16[3,256,256]{2,1,0:T(8,128)(2,1)S(1)} %pad_maximum_fusion.1), channel_id=1, source_target_pairs={{0,16},{1,17},{2,18},{3,19},{4,20},{5,21},{6,22},{7,23},{8,24},{9,... | collective-permute-start | bytes 1179656 | tf_op jit(solution)/shard_map/ppermute | solution.py:340
  46.7 12.7 %collective-permute-start.1 = (bf16[3,256,256]{2,1,0:T(8,128)(2,1)S(1)}, bf16[3,256,256]{2,1,0:T(8,128)(2,1)S(1)}, u32[]{:S(2)}, u32[]{:S(2)}) collective-permute-start(bf16[3,256,256]{2,1,0:T(8,128)(2,1)S(1)} %pad_maximum_fusion.2), channel_id=1, source_target_pairs={{16,0},{17,1},{18,2},{19,3},{20,4},{21,5},{22,6},{23,7},{24,8},{25... | collective-permute-start | bytes 1179656 | tf_op jit(solution)/shard_map/ppermute | solution.py:341
  129.4 3.7 %copy-start = (f32[8,320,128]{2,1,0:T(8,128)S(1)}, f32[8,320,128]{2,1,0:T(8,128)}, u32[]{:S(2)}) copy-start(f32[8,320,128]{2,1,0:T(8,128)} %sweep.1) | copy-start | bytes 3932164
  130.5 2.6 %slice-start = ((f32[8,320,128]{2,1,0:T(8,128)}), f32[8,256,128]{2,1,0:T(8,128)S(1)}, s32[]{:S(2)}) async-start(f32[8,320,128]{2,1,0:T(8,128)} %sweep.1), calls=%async_computation.2 | async-start | bytes 2097152 | tf_op jit(solution)/shard_map/slice | solution.py:387
  130.6 2.6 %collective-permute-start.8 = (f32[8,32,128]{2,1,0:T(8,128)S(1)}, f32[8,32,128]{2,1,0:T(8,128)S(1)}, u32[]{:S(2)}, u32[]{:S(2)}) collective-permute-start(f32[8,32,128]{2,1,0:T(8,128)S(1)} %get-tuple-element.38), channel_id=1, source_target_pairs={{0,15},{1,0},{2,1},{3,2},{4,3},{5,4},{6,5},{7,6},{8,7},{9,8},{10,9... | collective-permute-start | bytes 393224 | tf_op jit(solution)/shard_map/ppermute | solution.py:385
  130.6 7.1 %collective-permute-start.9 = (f32[8,32,128]{2,1,0:T(8,128)S(1)}, f32[8,32,128]{2,1,0:T(8,128)S(1)}, u32[]{:S(2)}, u32[]{:S(2)}) collective-permute-start(f32[8,32,128]{2,1,0:T(8,128)S(1)} %get-tuple-element.37), channel_id=1, source_target_pairs={{0,1},{1,2},{2,3},{3,4},{4,5},{5,6},{6,7},{7,8},{8,9},{9,10},{10,1... | collective-permute-start | bytes 393224 | tf_op jit(solution)/shard_map/ppermute | solution.py:386
  137.8 1.0 copy-start.1
Sparse Core Ops, SparseCore 0:
  138.9 16.2 reduce-scatter.1

commit v2 on v1

v2 whole, which is shorter than its diff:
```python
import functools

import jax
import jax.numpy as jnp
from jax import lax
from jax.experimental import pallas as pl
from jax.experimental.pallas import tpu as pltpu
from jax.sharding import PartitionSpec as P

TAPS = 8
SHIFT = 24
MARGIN = SHIFT + TAPS
GROUP = 4
VBLOCK = 64
SLOT = 16
BF16 = jnp.bfloat16
F32 = jnp.float32


def edge_kernel(
    side, cot_left, cot_right, second_left, second_right, first_left, first_right,
    cot_rim, second_rim, first_rim, left, right, rim, corner_left, corner_right,
):
    spheres = cot_left.shape[0]
    gate = lambda cot, saved: jnp.where(saved > 0, cot, jnp.zeros_like(cot))
    top = side[0]
    for message, corner, cot, saved, kept, columns, one in (
        (left, corner_left, cot_left, second_left, first_left, slice(0, 2), slice(0, 1)),
        (right, corner_right, cot_right, second_right, first_right, slice(6, 8), slice(7, 8)),
    ):
        message[:, 0:2] = gate(cot[:, columns], saved[:, columns])
        message[:, 2:3] = kept[:, one]
        message[:, 3:4] = kept[:, one]
        for index in range(2):
            sphere = top * (spheres - 1) + (1 - 2 * top) * index
            corner[index, 0:2] = gate(cot[sphere, columns], saved[sphere, columns])
            corner[index, 2:3] = kept[sphere, one]
            corner[index, 3:4] = kept[sphere, one]
    for index in range(2):
        place = top + (1 - 2 * top) * index
        rim[index] = gate(cot_rim[place], second_rim[place])
    rim[2] = first_rim[0]


def edges(side, cot, second, first):
    spheres, columns, merged = cot.shape
    pairs = spheres // 2
    low = pl.BlockSpec((spheres, 8, merged), lambda g, s: (0, 0, 0))
    high = pl.BlockSpec((spheres, 8, merged), lambda g, s: (0, columns // 8 - 1, 0))
    pair = pl.BlockSpec((2, columns, merged), lambda g, s: (s[0] * (pairs - 1), 0, 0))
    one = pl.BlockSpec((1, columns, merged), lambda g, s: (s[0] * (spheres - 1), 0, 0))
    shapes = (
        (spheres, 4, merged), (spheres, 4, merged), (3, columns, merged),
        (2, 4, merged), (2, 4, merged),
    )
    return pl.pallas_call(
        edge_kernel,
        grid_spec=pltpu.PrefetchScalarGridSpec(
            num_scalar_prefetch=1,
            grid=(1,),
            in_specs=[low, high, low, high, low, high, pair, pair, one],
            out_specs=[pl.BlockSpec(s, lambda g, s: (0, 0, 0)) for s in shapes],
        ),
        out_shape=[jax.ShapeDtypeStruct(s, BF16) for s in shapes],
        name="edges",
    )(side, cot, cot, second, second, first, first, cot, second, first)


def sweep_kernel(names, first_group, head, tail, row_count, pair_rows, *refs):
    ref = dict(zip(names, refs))
    flip = ref["info"][0]
    step = pl.program_id(0)
    group = step + first_group
    from_left, from_right = ref["from_left"], ref["from_right"]
    spheres, _, merged = from_left.shape
    taps_one, taps_two = ref["taps_one"], ref["taps_two"]
    columns = taps_two.shape[1]
    volume, mixed, total = ref["volume"], ref["mixed"], ref["total"]
    cameras = total.shape[0]
    channels = merged // row_count
    wide = columns + 16
    blocks = columns // VBLOCK
    window = VBLOCK + 2 * MARGIN
    padded_one, padded_two = ref["padded_one"], ref["padded_two"]
    actual = lambda v: flip * (spheres - 1) + (1 - 2 * flip) * v
    inner = lambda i: flip + (1 - 2 * flip) * i
    mixer_at = lambda name, depth: ref[name][2 * flip + (1 - 2 * flip) * depth]

    def store_taps(source, target, slot, rows):
        for tap in range(3):
            target[slot, :, tap * merged : (tap + 1) * merged] = source[
                9 - tap : 9 - tap + rows
            ].astype(BF16)

    def gate_second(grad, sides, index, slot):
        padded = padded_one.at[index]
        padded[16 : 16 + columns] = grad.astype(F32)
        padded[14:16] = sides[0][0:2].astype(F32)
        padded[16 + columns : 18 + columns] = sides[1][0:2].astype(F32)
        store_taps(padded, taps_one, slot, wide)

    def masked(cot, saved):
        return jnp.where(saved > 0, cot, jnp.zeros_like(cot))

    def sides_of(v):
        sphere = actual(v)
        return from_left[sphere], from_right[sphere]

    def old(name, slot):
        if tail and slot < 2:
            return ref["carry_" + name][slot]
        return ref[name][slot]

    def conv(name, mixers, slots):
        lhs = lambda depth: jnp.concatenate(
            [old(name, slot + 2 - depth) for slot in slots], axis=0
        )
        value = jnp.dot(lhs(2), mixer_at(mixers, 2), preferred_element_type=F32)
        value = value + jnp.dot(lhs(1), mixer_at(mixers, 1), preferred_element_type=F32)
        return value + jnp.dot(lhs(0), mixer_at(mixers, 0), preferred_element_type=F32)

    def gate_first(hidden, saved, sides, index, slot):
        low = jnp.broadcast_to(sides[0][2:3].astype(F32), (8, merged))
        high = jnp.broadcast_to(sides[1][2:3].astype(F32), (8, merged))
        keep = jnp.concatenate([low, saved.astype(F32), high], axis=0) > 0
        padded_two[index] = jnp.where(keep, hidden, 0.0)
        store_taps(padded_two.at[index], taps_two, slot, columns)

    lane = lax.broadcasted_iota(jnp.int32, (channels, merged), 1)
    sub = lax.broadcasted_iota(jnp.int32, (channels, merged), 0)
    diagonal = lax.rem(lane, channels) == sub
    table_lanes = cameras * row_count * row_count
    owner = lax.broadcasted_iota(
        jnp.int32, (cameras * row_count, table_lanes), 1
    ) // row_count == lax.broadcasted_iota(jnp.int32, (cameras * row_count, table_lanes), 0)

    def mix_rows(group, source):
        rows = [
            jnp.where(owner, ref["row_table"][actual(group * GROUP + sphere)], 0.0)
            for sphere in range(GROUP)
        ]
        spread = jnp.dot(
            jnp.concatenate(rows, axis=0).astype(BF16),
            ref["expand"][...],
            preferred_element_type=F32,
        )
        for camera in range(cameras):
            for sphere in range(GROUP):
                start = (sphere * cameras + camera) * row_count
                weights = jnp.concatenate(
                    [
                        jnp.where(diagonal, spread[start + r : start + r + 1], 0.0)
                        for r in range(row_count)
                    ],
                    axis=0,
                ).astype(BF16)
                value = jnp.dot(
                    source[sphere], weights, preferred_element_type=F32
                ).astype(BF16)
                for block in range(blocks):
                    mixed[camera, block, sphere * VBLOCK : (sphere + 1) * VBLOCK] = value[
                        block * VBLOCK : (block + 1) * VBLOCK
                    ]

    width = GROUP * VBLOCK
    distance = (
        lax.rem(lax.broadcasted_iota(jnp.int32, (window, width), 1), VBLOCK)
        - lax.broadcasted_iota(jnp.int32, (window, width), 0)
        + MARGIN
    ).astype(F32)

    def warp_columns(group):
        quarter = lax.broadcasted_iota(jnp.int32, (spheres, width), 1) // VBLOCK
        chosen = lax.broadcasted_iota(jnp.int32, (spheres, width), 0) == actual(
            group * GROUP + quarter
        )
        rows_all = jnp.dot(
            ref["tap_table"][...], chosen.astype(BF16), preferred_element_type=F32
        )
        for camera in range(cameras):
            rows = rows_all[camera * SLOT : (camera + 1) * SLOT]
            tap_of = distance - rows[TAPS : TAPS + 1]
            matrix = jnp.zeros((window, width), F32)
            for tap in range(TAPS):
                matrix = jnp.where(tap_of == float(tap), rows[tap : tap + 1], matrix)
            matrix = matrix.astype(BF16)
            for block in range(blocks):
                place = slice(block * VBLOCK, block * VBLOCK + window)
                total[camera, place] = total[camera, place] + jnp.dot(
                    matrix, mixed[camera, block], preferred_element_type=F32
                )

    @pl.when(step == 0)
    def _():
        from_table = lax.broadcasted_iota(jnp.int32, (table_lanes, merged), 0)
        to_lane = lax.broadcasted_iota(jnp.int32, (table_lanes, merged), 1)
        ref["expand"][...] = jnp.where(
            lax.rem(from_table, row_count) == to_lane // channels, 1.0, 0.0
        ).astype(BF16)
        if not head:
            total[...] = ref["carry_total"][...]
            return
        total[...] = jnp.zeros_like(total)
        volume[...] = jnp.zeros_like(volume)
        if "low_rim" in ref:
            low_rim = ref["low_rim"]
            for index in range(2):
                sides = ref["low_left"][1 - index], ref["low_right"][1 - index]
                gate_second(low_rim[1 - index], sides, index, 2 + index)
        else:
            taps_one[2] = jnp.zeros_like(taps_one[2])
            taps_one[3] = jnp.zeros_like(taps_one[3])
        for index in range(2):
            place = inner(index)
            grad = masked(ref["cot_zero"][place], ref["second_zero"][place])
            gate_second(grad, sides_of(index), 2 + index, index)
        order = (2, 3, 0, 1)
        for index in range(2):
            if index == 0 and "low_rim" not in ref:
                taps_two[0] = jnp.zeros_like(taps_two[0])
                continue
            hidden = jnp.zeros((wide, merged), F32)
            for depth in range(3):
                hidden = hidden + jnp.dot(
                    taps_one[order[index + 2 - depth]],
                    mixer_at("mixer_second", depth),
                    preferred_element_type=F32,
                )
            if index == 0:
                saved = ref["low_rim"][2]
                sides = ref["low_left"][0], ref["low_right"][0]
            else:
                saved = ref["first_zero"][0]
                sides = sides_of(0)
            gate_first(hidden, saved, sides, index, index)

    base = group * GROUP
    before = jnp.maximum(group - 1, 0)

    for index in range(2):
        place = inner(index)
        grad = masked(ref["cot_a"][place], ref["second_a"][place])
        gate_second(grad, sides_of(base + 2 + index), index, 2 + index)
    hidden = conv("taps_one", "mixer_second", (0, 1))
    gate_first(hidden[:wide], ref["first_a"][0], sides_of(base + 1), 0, 2)
    gate_first(hidden[wide:], ref["first_b"][0], sides_of(base + 2), 1, 3)
    for index in range(2):
        if tail:
            grad = ref["high_rim"][index]
            sides = ref["high_left"][index], ref["high_right"][index]
        else:
            place = inner(index)
            grad = masked(ref["cot_b"][place], ref["second_b"][place])
            sides = sides_of(base + 4 + index)
        gate_second(grad, sides, 2 + index, 4 + index)
    mix_rows(before, ref["carry_volume"] if tail else volume)
    hidden = conv("taps_one", "mixer_second", (2, 3))
    gate_first(hidden[:wide], ref["first_c"][0], sides_of(base + 3), 2, 4)
    if tail:
        saved = ref["high_rim"][2]
        sides = ref["high_left"][0], ref["high_right"][0]
    else:
        saved = ref["first_d"][0]
        sides = sides_of(base + 4)
    gate_first(hidden[wide:], saved, sides, 3, 5)
    for pair in range(2):
        value = conv("taps_two", "mixer_first", (2 * pair, 2 * pair + 1)).astype(BF16)
        volume[2 * pair] = value[:columns]
        volume[2 * pair + 1] = value[columns:]
        if pair == 0:
            warp_columns(before)

    if not tail:
        for slot in range(2):
            taps_one[slot] = taps_one[slot + 4]
            taps_two[slot] = taps_two[slot + 4]

        @pl.when(step == pl.num_programs(0) - 1)
        def _():
            for slot in range(2):
                ref["next_taps_one"][slot] = taps_one[slot]
                ref["next_taps_two"][slot] = taps_two[slot]
            ref["next_volume"][...] = volume[...]
            ref["next_total"][...] = total[...]

        return

    mix_rows(group, volume)
    warp_columns(group)

    def joined(row, place):
        return jnp.concatenate(
            [
                total[camera, place, row * channels : (row + 1) * channels]
                for camera in range(cameras)
            ],
            axis=1,
        )

    everything = slice(0, columns + 2 * MARGIN)
    if not pair_rows:
        for row in range(row_count):
            ref["whole"][row] = joined(row, everything)
        return
    half = row_count // 2
    own_high = ref["info"][1] > 0
    for row in range(half):
        low, high = joined(row, everything), joined(row + half, everything)
        for prefix, value in (
            ("own", jnp.where(own_high, high, low)),
            ("peer", jnp.where(own_high, low, high)),
        ):
            main = value[MARGIN : MARGIN + columns]
            ref[prefix][row] = main if prefix == "own" else main.astype(BF16)
            ref[prefix + "_left"][row] = value[:MARGIN].astype(BF16)
            ref[prefix + "_right"][row] = value[MARGIN + columns :].astype(BF16)


def sweep(first_group, count, head, tail, info, arrays, carry, row_count, pair_rows):
    cot, second, first = arrays["cot"], arrays["second"], arrays["first"]
    spheres, columns, merged = cot.shape
    cameras = arrays["cameras"]
    wide = columns + 16
    extended = columns + 2 * MARGIN
    pairs = spheres // 2
    channels = merged // row_count
    names, specs, operands = [], [], []

    def add(name, array, spec):
        names.append(name)
        specs.append(spec)
        operands.append(array)

    def whole(shape):
        zeros = (0,) * len(shape)
        return pl.BlockSpec(
            shape, lambda g, s: zeros, pipeline_mode=pl.Buffered(buffer_count=1)
        )

    def spheres_at(size, place, **more):
        limit = spheres // size - 1
        return pl.BlockSpec(
            (size, columns, merged),
            lambda g, s: (s[0] * limit + (1 - 2 * s[0]) * place(g + first_group), 0, 0),
            **more,
        )

    for name in ("from_left", "from_right", "mixer_second", "mixer_first", "row_table", "tap_table"):
        add(name, arrays[name], whole(arrays[name].shape))
    rims = (("low_rim", "low_left", "low_right") if head else ()) + (
        ("high_rim", "high_left", "high_right") if tail else ()
    )
    for name in rims:
        if name in arrays:
            add(name, arrays[name], whole(arrays[name].shape))
    for name, array in (("cot", cot), ("second", second)):
        add(name + "_a", array, spheres_at(2, lambda g: 2 * g + 1))
        if not tail:
            add(name + "_b", array, spheres_at(2, lambda g: 2 * g + 2))
        if head:
            add(name + "_zero", array, spheres_at(2, lambda g: 0, pipeline_mode=pl.Buffered(buffer_count=1)))
    for ahead, letter in ((1, "a"), (2, "b"), (3, "c"), (4, "d")):
        if not (tail and ahead == 4):
            add("first_" + letter, first, spheres_at(1, lambda g, ahead=ahead: GROUP * g + ahead))
    if head:
        add("first_zero", first, spheres_at(1, lambda g: 0, pipeline_mode=pl.Buffered(buffer_count=1)))
    carried = {
        "taps_one": ((2, wide, 3 * merged), BF16),
        "taps_two": ((2, columns, 3 * merged), BF16),
        "volume": ((GROUP, columns, merged), BF16),
        "total": ((cameras, extended, merged), F32),
    }
    if not head:
        for name in carried:
            add("carry_" + name, carry[name], whole(carried[name][0]))
    outputs = {}
    if not tail:
        outputs = {"next_" + name: value for name, value in carried.items()}
    elif pair_rows:
        half, lanes = row_count // 2, cameras * channels
        for prefix in ("own", "peer"):
            outputs[prefix] = ((half, columns, lanes), F32 if prefix == "own" else BF16)
            outputs[prefix + "_left"] = ((half, MARGIN, lanes), BF16)
            outputs[prefix + "_right"] = ((half, MARGIN, lanes), BF16)
    else:
        outputs["whole"] = ((row_count, extended, cameras * channels), F32)
    scratch = {
        "taps_one": ((6, wide, 3 * merged), BF16),
        "taps_two": ((6, columns, 3 * merged), BF16),
        "padded_one": ((4, columns + 32, merged), F32),
        "padded_two": ((4, wide, merged), F32),
        "volume": carried["volume"],
        "mixed": ((cameras, columns // VBLOCK, GROUP * VBLOCK, merged), BF16),
        "total": carried["total"],
        "expand": ((cameras * row_count * row_count, merged), BF16),
    }
    every = ["info", *names, *outputs, *scratch]
    flops = 2 * GROUP * count * columns * merged * merged * (18 + cameras + cameras // 2)
    results = pl.pallas_call(
        functools.partial(
            sweep_kernel, every, first_group, head, tail, row_count, pair_rows
        ),
        grid_spec=pltpu.PrefetchScalarGridSpec(
            num_scalar_prefetch=1,
            grid=(count,),
            in_specs=specs,
            out_specs=[whole(shape) for shape, _ in outputs.values()],
            scratch_shapes=[pltpu.VMEM(shape, kind) for shape, kind in scratch.values()],
        ),
        out_shape=[jax.ShapeDtypeStruct(shape, kind) for shape, kind in outputs.values()],
        compiler_params=pltpu.CompilerParams(
            dimension_semantics=("arbitrary",), vmem_limit_bytes=56 * 2**20
        ),
        cost_estimate=pl.CostEstimate(
            flops=flops, bytes_accessed=3 * GROUP * count * columns * merged * 2, transcendentals=0
        ),
        name="sweep_tail" if tail else "sweep",
    )(info, *operands)
    return {name.removeprefix("next_"): result for name, result in zip(outputs, results)}


def finish_kernel(own, peer, own_left, own_right, peer_left, peer_right, out):
    columns = out.shape[1]
    out[...] = own[...] + peer[...].astype(F32)
    start, end = slice(0, MARGIN), slice(columns - MARGIN, columns)
    out[:, start] = out[:, start] + (own_left[...].astype(F32) + peer_left[...].astype(F32))
    out[:, end] = out[:, end] + (own_right[...].astype(F32) + peer_right[...].astype(F32))


def row_mixers(kernel, row_count):
    channels = kernel.shape[3]
    strip = jnp.transpose(kernel, (0, 1, 4, 2, 3)).reshape(9, channels, 3 * channels)
    merged = row_count * channels
    strip = jnp.pad(strip, ((0, 0), (0, 0), (merged, merged)))
    rows = [
        lax.slice_in_dim(
            strip, merged - (row - 1) * channels, 2 * merged - (row - 1) * channels, axis=2
        )
        for row in range(row_count)
    ]
    return jnp.stack(rows, axis=1).reshape(3, 3 * merged, merged)


def ring(offset):
    count = lax.axis_size("azim")
    return [(i, (i + offset) % count) for i in range(count)]


def stride(offset):
    count = lax.axis_size("depth")
    if count == 2:
        return [(0, 1), (1, 0)]
    return [(i, i + offset) for i in range(count) if 0 <= i + offset < count]


def joint(depth_pairs, azim_pairs):
    width = lax.axis_size("azim")
    return [
        (d0 * width + a0, d1 * width + a1)
        for d0, d1 in depth_pairs
        for a0, a1 in azim_pairs
    ]


def body(cot, second, first, kernel_first, kernel_second, row_resample, col_taps, band_width, col_offset):
    spheres, columns, merged = cot.shape
    cameras, _, row_count, _ = row_resample.shape
    depth_index = lax.axis_index("depth").astype(jnp.int32)
    paired = lax.axis_size("depth") == 2
    both = ("depth", "azim")
    forward, backward = ring(1), ring(-1)
    arrays = {"cot": cot, "second": second, "first": first, "cameras": cameras}

    def send_rims(prefix, offset, side):
        left, right, rim, corner_left, corner_right = edges(
            jnp.full((1,), side, jnp.int32), cot, second, first
        )
        if "from_left" not in arrays:
            arrays["from_left"] = lax.ppermute(right, "azim", forward)
            arrays["from_right"] = lax.ppermute(left, "azim", backward)
        pairs = stride(offset)
        arrays[prefix + "_rim"] = lax.ppermute(rim, "depth", pairs)
        arrays[prefix + "_left"] = lax.ppermute(corner_right, both, joint(pairs, forward))
        arrays[prefix + "_right"] = lax.ppermute(corner_left, both, joint(pairs, backward))

    if paired:
        send_rims("high", -1, 1 - depth_index)
        flip = depth_index
    else:
        send_rims("low", 1, 1)
        send_rims("high", -1, 0)
        flip = jnp.zeros((), jnp.int32)
    info = jnp.stack([flip, depth_index])

    arrays["mixer_second"] = row_mixers(kernel_second, row_count)
    arrays["mixer_first"] = row_mixers(kernel_first, row_count)
    arrays["row_table"] = jnp.transpose(row_resample, (1, 0, 2, 3)).reshape(spheres, 1, -1)
    keep = lax.broadcasted_iota(jnp.int32, col_taps.shape, 2) < band_width[:, :, None]
    taps = jnp.where(keep, col_taps, 0.0)
    table = jnp.concatenate([taps, col_offset[:, :, None].astype(F32)], axis=2)
    table = jnp.pad(jnp.transpose(table, (0, 2, 1)), ((0, 0), (0, SLOT - TAPS - 1), (0, 0)))
    arrays["tap_table"] = table.reshape(cameras * SLOT, spheres).astype(BF16)

    groups = spheres // GROUP
    carry = sweep(0, groups - 1, True, False, info, arrays, None, row_count, paired)
    parts = sweep(groups - 1, 1, False, True, info, arrays, carry, row_count, paired)

    if paired:
        swap = [(0, 1), (1, 0)]
        got = (
            lax.ppermute(parts["peer"], "depth", swap),
            lax.ppermute(parts["own_right"], "azim", forward),
            lax.ppermute(parts["own_left"], "azim", backward),
            lax.ppermute(parts["peer_right"], both, joint(swap, forward)),
            lax.ppermute(parts["peer_left"], both, joint(swap, backward)),
        )
        return pl.pallas_call(
            finish_kernel,
            out_shape=jax.ShapeDtypeStruct(parts["own"].shape, F32),
            name="finish",
        )(parts["own"], *got)
    partial = parts["whole"]
    spill_left = lax.ppermute(partial[:, :MARGIN], "azim", backward)
    spill_right = lax.ppermute(partial[:, columns + MARGIN :], "azim", forward)
    inner = partial[:, MARGIN : columns + MARGIN]
    inner = inner.at[:, columns - MARGIN :].add(spill_left)
    inner = inner.at[:, :MARGIN].add(spill_right)
    return lax.psum_scatter(inner, "depth", scatter_dimension=0, tiled=True)


def solution(mesh):
    placed = (
        P("depth", "azim", None),
        P("depth", "azim", None),
        P("depth", "azim", None),
        P(),
        P(),
        P(None, "depth", None, None),
        P(None, "depth", None),
        P(None, "depth"),
        P(None, "depth"),
    )
    return jax.shard_map(
        body, mesh=mesh, in_specs=placed, out_specs=P("depth", "azim", None), check_vma=False
    )
```

time: 162 us -> 116 us (0.72)
  waiting for transfers between devices: 27.7 us -> 1.91 us
  local copies, waits for them, and re-layouts: 23.9 us -> 5.47 us
  Pallas kernels: 69.1 us -> 84.7 us
  between operations: 13.9 us -> 0.32 us
  other arithmetic: 4.27 us -> 0.6 us
    reduce_scatter x1 -> x0, waiting for transfers between devices: 16.4 us -> none  [body(): return lax.psum_scatter(inner, 'depth', scatter_dimension=0, tiled=True)]
    pallas_call x1 -> x4, Pallas kernels: 69.1 us -> 84.7 us  [the longest x2 80 us: sweep(): pl.pallas_call(functools.partial(sweep_kernel, every, first_group, head,...]
    ppermute x10, waiting for transfers between devices: 11.2 us -> 1.91 us  [the longest x1 1.78 us: body(): lax.ppermute(parts['peer_right'], both, joint(swap, forward))]
    concatenate x5 -> x0, local copies, waits for them, and re-layouts: 6.38 us -> none  [the longest x1 6.07 us: body(): jnp.concatenate([blank(6), side_left[:, :2], side_right[:, :2], blank(6),...]
    reshape x3 -> x1, local copies, waits for them, and re-layouts: 5.28 us -> 0.7 us  [body(): jnp.transpose(row_resample, (1, 0, 2, 3)).reshape(spheres, 1, -1)]
    slice x9 -> x0, local copies, waits for them, and re-layouts: 3.52 us -> none  [the longest x2 2.17 us: edge(): first[sphere_first, column_first]]
    broadcast_in_dim x2 -> x0, local copies, waits for them, and re-layouts: 3.04 us -> none  [the longest x1 2.29 us: body(): jnp.repeat(jnp.transpose(row_resample, (1, 0, 2, 3)), channels, axis=3)]
    select_n x2 -> x0, other arithmetic: 2.68 us -> none  [body(): jnp.where(second[where] > 0, cot[where], jnp.zeros((), BF16))]
  transfers between devices with their start and end apart: 11 -> 10, of which waited for: 5 -> 2; matrix products, arithmetic and copies ran while one was open for 13% -> 3% of each run, Pallas kernels for 0% -> 59%
where the time goes in v2:
time: 116 us
  Pallas kernels  84.7 us (73%)
  starting transfers between devices  22.7 us (20%)
  local copies, waits for them, and re-layouts  5.47 us (5%)
  waiting for transfers between devices  1.91 us (2%)
    pallas_call x2, Pallas kernels, sweep(): pl.pallas_call(functools.partial(sweep_kernel, every, first_group, head,...  80 us
    ppermute x1, starting transfers between devices, body(): lax.ppermute(parts['peer_left'], both, joint(swap, backward))  5.34 us
    ppermute x1, starting transfers between devices, send_rims(): arrays['from_right'] = lax.ppermute(left, 'azim', backward)  4.44 us
    ppermute x1, starting transfers between devices, body(): lax.ppermute(parts['own_left'], 'azim', backward)  4.44 us
    ppermute x1, starting transfers between devices, send_rims(): lax.ppermute(corner_left, both, joint(pairs, backward))  4.02 us
    unnamed x50, local copies, waits for them, and re-layouts  3.69 us
    pallas_call x1, Pallas kernels, edges(): pl.pallas_call(edge_kernel, grid_spec=pltpu.PrefetchScalarGridSpec(num_sc...  2.76 us
    ppermute x1, starting transfers between devices, send_rims(): lax.ppermute(corner_right, both, joint(pairs, forward))  2.45 us
  transfers between devices with their start and end apart: 10, of which 2 were waited for; matrix products, arithmetic and copies ran while one was open for 3% of the time, Pallas kernels for 59%

profile of v2, /device:TPU:0, one launch (start us, length us, event | category | flops | bytes accessed | tf_op | source)
XLA Modules:
  0.0 115.8 jit_solution(11357600633470820473)
XLA Ops:
  0.0 2.8 %edges.1 = (bf16[64,4,256]{2,1,0:T(4,128)(2,1)}, bf16[64,4,256]{2,1,0:T(4,128)(2,1)}, bf16[3,256,256]{2,1,0:T(8,128)(2,1)}, bf16[2,4,256]{2,1,0:T(4,128)(2,1)}, bf16[2,4,256]{2,1,0:T(4,128)(2,1)}) custom-call(s32[1]{0:T(128)} %bitcast.1.side, bf16[64,256,256]{2,1,0:T(8,128)(2,1)} %refs_10_.3, bf16[64,256,256]{2,1,0:T(8,128)(2,1)} %refs_10_.3, ...), custom_call_target="tpu_custom_call" | custom-call | tf_op jit(solution)/shard_map/edges/pallas_call | solution.py:56
  2.8 2.4 %collective-permute-start.3 = (bf16[2,4,256]{2,1,0:T(4,128)(2,1)}, bf16[2,4,256]{2,1,0:T(4,128)(2,1)S(1)}, u32[]{:S(2)}, u32[]{:S(2)}) collective-permute-start(bf16[2,4,256]{2,1,0:T(4,128)(2,1)} %get-tuple-element.23), channel_id=1, source_target_pairs={{0,17},{1,18},{2,19},{3,20},{4,21},{5,22},{6,23},{7,24},{8,25},{9,... | collective-permute-start | bytes 12296 | tf_op jit(solution)/shard_map/ppermute | solution.py:483
  5.2 4.0 %collective-permute-start.4 = (bf16[2,4,256]{2,1,0:T(4,128)(2,1)}, bf16[2,4,256]{2,1,0:T(4,128)(2,1)S(1)}, u32[]{:S(2)}, u32[]{:S(2)}) collective-permute-start(bf16[2,4,256]{2,1,0:T(4,128)(2,1)} %get-tuple-element.24), channel_id=1, source_target_pairs={{0,31},{1,16},{2,17},{3,18},{4,19},{5,20},{6,21},{7,22},{8,23},{9,... | collective-permute-start | bytes 12296 | tf_op jit(solution)/shard_map/ppermute | solution.py:484
  9.2 4.4 %collective-permute-start.1 = (bf16[64,4,256]{2,1,0:T(4,128)(2,1)}, bf16[64,4,256]{2,1,0:T(4,128)(2,1)S(1)}, u32[]{:S(2)}, u32[]{:S(2)}) collective-permute-start(bf16[64,4,256]{2,1,0:T(4,128)(2,1)} %get-tuple-element.21), channel_id=1, source_target_pairs={{0,15},{1,0},{2,1},{3,2},{4,3},{5,4},{6,5},{7,6},{8,7},{9,8},{10,9... | collective-permute-start | bytes 393224 | tf_op jit(solution)/shard_map/ppermute | solution.py:480
  13.7 1.9 %collective-permute-start.2 = (bf16[3,256,256]{2,1,0:T(8,128)(2,1)}, bf16[3,256,256]{2,1,0:T(8,128)(2,1)S(1)}, u32[]{:S(2)}, u32[]{:S(2)}) collective-permute-start(bf16[3,256,256]{2,1,0:T(8,128)(2,1)} %get-tuple-element.22), channel_id=1, source_target_pairs={{0,16},{16,0},{1,17},{17,1},{2,18},{18,2},{3,19},{19,3},{4,20},{20... | collective-permute-start | bytes 1179656 | tf_op jit(solution)/shard_map/ppermute | solution.py:482
  15.6 0.1 copy.36
  15.7 0.1 copy.28
  15.9 0.1 fusion.1
  16.0 0.1 fusion.5
  16.1 0.1 fusion.7
  16.3 0.1 fusion.9
  16.4 0.1 fusion.13
  16.8 0.1 fusion.21
  16.9 0.1 fusion.23
  17.0 0.1 fusion.25
  17.3 0.6 pad_add_fusion.refs_0_
  17.9 0.7 copy.46.refs_5_
  18.6 0.6 pad.14
  19.3 1.0 copy-done.1
  20.4 68.4 %sweep.1 = (bf16[2,272,768]{2,1,0:T(8,128)(2,1)}, bf16[2,256,768]{2,1,0:T(8,128)(2,1)}, bf16[4,256,256]{2,1,0:T(8,128)(2,1)}, f32[4,320,256]{2,1,0:T(8,128)}) custom-call(s32[2]{0:T(128)} %pad_add_fusion.refs_0_, bf16[64,4,256]{2,1,0:T(4,128)(2,1)} %copy-done.6, bf16[64,4,256]{2,1,0:T(4,128)(2,1)} %copy-done.7, bf16[3,768,256]{2,1,0:T(8,128)(2,1)} %bitcast.110, ...), custom_call_target="tpu_custom_call" | custom-call | flops 48318382080 | bytes 23592960 | tf_op jit(solution)/shard_map/sweep/pallas_call | solution.py:399
  88.8 0.5 copy-done.14
  89.4 0.2 copy-done.2
  89.6 11.6 %sweep_tail.1 = (f32[4,256,128]{2,1,0:T(8,128)}, bf16[4,32,128]{2,1,0:T(8,128)(2,1)}, bf16[4,32,128]{2,1,0:T(8,128)(2,1)}, bf16[4,256,128]{2,1,0:T(8,128)(2,1)},...) custom-call(s32[2]{0:T(128)} %pad_add_fusion.refs_0_, bf16[64,4,256]{2,1,0:T(4,128)(2,1)} %copy-done.6, ...), custom_call_target="tpu_custom_call" | custom-call | flops 3221225472 | bytes 1572864 | tf_op jit(solution)/shard_map/sweep_tail/pallas_call | solution.py:399
  101.2 0.2 collective-permute-start.5
  101.4 4.4 %collective-permute-start.7 = (bf16[4,32,128]{2,1,0:T(8,128)(2,1)}, bf16[4,32,128]{2,1,0:T(8,128)(2,1)S(1)}, u32[]{:S(2)}, u32[]{:S(2)}) collective-permute-start(bf16[4,32,128]{2,1,0:T(8,128)(2,1)} %get-tuple-element.32), channel_id=1, source_target_pairs={{0,15},{1,0},{2,1},{3,2},{4,3},{5,4},{6,5},{7,6},{8,7},{9,8},{10,9... | collective-permute-start | bytes 98312 | tf_op jit(solution)/shard_map/ppermute | solution.py:513
  105.8 5.3 %collective-permute-start.9 = (bf16[4,32,128]{2,1,0:T(8,128)(2,1)}, bf16[4,32,128]{2,1,0:T(8,128)(2,1)S(1)}, u32[]{:S(2)}, u32[]{:S(2)}) collective-permute-start(bf16[4,32,128]{2,1,0:T(8,128)(2,1)} %get-tuple-element.34), channel_id=1, source_target_pairs={{0,31},{1,16},{2,17},{3,18},{4,19},{5,20},{6,21},{7,22},{8,23},{9,... | collective-permute-start | bytes 98312 | tf_op jit(solution)/shard_map/ppermute | solution.py:515
  111.2 1.8 %collective-permute-done.8.peer_left = bf16[4,32,128]{2,1,0:T(8,128)(2,1)S(1)} collective-permute-done((bf16[4,32,128]{2,1,0:T(8,128)(2,1)}, bf16[4,32,128]{2,1,0:T(8,128)(2,1)S(1)}, u32[]{:S(2)}, u32[]{:S(2)}) %collective-permute-start.8) | collective-permute-done | bytes 32800 | tf_op jit(solution)/shard_map/ppermute | solution.py:514
  112.9 0.1 collective-permute-done.9.peer_right
  113.1 0.5 copy-done.11
  113.5 0.1 copy-done.12
  113.7 0.1 copy-done.3
  113.8 2.0 %finish.1 = f32[4,256,128]{2,1,0:T(8,128)} custom-call(f32[4,256,128]{2,1,0:T(8,128)} %get-tuple-element.29.own, bf16[4,256,128]{2,1,0:T(8,128)(2,1)} %copy-done.3, bf16[4,32,128]{2,1,0:T(8,128)(2,1)} %copy-done.9, bf16[4,32,128]{2,1,0:T(8,128)(2,1)} %copy-done.10, bf16[4,32,128]{2,1,0:T(8,128)(2,1)} %copy-done.11, bf16[4,32,128]{2,1,0:T(8,128)(2,1)} %copy-done.12), custom_call_target="tpu_custom_call" | custom-call | tf_op jit(solution)/shard_map/finish/pallas_call | solution.py:517
  (53 shorter events, 0.7 us)
Async XLA Ops:
  0.0 15.6 %copy-start.16 = (s32[4,64]{1,0:T(4,128)S(1)}, s32[4,64]{1,0:T(4,128)}, u32[]{:S(2)}) copy-start(s32[4,64]{1,0:T(4,128)} %param.17) | copy-start | bytes 3076
  0.0 15.6 %copy-start.4 = (bf16[3,3,3,32,32]{4,3,2,1,0:T(8,128)(2,1)S(1)}, bf16[3,3,3,32,32]{4,3,2,1,0:T(8,128)(2,1)}, u32[]{:S(2)}) copy-start(bf16[3,3,3,32,32]{4,3,2,1,0:T(8,128)(2,1)} %param.12) | copy-start | bytes 165892
  0.0 15.7 %copy-start.5 = (bf16[3,3,3,32,32]{4,3,2,1,0:T(8,128)(2,1)S(1)}, bf16[3,3,3,32,32]{4,3,2,1,0:T(8,128)(2,1)}, u32[]{:S(2)}) copy-start(bf16[3,3,3,32,32]{4,3,2,1,0:T(8,128)(2,1)} %param.13) | copy-start | bytes 165892
  2.8 86.0 %collective-permute-start.3 = (bf16[2,4,256]{2,1,0:T(4,128)(2,1)}, bf16[2,4,256]{2,1,0:T(4,128)(2,1)S(1)}, u32[]{:S(2)}, u32[]{:S(2)}) collective-permute-start(bf16[2,4,256]{2,1,0:T(4,128)(2,1)} %get-tuple-element.23), channel_id=1, source_target_pairs={{0,17},{1,18},{2,19},{3,20},{4,21},{5,22},{6,23},{7,24},{8,25},{9,... | collective-permute-start | bytes 12296 | tf_op jit(solution)/shard_map/ppermute | solution.py:483
  5.2 83.6 %collective-permute-start.4 = (bf16[2,4,256]{2,1,0:T(4,128)(2,1)}, bf16[2,4,256]{2,1,0:T(4,128)(2,1)S(1)}, u32[]{:S(2)}, u32[]{:S(2)}) collective-permute-start(bf16[2,4,256]{2,1,0:T(4,128)(2,1)} %get-tuple-element.24), channel_id=1, source_target_pairs={{0,31},{1,16},{2,17},{3,18},{4,19},{5,20},{6,21},{7,22},{8,23},{9,... | collective-permute-start | bytes 12296 | tf_op jit(solution)/shard_map/ppermute | solution.py:484
  9.2 10.1 %collective-permute-start = (bf16[64,4,256]{2,1,0:T(4,128)(2,1)}, bf16[64,4,256]{2,1,0:T(4,128)(2,1)S(1)}, u32[]{:S(2)}, u32[]{:S(2)}) collective-permute-start(bf16[64,4,256]{2,1,0:T(4,128)(2,1)} %get-tuple-element.20), channel_id=1, source_target_pairs={{0,1},{1,2},{2,3},{3,4},{4,5},{5,6},{6,7},{7,8},{8,9},{9,10},{10,1... | collective-permute-start | bytes 393224 | tf_op jit(solution)/shard_map/ppermute | solution.py:479
  9.2 10.1 %collective-permute-start.1 = (bf16[64,4,256]{2,1,0:T(4,128)(2,1)}, bf16[64,4,256]{2,1,0:T(4,128)(2,1)S(1)}, u32[]{:S(2)}, u32[]{:S(2)}) collective-permute-start(bf16[64,4,256]{2,1,0:T(4,128)(2,1)} %get-tuple-element.21), channel_id=1, source_target_pairs={{0,15},{1,0},{2,1},{3,2},{4,3},{5,4},{6,5},{7,6},{8,7},{9,8},{10,9... | collective-permute-start | bytes 393224 | tf_op jit(solution)/shard_map/ppermute | solution.py:480
  13.7 75.1 %collective-permute-start.2 = (bf16[3,256,256]{2,1,0:T(8,128)(2,1)}, bf16[3,256,256]{2,1,0:T(8,128)(2,1)S(1)}, u32[]{:S(2)}, u32[]{:S(2)}) collective-permute-start(bf16[3,256,256]{2,1,0:T(8,128)(2,1)} %get-tuple-element.22), channel_id=1, source_target_pairs={{0,16},{16,0},{1,17},{17,1},{2,18},{18,2},{3,19},{19,3},{4,20},{20... | collective-permute-start | bytes 1179656 | tf_op jit(solution)/shard_map/ppermute | solution.py:482
  16.2 1.0 copy-start.13
  16.3 1.0 copy-start.17
  16.4 1.5 %copy-start.8 = (f32[4,64,8,8]{1,3,2,0:T(8,128)S(1)}, f32[4,64,8,8]{1,3,2,0:T(8,128)}, u32[]{:S(2)}) copy-start(f32[4,64,8,8]{1,3,2,0:T(8,128)} %param.14) | copy-start | bytes 196612
  16.6 2.7 %copy-start = (bf16[9,8,32,256]{3,2,1,0:T(8,128)(2,1)}, bf16[9,8,32,256]{3,2,1,0:T(8,128)(2,1)S(1)}, u32[]{:S(2)}) copy-start(bf16[9,8,32,256]{3,2,1,0:T(8,128)(2,1)S(1)} %fusion.15) | copy-start | bytes 3538948
  19.3 1.0 copy-start.1
  19.3 1.1 copy-start.6
  19.3 1.1 copy-start.7
  88.8 0.6 copy-start.14
  88.8 0.6 copy-start.15
  88.8 0.8 copy-start.2
  101.2 11.9 %collective-permute-start.5 = (bf16[4,256,128]{2,1,0:T(8,128)(2,1)}, bf16[4,256,128]{2,1,0:T(8,128)(2,1)S(1)}, u32[]{:S(2)}, u32[]{:S(2)}) collective-permute-start(bf16[4,256,128]{2,1,0:T(8,128)(2,1)} %get-tuple-element.30), channel_id=1, source_target_pairs={{0,16},{16,0},{1,17},{17,1},{2,18},{18,2},{3,19},{19,3},{4,20},{20... | collective-permute-start | bytes 786440 | tf_op jit(solution)/shard_map/ppermute | solution.py:511
  101.3 9.8 %collective-permute-start.6 = (bf16[4,32,128]{2,1,0:T(8,128)(2,1)}, bf16[4,32,128]{2,1,0:T(8,128)(2,1)S(1)}, u32[]{:S(2)}, u32[]{:S(2)}) collective-permute-start(bf16[4,32,128]{2,1,0:T(8,128)(2,1)} %get-tuple-element.31), channel_id=1, source_target_pairs={{0,1},{1,2},{2,3},{3,4},{4,5},{5,6},{6,7},{7,8},{8,9},{9,10},{10,1... | collective-permute-start | bytes 98312 | tf_op jit(solution)/shard_map/ppermute | solution.py:512
  101.4 9.8 %collective-permute-start.7 = (bf16[4,32,128]{2,1,0:T(8,128)(2,1)}, bf16[4,32,128]{2,1,0:T(8,128)(2,1)S(1)}, u32[]{:S(2)}, u32[]{:S(2)}) collective-permute-start(bf16[4,32,128]{2,1,0:T(8,128)(2,1)} %get-tuple-element.32), channel_id=1, source_target_pairs={{0,15},{1,0},{2,1},{3,2},{4,3},{5,4},{6,5},{7,6},{8,7},{9,8},{10,9... | collective-permute-start | bytes 98312 | tf_op jit(solution)/shard_map/ppermute | solution.py:513
  105.8 7.1 %collective-permute-start.8 = (bf16[4,32,128]{2,1,0:T(8,128)(2,1)}, bf16[4,32,128]{2,1,0:T(8,128)(2,1)S(1)}, u32[]{:S(2)}, u32[]{:S(2)}) collective-permute-start(bf16[4,32,128]{2,1,0:T(8,128)(2,1)} %get-tuple-element.33), channel_id=1, source_target_pairs={{0,17},{1,18},{2,19},{3,20},{4,21},{5,22},{6,23},{7,24},{8,25},{9,... | collective-permute-start | bytes 98312 | tf_op jit(solution)/shard_map/ppermute | solution.py:514
  105.8 7.3 %collective-permute-start.9 = (bf16[4,32,128]{2,1,0:T(8,128)(2,1)}, bf16[4,32,128]{2,1,0:T(8,128)(2,1)S(1)}, u32[]{:S(2)}, u32[]{:S(2)}) collective-permute-start(bf16[4,32,128]{2,1,0:T(8,128)(2,1)} %get-tuple-element.34), channel_id=1, source_target_pairs={{0,31},{1,16},{2,17},{3,18},{4,19},{5,20},{6,21},{7,22},{8,23},{9,... | collective-permute-start | bytes 98312 | tf_op jit(solution)/shard_map/ppermute | solution.py:515
  111.1 1.9 %copy-start.9 = (bf16[4,32,128]{2,1,0:T(8,128)(2,1)}, bf16[4,32,128]{2,1,0:T(8,128)(2,1)S(1)}, u32[]{:S(2)}) copy-start(bf16[4,32,128]{2,1,0:T(8,128)(2,1)S(1)} %collective-permute-done.6.own_left) | copy-start | bytes 98308
  111.1 1.9 %copy-start.10 = (bf16[4,32,128]{2,1,0:T(8,128)(2,1)}, bf16[4,32,128]{2,1,0:T(8,128)(2,1)S(1)}, u32[]{:S(2)}) copy-start(bf16[4,32,128]{2,1,0:T(8,128)(2,1)S(1)} %collective-permute-done.7.own_right) | copy-start | bytes 98308
  112.9 0.6 copy-start.11
  113.0 0.6 copy-start.12
  113.1 0.7 copy-start.3

commit v3 on v2

v3 whole, which is shorter than its diff:
```python
import functools
from types import SimpleNamespace

import jax
import jax.numpy as jnp
from jax import lax
from jax.experimental import pallas as pl
from jax.experimental.pallas import tpu as pltpu
from jax.sharding import PartitionSpec as P

TAPS = 8
SHIFT = 24
HALO = 4
LEAD = 2
LEFT = 40
RIGHT = 24
GROUP = 4
VBLOCK = 64
WINDOW = VBLOCK + LEFT + RIGHT
SLOT = 16
UNROLL = 1
BF16 = jnp.bfloat16
F32 = jnp.float32


def edge_kernel(
    side, cot_right, second_right, first_right, cot_rim, second_rim, first_rim, right, rim, corner
):
    spheres = cot_right.shape[0]
    gate = lambda cot, saved: jnp.where(saved > 0, cot, jnp.zeros_like(cot))
    top = side[0]
    for index in range(2):
        place = top + (1 - 2 * top) * index
        rim[index] = gate(cot_rim[place], second_rim[place])
    rim[2] = first_rim[0]
    last = slice(8 - HALO, 8)
    right[:, 0:HALO] = gate(cot_right[:, last], second_right[:, last])
    right[:, HALO : 2 * HALO] = first_right[:, last]
    for index in range(2):
        corner[index] = right[top * (spheres - 1) + (1 - 2 * top) * index]


def edges(side, cot, second, first):
    spheres, columns, merged = cot.shape
    pairs = spheres // 2
    high = pl.BlockSpec((spheres, 8, merged), lambda g, s: (0, columns // 8 - 1, 0))
    pair = pl.BlockSpec((2, columns, merged), lambda g, s: (s[0] * (pairs - 1), 0, 0))
    one = pl.BlockSpec((1, columns, merged), lambda g, s: (s[0] * (spheres - 1), 0, 0))
    shapes = ((spheres, 2 * HALO, merged), (3, columns, merged), (2, 2 * HALO, merged))
    return pl.pallas_call(
        edge_kernel,
        grid_spec=pltpu.PrefetchScalarGridSpec(
            num_scalar_prefetch=1,
            grid=(1,),
            in_specs=[high, high, high, pair, pair, one],
            out_specs=[pl.BlockSpec(s, lambda g, s: (0, 0, 0)) for s in shapes],
        ),
        out_shape=[jax.ShapeDtypeStruct(s, BF16) for s in shapes],
        name="edges",
    )(side, cot, second, first, cot, second, first)


def block_start(flip, sphere, count, spheres):
    sphere = jnp.minimum(sphere, spheres - count)
    return sphere + flip * (spheres - count - 2 * sphere)


def sweep_kernel(names, row_count, paired, *refs):
    ref = SimpleNamespace(**dict(zip(names, refs)))
    flip = ref.info[0]
    step = pl.program_id(0)
    last = step == pl.num_programs(0) - 1
    spheres, _, merged = ref.from_left.shape
    taps_one, taps_two = ref.taps_one, ref.taps_two
    columns = taps_two.shape[1]
    volume, mixed, total = ref.volume, ref.mixed, ref.total
    cameras = total.shape[0]
    channels = merged // row_count
    wide = columns + 16
    blocks = columns // VBLOCK
    actual = lambda v: flip * (spheres - 1) + (1 - 2 * flip) * v
    inner = lambda i: flip + (1 - 2 * flip) * i
    mixer_at = lambda mixers, depth: mixers[depth]

    def store_taps(source, target, slot, first_row, rows):
        for tap in range(3):
            target[slot, :, tap * merged : (tap + 1) * merged] = source[
                first_row - tap : first_row - tap + rows
            ].astype(BF16)

    def gate_second(grad, side, index, slot):
        padded = ref.padded_one.at[index]
        padded[16 : 16 + columns] = grad.astype(F32)
        padded[16 - HALO : 16] = side[0:HALO].astype(F32)
        store_taps(padded, taps_one, slot, 9, wide)

    def masked(cot, saved):
        return jnp.where(saved > 0, cot, jnp.zeros_like(cot))

    def gated(v, first_sphere):
        place = inside(v, first_sphere, ref.cot.shape[0])
        return masked(ref.cot[place], ref.second[place])

    def inside(v, first_sphere, count):
        start = block_start(flip, first_sphere, count, spheres)
        return actual(jnp.minimum(v, spheres - 1)) - start

    def side_of(v):
        return ref.from_left[actual(jnp.minimum(v, spheres - 1))]

    def conv(source, mixers, slot):
        value = None
        for depth in (2, 1, 0):
            lhs = jnp.concatenate(
                [source[slot + 2 - depth], source[slot + 3 - depth]], axis=0
            )
            part = jnp.dot(lhs, mixer_at(mixers, depth), preferred_element_type=F32)
            value = part if value is None else value + part
        rows = source.shape[1]
        return value[:rows], value[rows:]

    def gate_first(hidden, saved, side, index, slot):
        low = side.astype(F32)
        keep = jnp.concatenate([low, saved.astype(F32), low], axis=0) > 0
        ref.padded_two[index] = jnp.where(keep, hidden, 0.0)
        store_taps(ref.padded_two.at[index], taps_two, slot, 9 - LEAD, columns)

    lane = lax.broadcasted_iota(jnp.int32, (channels, merged), 1)
    sub = lax.broadcasted_iota(jnp.int32, (channels, merged), 0)
    diagonal = lax.rem(lane, channels) == sub
    table_lanes = cameras * row_count * row_count
    owner = lax.broadcasted_iota(
        jnp.int32, (cameras * row_count, table_lanes), 1
    ) // row_count == lax.broadcasted_iota(jnp.int32, (cameras * row_count, table_lanes), 0)

    def spread_rows(group):
        rows = [
            jnp.where(owner, ref.row_table[actual(group * GROUP + sphere)], 0.0)
            for sphere in range(GROUP)
        ]
        return jnp.dot(
            jnp.concatenate(rows, axis=0).astype(BF16),
            ref.expand[...],
            preferred_element_type=F32,
        )

    def mix_rows(spread, earlier):
        for camera in range(cameras):
            for sphere in range(GROUP):
                start = (sphere * cameras + camera) * row_count
                weights = jnp.concatenate(
                    [
                        jnp.where(diagonal, spread[start + r : start + r + 1], 0.0)
                        for r in range(row_count)
                    ],
                    axis=0,
                ).astype(BF16)
                value = jnp.dot(
                    volume[earlier + sphere], weights, preferred_element_type=F32
                ).astype(BF16)
                for block in range(blocks):
                    mixed[camera, block, sphere * VBLOCK : (sphere + 1) * VBLOCK] = value[
                        block * VBLOCK : (block + 1) * VBLOCK
                    ]

    width = GROUP * VBLOCK
    distance = (
        lax.rem(lax.broadcasted_iota(jnp.int32, (WINDOW, width), 1), VBLOCK)
        - lax.broadcasted_iota(jnp.int32, (WINDOW, width), 0)
        + (LEFT - LEAD)
    ).astype(F32)

    def tap_rows(group):
        quarter = lax.broadcasted_iota(jnp.int32, (spheres, width), 1) // VBLOCK
        chosen = lax.broadcasted_iota(jnp.int32, (spheres, width), 0) == actual(
            group * GROUP + quarter
        )
        return jnp.dot(
            ref.tap_table[...], chosen.astype(BF16), preferred_element_type=F32
        )

    def warp_columns(rows_all, first, last):
        for camera in range(first, last):
            rows = rows_all[camera * SLOT : (camera + 1) * SLOT]
            tap_of = distance - rows[TAPS : TAPS + 1]
            matrix = jnp.zeros((WINDOW, width), F32)
            for tap in range(TAPS):
                matrix = jnp.where(tap_of == float(tap), rows[tap : tap + 1], matrix)
            matrix = matrix.astype(BF16)
            for block in range(blocks):
                place = slice(block * VBLOCK, block * VBLOCK + WINDOW)
                total[camera, place] = total[camera, place] + jnp.dot(
                    matrix, mixed[camera, block], preferred_element_type=F32
                )

    @pl.when(step == 0)
    def _():
        from_table = lax.broadcasted_iota(jnp.int32, (table_lanes, merged), 0)
        to_lane = lax.broadcasted_iota(jnp.int32, (table_lanes, merged), 1)
        ref.expand[...] = jnp.where(
            lax.rem(from_table, row_count) == to_lane // channels, 1.0, 0.0
        ).astype(BF16)
        total[...] = jnp.zeros_like(total)
        volume[...] = jnp.zeros_like(volume)
        ref.spread[...] = jnp.zeros_like(ref.spread)
        ref.tap_rows[...] = jnp.zeros_like(ref.tap_rows)
        if paired:
            taps_one[2] = jnp.zeros_like(taps_one[2])
            taps_one[3] = jnp.zeros_like(taps_one[3])
        else:
            for index in range(2):
                gate_second(ref.low_rim[1 - index], ref.low_corner[1 - index], index, 2 + index)
        for index in range(2):
            place = inner(index)
            grad = masked(ref.cot_zero[place], ref.second_zero[place])
            gate_second(grad, side_of(index), 2 + index, index)
        order = (2, 3, 0, 1)
        for index in range(2):
            if index == 0 and paired:
                taps_two[0] = jnp.zeros_like(taps_two[0])
                continue
            hidden = jnp.zeros((wide, merged), F32)
            for depth in range(3):
                hidden = hidden + jnp.dot(
                    taps_one[order[index + 2 - depth]],
                    mixer_at(ref.mixer_second, depth),
                    preferred_element_type=F32,
                )
            if index == 0:
                gate_first(hidden, ref.low_rim[2], ref.low_corner[0], index, index)
            else:
                gate_first(hidden, ref.first_zero[0], side_of(0), index, index)

    first_sphere = step * (UNROLL * GROUP)
    for part in range(UNROLL):
        base = first_sphere + part * GROUP
        slot = part * GROUP
        final = last if part == UNROLL - 1 else None
        earlier = ((part - 1) % UNROLL) * GROUP
        for index in range(2):
            sphere = base + 2 + index
            gate_second(
                gated(sphere, first_sphere + 2), side_of(sphere), slot + index, slot + 2 + index
            )
        pair = conv(taps_one, ref.mixer_second, slot)
        for index in range(2):
            sphere = base + 1 + index
            saved = ref.first[inside(sphere, first_sphere + 1, ref.first.shape[0])]
            gate_first(pair[index], saved, side_of(sphere), slot + index, slot + 2 + index)
        for index in range(2):
            sphere = base + 4 + index
            grad, side = gated(sphere, first_sphere + 2), side_of(sphere)
            if final is not None:
                grad = jnp.where(final, ref.high_rim[index], grad)
                side = jnp.where(final, ref.high_corner[index], side)
            gate_second(grad, side, slot + 2 + index, slot + 4 + index)
        mix_rows(ref.spread, earlier)
        pair = conv(taps_one, ref.mixer_second, slot + 2)
        for index in range(2):
            sphere = base + 3 + index
            saved = ref.first[inside(sphere, first_sphere + 1, ref.first.shape[0])]
            side = side_of(sphere)
            if final is not None and index == 1:
                saved = jnp.where(final, ref.high_rim[2], saved)
                side = jnp.where(final, ref.high_corner[0], side)
            gate_first(pair[index], saved, side, slot + 2 + index, slot + 4 + index)
        for start in range(0, GROUP, 2):
            pair = conv(taps_two, ref.mixer_first, slot + start)
            for index in range(2):
                volume[slot + start + index] = pair[index].astype(BF16)
            warp_columns(ref.tap_rows, start * cameras // GROUP, (start + 2) * cameras // GROUP)
        ref.spread[...] = spread_rows(step * UNROLL + part)
        ref.tap_rows[...] = tap_rows(step * UNROLL + part)
    for slot in range(2):
        taps_one[slot] = taps_one[slot + UNROLL * GROUP]
        taps_two[slot] = taps_two[slot + UNROLL * GROUP]

    def joined(row):
        return jnp.concatenate(
            [
                total[camera, :, row * channels : (row + 1) * channels]
                for camera in range(cameras)
            ],
            axis=1,
        )

    @pl.when(last)
    def _():
        mix_rows(ref.spread, (UNROLL - 1) * GROUP)
        warp_columns(ref.tap_rows, 0, cameras)
        if not paired:
            for row in range(row_count):
                ref.whole[row] = joined(row)
            return
        half = row_count // 2
        own_high = ref.info[1] > 0
        for row in range(half):
            low, high = joined(row), joined(row + half)
            for mine, main, left, right in (
                (True, ref.own, ref.own_left, ref.own_right),
                (False, ref.peer, ref.peer_left, ref.peer_right),
            ):
                value = jnp.where(own_high, high, low) if mine else jnp.where(own_high, low, high)
                main[row] = value[LEFT : LEFT + columns].astype(main.dtype)
                left[row] = value[:LEFT].astype(BF16)
                right[row] = value[LEFT + columns :].astype(BF16)


def sweep(info, volumes, tables, row_count, cameras, paired):
    cot, second, first = volumes
    spheres, columns, merged = cot.shape
    groups = spheres // GROUP
    wide = columns + 16
    extended = columns + LEFT + RIGHT
    channels = merged // row_count
    half, lanes = row_count // 2, cameras * channels
    once = pl.Buffered(buffer_count=1)

    def whole(shape):
        zeros = (0,) * len(shape)
        return pl.BlockSpec(shape, lambda g, s: zeros, pipeline_mode=once)

    def spheres_from(ahead, count, **more):
        def index_map(g, s):
            return block_start(s[0], ahead(g), count, spheres), 0, 0

        shape = (pl.Element(count), pl.Element(columns), pl.Element(merged))
        return pl.BlockSpec(shape, index_map, **more)

    block = UNROLL * GROUP
    inputs = {name: (array, whole(array.shape)) for name, array in tables.items()}
    inputs.update(
        cot=(cot, spheres_from(lambda g: block * g + 2, block)),
        second=(second, spheres_from(lambda g: block * g + 2, block)),
        first=(first, spheres_from(lambda g: block * g + 1, block)),
        cot_zero=(cot, spheres_from(lambda g: 0, 2, pipeline_mode=once)),
        second_zero=(second, spheres_from(lambda g: 0, 2, pipeline_mode=once)),
        first_zero=(first, spheres_from(lambda g: 0, 1, pipeline_mode=once)),
    )
    if paired:
        outputs = dict(
            own=((half, columns, lanes), F32),
            own_left=((half, LEFT, lanes), BF16),
            own_right=((half, RIGHT, lanes), BF16),
            peer=((half, columns, lanes), BF16),
            peer_left=((half, LEFT, lanes), BF16),
            peer_right=((half, RIGHT, lanes), BF16),
        )
    else:
        outputs = dict(whole=((row_count, extended, lanes), F32))
    scratch = dict(
        taps_one=((block + 2, wide, 3 * merged), BF16),
        taps_two=((block + 2, columns, 3 * merged), BF16),
        padded_one=((block, columns + 32, merged), F32),
        padded_two=((block, wide, merged), F32),
        volume=((block, columns, merged), BF16),
        mixed=((cameras, columns // VBLOCK, GROUP * VBLOCK, merged), BF16),
        total=((cameras, extended, merged), F32),
        expand=((cameras * row_count * row_count, merged), BF16),
        spread=((GROUP * cameras * row_count, merged), F32),
        tap_rows=((cameras * SLOT, GROUP * VBLOCK), F32),
    )
    names = list(dict(info=0)) + list(inputs) + list(outputs) + list(scratch)
    flops = 2 * spheres * columns * merged * merged * (18 + cameras + cameras // 2)
    results = pl.pallas_call(
        functools.partial(sweep_kernel, names, row_count, paired),
        grid_spec=pltpu.PrefetchScalarGridSpec(
            num_scalar_prefetch=1,
            grid=(groups // UNROLL,),
            in_specs=[spec for _, spec in inputs.values()],
            out_specs=[whole(shape) for shape, _ in outputs.values()],
            scratch_shapes=[pltpu.VMEM(shape, kind) for shape, kind in scratch.values()],
        ),
        out_shape=[jax.ShapeDtypeStruct(shape, kind) for shape, kind in outputs.values()],
        compiler_params=pltpu.CompilerParams(
            dimension_semantics=(pltpu.ARBITRARY,), vmem_limit_bytes=56 * 2**20
        ),
        cost_estimate=pl.CostEstimate(
            flops=flops, bytes_accessed=3 * cot.size * 2, transcendentals=0
        ),
        name="sweep",
    )(info, *[array for array, _ in inputs.values()])
    return SimpleNamespace(**dict(zip(outputs, results)))


def finish_kernel(own, peer, own_start, own_end, peer_start, peer_end, out):
    columns = out.shape[1]
    out[...] = own[...] + peer[...].astype(F32)
    start, end = slice(0, RIGHT), slice(columns - LEFT, columns)
    out[:, start] = out[:, start] + (own_start[...].astype(F32) + peer_start[...].astype(F32))
    out[:, end] = out[:, end] + (own_end[...].astype(F32) + peer_end[...].astype(F32))


def row_mixers(kernel, row_count):
    channels = kernel.shape[3]
    strip = jnp.transpose(kernel, (0, 1, 4, 2, 3)).reshape(9, channels, 3 * channels)
    merged = row_count * channels
    strip = jnp.pad(strip, ((0, 0), (0, 0), (merged, merged)))
    rows = [
        lax.slice_in_dim(
            strip, merged - (row - 1) * channels, 2 * merged - (row - 1) * channels, axis=2
        )
        for row in range(row_count)
    ]
    return jnp.stack(rows, axis=1).reshape(3, 3 * merged, merged)


def ring(offset):
    count = lax.axis_size("azim")
    return [(i, (i + offset) % count) for i in range(count)]


def stride(offset):
    count = lax.axis_size("depth")
    if count == 2:
        return [(0, 1), (1, 0)]
    return [(i, i + offset) for i in range(count) if 0 <= i + offset < count]


def joint(depth_pairs, azim_pairs):
    width = lax.axis_size("azim")
    return [
        (d0 * width + a0, d1 * width + a1)
        for d0, d1 in depth_pairs
        for a0, a1 in azim_pairs
    ]


def body(cot, second, first, kernel_first, kernel_second, row_resample, col_taps, band_width, col_offset):
    spheres, columns, merged = cot.shape
    cameras, _, row_count, _ = row_resample.shape
    depth_index = lax.axis_index("depth").astype(jnp.int32)
    paired = lax.axis_size("depth") == 2
    both = ("depth", "azim")
    forward, backward = ring(1), ring(-1)
    tables = {}

    def send(offset, side):
        right, rim, corner = edges(jnp.full((1,), side, jnp.int32), cot, second, first)
        pairs = stride(offset)
        got_rim = lax.ppermute(rim, "depth", pairs)
        return right, got_rim, lax.ppermute(corner, both, joint(pairs, forward))

    if paired:
        right, high_rim, high_corner = send(-1, 1 - depth_index)
        flip = depth_index
    else:
        right, low_rim, low_corner = send(1, 1)
        _, high_rim, high_corner = send(-1, 0)
        tables.update(low_rim=low_rim, low_corner=low_corner)
        flip = jnp.zeros((), jnp.int32)
    info = jnp.stack([flip, depth_index])
    turned = lambda kernel: jnp.where(flip > 0, kernel[::-1], kernel)

    keep = lax.broadcasted_iota(jnp.int32, col_taps.shape, 2) < band_width[:, :, None]
    taps = jnp.where(keep, col_taps, 0.0)
    table = jnp.concatenate([taps, col_offset[:, :, None].astype(F32)], axis=2)
    table = jnp.pad(jnp.transpose(table, (0, 2, 1)), ((0, 0), (0, SLOT - TAPS - 1), (0, 0)))
    tables.update(
        high_rim=high_rim,
        high_corner=high_corner,
        from_left=lax.ppermute(right, "azim", forward),
        mixer_second=row_mixers(turned(kernel_second), row_count),
        mixer_first=row_mixers(turned(kernel_first), row_count),
        row_table=jnp.transpose(row_resample, (1, 0, 2, 3)).reshape(spheres, 1, -1),
        tap_table=table.reshape(cameras * SLOT, spheres).astype(BF16),
    )
    parts = sweep(info, (cot, second, first), tables, row_count, cameras, paired)

    if paired:
        swap = stride(1)
        got = (
            lax.ppermute(parts.peer, "depth", swap),
            lax.ppermute(parts.own_right, "azim", forward),
            lax.ppermute(parts.own_left, "azim", backward),
            lax.ppermute(parts.peer_right, both, joint(swap, forward)),
            lax.ppermute(parts.peer_left, both, joint(swap, backward)),
        )
        return pl.pallas_call(
            finish_kernel,
            out_shape=jax.ShapeDtypeStruct(parts.own.shape, F32),
            name="finish",
        )(parts.own, *got)
    partial = parts.whole
    at_end = lax.ppermute(partial[:, :LEFT], "azim", backward)
    at_start = lax.ppermute(partial[:, columns + LEFT :], "azim", forward)
    inner = partial[:, LEFT : columns + LEFT]
    inner = inner.at[:, columns - LEFT :].add(at_end)
    inner = inner.at[:, :RIGHT].add(at_start)
    return lax.psum_scatter(inner, "depth", scatter_dimension=0, tiled=True)


def solution(mesh):
    placed = (
        P("depth", "azim", None),
        P("depth", "azim", None),
        P("depth", "azim", None),
        P(),
        P(),
        P(None, "depth", None, None),
        P(None, "depth", None),
        P(None, "depth"),
        P(None, "depth"),
    )
    return jax.shard_map(
        body, mesh=mesh, in_specs=placed, out_specs=P("depth", "azim", None), check_vma=False
    )
```

time: 116 us -> 99.5 us (0.86)
  Pallas kernels: 84.7 us -> 71.6 us
  starting transfers between devices: 22.7 us -> 12.3 us
  waiting for transfers between devices: 1.91 us -> 9.87 us
    pallas_call x3 -> x2, Pallas kernels: 82 us -> 69.4 us  [the longest x1 67.4 us: sweep(): pl.pallas_call(functools.partial(sweep_kernel, names, row_count, paired),...]
    ppermute x10 -> x8, starting transfers between devices: 22.7 us -> 12.3 us  [the longest x1 4.06 us: body(): lax.ppermute(parts.own_left, 'azim', backward)]
    ppermute x10 -> x8, waiting for transfers between devices: 1.91 us -> 9.87 us  [the longest x1 4.93 us: body(): lax.ppermute(parts.own_right, 'azim', forward)]
    unnamed x50 -> x46, local copies, waits for them, and re-layouts: 3.69 us -> 2.6 us
  transfers between devices with their start and end apart: 10 -> 8, of which waited for: 2 -> 4; matrix products, arithmetic and copies ran while one was open for 3% -> 4% of each run, Pallas kernels for 59% -> 0%
where the time goes in v3:
time: 99.5 us; the launch traced here: 99.3 us
  Pallas kernels  71.6 us (72%)
  starting transfers between devices  12.3 us (12%)
  waiting for transfers between devices  9.87 us (10%)
  local copies, waits for them, and re-layouts  4.37 us (4%)
    pallas_call x1, Pallas kernels, sweep(): pl.pallas_call(functools.partial(sweep_kernel, names, row_count, paired),...  67.4 us
    ppermute x1, waiting for transfers between devices, body(): lax.ppermute(parts.own_right, 'azim', forward)  4.93 us
    ppermute x1, starting transfers between devices, body(): lax.ppermute(parts.own_left, 'azim', backward)  4.06 us
    ppermute x1, waiting for transfers between devices, send(): return (right, got_rim, lax.ppermute(corner, both, joint(pairs, forward)))  3.08 us
    ppermute x1, starting transfers between devices, send(): got_rim = lax.ppermute(rim, 'depth', pairs)  3 us
    unnamed x46, local copies, waits for them, and re-layouts  2.6 us
    pallas_call x1, Pallas kernels, edges(): pl.pallas_call(edge_kernel, grid_spec=pltpu.PrefetchScalarGridSpec(num_sc...  2.23 us
    pallas_call x1, Pallas kernels, body(): pl.pallas_call(finish_kernel, out_shape=jax.ShapeDtypeStruct(parts.own.sh...  2.02 us
  transfers between devices with their start and end apart: 8, of which 4 were waited for; matrix products, arithmetic and copies ran while one was open for 4% of the time, Pallas kernels for 0%

profile of v3, /device:TPU:0, one launch (start us, length us, event | category | flops | bytes accessed | tf_op | source)
XLA Modules:
  0.0 99.3 jit_solution(15655519750818342140)
XLA Ops:
  0.0 2.2 %edges.1 = (bf16[64,8,256]{2,1,0:T(8,128)(2,1)}, bf16[3,256,256]{2,1,0:T(8,128)(2,1)}, bf16[2,8,256]{2,1,0:T(8,128)(2,1)}) custom-call(s32[1]{0:T(128)} %bitcast.1.side, bf16[64,256,256]{2,1,0:T(8,128)(2,1)} %refs_11_.1, bf16[64,256,256]{2,1,0:T(8,128)(2,1)} %refs_12_.1, bf16[64,256,256]{2,1,0:T(8,128)(2,1)} %refs_13_.1, bf16[64,256,256]{2,1,0:T(8,128)(2,1)} %refs_11_.1, ...), custom_call_target="tpu_custom_call" | custom-call | tf_op jit(solution)/shard_map/edges/pallas_call | solution.py:50
  2.2 3.0 %collective-permute-start = (bf16[3,256,256]{2,1,0:T(8,128)(2,1)}, bf16[3,256,256]{2,1,0:T(8,128)(2,1)S(1)}, u32[]{:S(2)}, u32[]{:S(2)}) collective-permute-start(bf16[3,256,256]{2,1,0:T(8,128)(2,1)} %get-tuple-element.14), channel_id=1, source_target_pairs={{0,16},{16,0},{1,17},{17,1},{2,18},{18,2},{3,19},{19,3},{4,20},{20... | collective-permute-start | bytes 1179656 | tf_op jit(solution)/shard_map/ppermute | solution.py:441
  5.2 1.7 %collective-permute-start.1 = (bf16[2,8,256]{2,1,0:T(8,128)(2,1)}, bf16[2,8,256]{2,1,0:T(8,128)(2,1)S(1)}, u32[]{:S(2)}, u32[]{:S(2)}) collective-permute-start(bf16[2,8,256]{2,1,0:T(8,128)(2,1)} %get-tuple-element.15), channel_id=1, source_target_pairs={{0,17},{1,18},{2,19},{3,20},{4,21},{5,22},{6,23},{7,24},{8,25},{9,... | collective-permute-start | bytes 24584 | tf_op jit(solution)/shard_map/ppermute | solution.py:442
  7.0 0.1 copy.36
  7.2 0.1 fusion.17
  7.3 0.1 fusion.21
  7.4 0.1 fusion.23
  7.5 0.1 fusion.25
  7.7 0.1 fusion.29
  7.8 0.1 fusion.31
  7.9 0.1 copy.28
  8.1 0.1 fusion.1
  8.2 0.1 fusion.5
  8.3 0.1 fusion.7
  8.4 0.1 fusion.9
  8.8 0.1 fusion.15
  8.9 0.7 pad_add_fusion.refs_0_
  9.6 0.7 copy.45.refs_6_
  10.3 0.6 pad.14
  10.9 3.1 %collective-permute-done.1.refs_2_ = bf16[2,8,256]{2,1,0:T(8,128)(2,1)S(1)} collective-permute-done((bf16[2,8,256]{2,1,0:T(8,128)(2,1)}, bf16[2,8,256]{2,1,0:T(8,128)(2,1)S(1)}, u32[]{:S(2)}, u32[]{:S(2)}) %collective-permute-start.1) | collective-permute-done | bytes 8224 | tf_op jit(solution)/shard_map/ppermute | solution.py:442
  14.0 0.6 collective-permute-done.refs_1_
  14.7 0.7 copy-done.13
  15.4 67.4 %sweep.1 = (f32[4,256,128]{2,1,0:T(8,128)}, bf16[4,40,128]{2,1,0:T(8,128)(2,1)}, bf16[4,24,128]{2,1,0:T(8,128)(2,1)}, bf16[4,256,128]{2,1,0:T(8,128)(2,1)}, bf16...) custom-call(s32[2]{0:T(128)} %pad_add_fusion.refs_0_, bf16[3,256,256]{2,1,0:T(8,128)(2,1)} %copy-done.13, ...), custom_call_target="tpu_custom_call" | custom-call | flops 51539607552 | bytes 25165824 | tf_op jit(solution)/shard_map/sweep/pallas_call | solution.py:365
  82.8 1.8 %collective-permute-start.3 = (bf16[4,256,128]{2,1,0:T(8,128)(2,1)}, bf16[4,256,128]{2,1,0:T(8,128)(2,1)S(1)}, u32[]{:S(2)}, u32[]{:S(2)}) collective-permute-start(bf16[4,256,128]{2,1,0:T(8,128)(2,1)} %get-tuple-element.18), channel_id=1, source_target_pairs={{0,16},{16,0},{1,17},{17,1},{2,18},{18,2},{3,19},{19,3},{4,20},{20... | collective-permute-start | bytes 786440 | tf_op jit(solution)/shard_map/ppermute | solution.py:473
  84.6 4.1 %collective-permute-start.5 = (bf16[4,40,128]{2,1,0:T(8,128)(2,1)}, bf16[4,40,128]{2,1,0:T(8,128)(2,1)S(1)}, u32[]{:S(2)}, u32[]{:S(2)}) collective-permute-start(bf16[4,40,128]{2,1,0:T(8,128)(2,1)} %get-tuple-element.20), channel_id=1, source_target_pairs={{0,15},{1,0},{2,1},{3,2},{4,3},{5,4},{6,5},{7,6},{8,7},{9,8},{10,9... | collective-permute-start | bytes 122888 | tf_op jit(solution)/shard_map/ppermute | solution.py:475
  88.6 0.5 collective-permute-start.7
  89.2 0.1 collective-permute-start.4
  89.3 1.1 %collective-permute-start.6 = (bf16[4,24,128]{2,1,0:T(8,128)(2,1)}, bf16[4,24,128]{2,1,0:T(8,128)(2,1)S(1)}, u32[]{:S(2)}, u32[]{:S(2)}) collective-permute-start(bf16[4,24,128]{2,1,0:T(8,128)(2,1)} %get-tuple-element.21), channel_id=1, source_target_pairs={{0,17},{1,18},{2,19},{3,20},{4,21},{5,22},{6,23},{7,24},{8,25},{9,... | collective-permute-start | bytes 73736 | tf_op jit(solution)/shard_map/ppermute | solution.py:476
  90.4 4.9 %collective-permute-done.4.own_start = bf16[4,24,128]{2,1,0:T(8,128)(2,1)S(1)} collective-permute-done((bf16[4,24,128]{2,1,0:T(8,128)(2,1)}, bf16[4,24,128]{2,1,0:T(8,128)(2,1)S(1)}, u32[]{:S(2)}, u32[]{:S(2)}) %collective-permute-start.4) | collective-permute-done | bytes 24608 | tf_op jit(solution)/shard_map/ppermute | solution.py:474
  95.3 1.2 %collective-permute-done.6.peer_start = bf16[4,24,128]{2,1,0:T(8,128)(2,1)S(1)} collective-permute-done((bf16[4,24,128]{2,1,0:T(8,128)(2,1)}, bf16[4,24,128]{2,1,0:T(8,128)(2,1)S(1)}, u32[]{:S(2)}, u32[]{:S(2)}) %collective-permute-start.6) | collective-permute-done | bytes 24608 | tf_op jit(solution)/shard_map/ppermute | solution.py:476
  96.6 0.5 copy-done.7
  97.3 2.0 %finish.1 = f32[4,256,128]{2,1,0:T(8,128)} custom-call(f32[4,256,128]{2,1,0:T(8,128)} %get-tuple-element.17.own, bf16[4,256,128]{2,1,0:T(8,128)(2,1)} %copy-done, bf16[4,24,128]{2,1,0:T(8,128)(2,1)} %copy-done.6, bf16[4,40,128]{2,1,0:T(8,128)(2,1)} %copy-done.4, bf16[4,24,128]{2,1,0:T(8,128)(2,1)} %copy-done.7, bf16[4,40,128]{2,1,0:T(8,128)(2,1)} %copy-done.5), custom_call_target="tpu_custom_call" | custom-call | tf_op jit(solution)/shard_map/finish/pallas_call | solution.py:479
  (45 shorter events, 0.6 us)
Async XLA Ops:
  0.0 7.0 %copy-start.1 = (bf16[3,3,3,32,32]{4,3,2,1,0:T(8,128)(2,1)S(1)}, bf16[3,3,3,32,32]{4,3,2,1,0:T(8,128)(2,1)}, u32[]{:S(2)}) copy-start(bf16[3,3,3,32,32]{4,3,2,1,0:T(8,128)(2,1)} %param.12) | copy-start | bytes 165892
  0.0 7.0 %copy-start.2 = (bf16[3,3,3,32,32]{4,3,2,1,0:T(8,128)(2,1)S(1)}, bf16[3,3,3,32,32]{4,3,2,1,0:T(8,128)(2,1)}, u32[]{:S(2)}) copy-start(bf16[3,3,3,32,32]{4,3,2,1,0:T(8,128)(2,1)} %param.13) | copy-start | bytes 165892
  2.2 12.4 %collective-permute-start = (bf16[3,256,256]{2,1,0:T(8,128)(2,1)}, bf16[3,256,256]{2,1,0:T(8,128)(2,1)S(1)}, u32[]{:S(2)}, u32[]{:S(2)}) collective-permute-start(bf16[3,256,256]{2,1,0:T(8,128)(2,1)} %get-tuple-element.14), channel_id=1, source_target_pairs={{0,16},{16,0},{1,17},{17,1},{2,18},{18,2},{3,19},{19,3},{4,20},{20... | collective-permute-start | bytes 1179656 | tf_op jit(solution)/shard_map/ppermute | solution.py:441
  5.2 8.8 %collective-permute-start.2 = (bf16[64,8,256]{2,1,0:T(8,128)(2,1)}, bf16[64,8,256]{2,1,0:T(8,128)(2,1)S(1)}, u32[]{:S(2)}, u32[]{:S(2)}) collective-permute-start(bf16[64,8,256]{2,1,0:T(8,128)(2,1)} %get-tuple-element.16), channel_id=1, source_target_pairs={{0,1},{1,2},{2,3},{3,4},{4,5},{5,6},{6,7},{7,8},{8,9},{9,10},{10,1... | collective-permute-start | bytes 786440 | tf_op jit(solution)/shard_map/ppermute | solution.py:462
  5.2 8.8 %collective-permute-start.1 = (bf16[2,8,256]{2,1,0:T(8,128)(2,1)}, bf16[2,8,256]{2,1,0:T(8,128)(2,1)S(1)}, u32[]{:S(2)}, u32[]{:S(2)}) collective-permute-start(bf16[2,8,256]{2,1,0:T(8,128)(2,1)} %get-tuple-element.15), channel_id=1, source_target_pairs={{0,17},{1,18},{2,19},{3,20},{4,21},{5,22},{6,23},{7,24},{8,25},{9,... | collective-permute-start | bytes 24584 | tf_op jit(solution)/shard_map/ppermute | solution.py:442
  7.7 0.9 copy-start.11
  7.7 0.9 copy-start.10
  7.7 0.9 copy-start.12
  7.8 1.8 %copy-start.3 = (f32[4,64,8,8]{1,3,2,0:T(8,128)S(1)}, f32[4,64,8,8]{1,3,2,0:T(8,128)}, u32[]{:S(2)}) copy-start(f32[4,64,8,8]{1,3,2,0:T(8,128)} %param.14) | copy-start | bytes 196612
  7.9 3.0 %copy-start.8 = (bf16[9,8,32,256]{3,2,1,0:T(8,128)(2,1)}, bf16[9,8,32,256]{3,2,1,0:T(8,128)(2,1)S(1)}, u32[]{:S(2)}) copy-start(bf16[9,8,32,256]{3,2,1,0:T(8,128)(2,1)S(1)} %fusion.31) | copy-start | bytes 3538948
  8.9 5.8 %copy-start.9 = (bf16[9,8,32,256]{3,2,1,0:T(8,128)(2,1)}, bf16[9,8,32,256]{3,2,1,0:T(8,128)(2,1)S(1)}, u32[]{:S(2)}) copy-start(bf16[9,8,32,256]{3,2,1,0:T(8,128)(2,1)S(1)} %fusion.15) | copy-start | bytes 3538948
  14.0 0.6 copy-start.15
  14.0 0.7 copy-start.14
  14.6 0.7 copy-start.13
  82.8 13.8 %collective-permute-start.3 = (bf16[4,256,128]{2,1,0:T(8,128)(2,1)}, bf16[4,256,128]{2,1,0:T(8,128)(2,1)S(1)}, u32[]{:S(2)}, u32[]{:S(2)}) collective-permute-start(bf16[4,256,128]{2,1,0:T(8,128)(2,1)} %get-tuple-element.18), channel_id=1, source_target_pairs={{0,16},{16,0},{1,17},{17,1},{2,18},{18,2},{3,19},{19,3},{4,20},{20... | collective-permute-start | bytes 786440 | tf_op jit(solution)/shard_map/ppermute | solution.py:473
  84.6 12.0 %collective-permute-start.5 = (bf16[4,40,128]{2,1,0:T(8,128)(2,1)}, bf16[4,40,128]{2,1,0:T(8,128)(2,1)S(1)}, u32[]{:S(2)}, u32[]{:S(2)}) collective-permute-start(bf16[4,40,128]{2,1,0:T(8,128)(2,1)} %get-tuple-element.20), channel_id=1, source_target_pairs={{0,15},{1,0},{2,1},{3,2},{4,3},{5,4},{6,5},{7,6},{8,7},{9,8},{10,9... | collective-permute-start | bytes 122888 | tf_op jit(solution)/shard_map/ppermute | solution.py:475
  88.6 7.9 %collective-permute-start.7 = (bf16[4,40,128]{2,1,0:T(8,128)(2,1)}, bf16[4,40,128]{2,1,0:T(8,128)(2,1)S(1)}, u32[]{:S(2)}, u32[]{:S(2)}) collective-permute-start(bf16[4,40,128]{2,1,0:T(8,128)(2,1)} %get-tuple-element.22), channel_id=1, source_target_pairs={{0,31},{1,16},{2,17},{3,18},{4,19},{5,20},{6,21},{7,22},{8,23},{9,... | collective-permute-start | bytes 122888 | tf_op jit(solution)/shard_map/ppermute | solution.py:477
  89.2 6.2 %collective-permute-start.4 = (bf16[4,24,128]{2,1,0:T(8,128)(2,1)}, bf16[4,24,128]{2,1,0:T(8,128)(2,1)S(1)}, u32[]{:S(2)}, u32[]{:S(2)}) collective-permute-start(bf16[4,24,128]{2,1,0:T(8,128)(2,1)} %get-tuple-element.19), channel_id=1, source_target_pairs={{0,1},{1,2},{2,3},{3,4},{4,5},{5,6},{6,7},{7,8},{8,9},{9,10},{10,1... | collective-permute-start | bytes 73736 | tf_op jit(solution)/shard_map/ppermute | solution.py:474
  89.3 7.3 %collective-permute-start.6 = (bf16[4,24,128]{2,1,0:T(8,128)(2,1)}, bf16[4,24,128]{2,1,0:T(8,128)(2,1)S(1)}, u32[]{:S(2)}, u32[]{:S(2)}) collective-permute-start(bf16[4,24,128]{2,1,0:T(8,128)(2,1)} %get-tuple-element.21), channel_id=1, source_target_pairs={{0,17},{1,18},{2,19},{3,20},{4,21},{5,22},{6,23},{7,24},{8,25},{9,... | collective-permute-start | bytes 73736 | tf_op jit(solution)/shard_map/ppermute | solution.py:476
  95.3 1.3 %copy-start.6 = (bf16[4,24,128]{2,1,0:T(8,128)(2,1)}, bf16[4,24,128]{2,1,0:T(8,128)(2,1)S(1)}, u32[]{:S(2)}) copy-start(bf16[4,24,128]{2,1,0:T(8,128)(2,1)S(1)} %collective-permute-done.4.own_start) | copy-start | bytes 73732
  96.5 0.6 copy-start.7
  96.5 0.6 copy-start.4
  96.6 0.6 copy-start.5
  96.6 0.7 copy-start

commit v4 on v3

--- a/solution.py
+++ b/solution.py
@@ -84,7 +84,7 @@
 
     def store_taps(source, target, slot, first_row, rows):
         for tap in range(3):
-            target[slot, :, tap * merged : (tap + 1) * merged] = source[
+            target[slot % target.shape[0], :, tap * merged : (tap + 1) * merged] = source[
                 first_row - tap : first_row - tap + rows
             ].astype(BF16)
 
@@ -112,7 +112,7 @@
         value = None
         for depth in (2, 1, 0):
             lhs = jnp.concatenate(
-                [source[slot + 2 - depth], source[slot + 3 - depth]], axis=0
+                [source[(slot + at - depth) % source.shape[0]] for at in (2, 3)], axis=0
             )
             part = jnp.dot(lhs, mixer_at(mixers, depth), preferred_element_type=F32)
             value = part if value is None else value + part
@@ -272,7 +272,6 @@
         ref.spread[...] = spread_rows(step * UNROLL + part)
         ref.tap_rows[...] = tap_rows(step * UNROLL + part)
     for slot in range(2):
-        taps_one[slot] = taps_one[slot + UNROLL * GROUP]
         taps_two[slot] = taps_two[slot + UNROLL * GROUP]
 
     def joined(row):
@@ -349,7 +348,7 @@
     else:
         outputs = dict(whole=((row_count, extended, lanes), F32))
     scratch = dict(
-        taps_one=((block + 2, wide, 3 * merged), BF16),
+        taps_one=((GROUP, wide, 3 * merged), BF16),
         taps_two=((block + 2, columns, 3 * merged), BF16),
         padded_one=((block, columns + 32, merged), F32),
         padded_two=((block, wide, merged), F32),
@@ -373,7 +372,7 @@
         ),
         out_shape=[jax.ShapeDtypeStruct(shape, kind) for shape, kind in outputs.values()],
         compiler_params=pltpu.CompilerParams(
-            dimension_semantics=(pltpu.ARBITRARY,), vmem_limit_bytes=56 * 2**20
+            dimension_semantics=(pltpu.ARBITRARY,), vmem_limit_bytes=30 * 2**20
         ),
         cost_estimate=pl.CostEstimate(
             flops=flops, bytes_accessed=3 * cot.size * 2, transcendentals=0

time: 99.5 us -> 102 us (1.025)
  local copies, waits for them, and re-layouts: 4.37 us -> 9.98 us
  Pallas kernels: 71.6 us -> 66.9 us
  waiting for transfers between devices: 9.87 us -> 11.6 us
    unnamed x46 -> x42, local copies, waits for them, and re-layouts: 2.6 us -> 9.41 us
    pallas_call x1, Pallas kernels: 67.4 us -> 62.7 us  [sweep(): pl.pallas_call(functools.partial(sweep_kernel, names, row_count, paired),...]
    ppermute x1, waiting for transfers between devices: 3.08 us -> 4.96 us  [send(): return (right, got_rim, lax.ppermute(corner, both, joint(pairs, forward)))]
  transfers between devices with their start and end apart: 8 -> 8, of which waited for: 4 -> 4; matrix products, arithmetic and copies ran while one was open for 4% -> 2% of each run, Pallas kernels for 0% -> 0%
where the time goes in v4:
time: 102 us; the launch traced here: 101 us
  Pallas kernels  66.9 us (66%)
  starting transfers between devices  12.3 us (12%)
  waiting for transfers between devices  11.6 us (11%)
  local copies, waits for them, and re-layouts  9.98 us (10%)
    pallas_call x1, Pallas kernels, sweep(): pl.pallas_call(functools.partial(sweep_kernel, names, row_count, paired),...  62.7 us
    unnamed x42, local copies, waits for them, and re-layouts  9.41 us
    ppermute x1, waiting for transfers between devices, send(): return (right, got_rim, lax.ppermute(corner, both, joint(pairs, forward)))  4.96 us
    ppermute x1, waiting for transfers between devices, body(): lax.ppermute(parts.own_right, 'azim', forward)  4.74 us
    ppermute x1, starting transfers between devices, body(): lax.ppermute(parts.own_left, 'azim', backward)  3.98 us
    ppermute x1, starting transfers between devices, send(): got_rim = lax.ppermute(rim, 'depth', pairs)  3 us
    pallas_call x1, Pallas kernels, edges(): pl.pallas_call(edge_kernel, grid_spec=pltpu.PrefetchScalarGridSpec(num_sc...  2.25 us
  transfers between devices with their start and end apart: 8, of which 4 were waited for; matrix products, arithmetic and copies ran while one was open for 2% of the time, Pallas kernels for 0%

profile of v4, /device:TPU:0, one launch (start us, length us, event | category | flops | bytes accessed | tf_op | source)
XLA Modules:
  0.0 101.3 jit_solution(2614661121004046552)
XLA Ops:
  0.0 2.2 %edges.1 = (bf16[64,8,256]{2,1,0:T(8,128)(2,1)}, bf16[3,256,256]{2,1,0:T(8,128)(2,1)}, bf16[2,8,256]{2,1,0:T(8,128)(2,1)}) custom-call(s32[1]{0:T(128)} %bitcast.1.side, bf16[64,256,256]{2,1,0:T(8,128)(2,1)} %refs_11_.1, bf16[64,256,256]{2,1,0:T(8,128)(2,1)} %refs_12_.1, bf16[64,256,256]{2,1,0:T(8,128)(2,1)} %refs_13_.1, bf16[64,256,256]{2,1,0:T(8,128)(2,1)} %refs_11_.1, ...), custom_call_target="tpu_custom_call" | custom-call | tf_op jit(solution)/shard_map/edges/pallas_call | solution.py:50
  2.3 3.0 %collective-permute-start = (bf16[3,256,256]{2,1,0:T(8,128)(2,1)}, bf16[3,256,256]{2,1,0:T(8,128)(2,1)S(1)}, u32[]{:S(2)}, u32[]{:S(2)}) collective-permute-start(bf16[3,256,256]{2,1,0:T(8,128)(2,1)} %get-tuple-element.14), channel_id=1, source_target_pairs={{0,16},{16,0},{1,17},{17,1},{2,18},{18,2},{3,19},{19,3},{4,20},{20... | collective-permute-start | bytes 1179656 | tf_op jit(solution)/shard_map/ppermute | solution.py:440
  5.3 1.7 %collective-permute-start.1 = (bf16[2,8,256]{2,1,0:T(8,128)(2,1)}, bf16[2,8,256]{2,1,0:T(8,128)(2,1)S(1)}, u32[]{:S(2)}, u32[]{:S(2)}) collective-permute-start(bf16[2,8,256]{2,1,0:T(8,128)(2,1)} %get-tuple-element.15), channel_id=1, source_target_pairs={{0,17},{1,18},{2,19},{3,20},{4,21},{5,22},{6,23},{7,24},{8,25},{9,... | collective-permute-start | bytes 24584 | tf_op jit(solution)/shard_map/ppermute | solution.py:441
  7.1 0.1 copy.36
  7.2 0.1 fusion.17
  7.3 0.1 fusion.21
  7.4 0.1 fusion.23
  7.6 0.1 fusion.25
  7.7 0.1 fusion.29
  7.8 0.1 fusion.31
  7.9 0.1 copy.28
  8.1 0.1 fusion.1
  8.2 0.1 fusion.5
  8.3 0.1 fusion.7
  8.5 0.1 fusion.9
  8.7 0.1 fusion.13
  8.8 0.1 fusion.15
  9.1 5.0 %collective-permute-done.1.refs_2_ = bf16[2,8,256]{2,1,0:T(8,128)(2,1)S(1)} collective-permute-done((bf16[2,8,256]{2,1,0:T(8,128)(2,1)}, bf16[2,8,256]{2,1,0:T(8,128)(2,1)S(1)}, u32[]{:S(2)}, u32[]{:S(2)}) %collective-permute-start.1) | collective-permute-done | bytes 8224 | tf_op jit(solution)/shard_map/ppermute | solution.py:441
  14.0 0.6 collective-permute-done.refs_1_
  14.7 3.4 %copy-done = bf16[64,256,256]{2,1,0:T(8,128)(2,1)S(1)} copy-done((bf16[64,256,256]{2,1,0:T(8,128)(2,1)S(1)}, bf16[64,256,256]{2,1,0:T(8,128)(2,1)}, u32[]{:S(2)}) %copy-start) | copy-done | bytes 8388632
  18.0 3.4 %copy-done.1 = bf16[64,256,256]{2,1,0:T(8,128)(2,1)S(1)} copy-done((bf16[64,256,256]{2,1,0:T(8,128)(2,1)S(1)}, bf16[64,256,256]{2,1,0:T(8,128)(2,1)}, u32[]{:S(2)}) %copy-start.1) | copy-done | bytes 8388632
  21.4 62.7 %sweep.1 = (f32[4,256,128]{2,1,0:T(8,128)S(1)}, bf16[4,40,128]{2,1,0:T(8,128)(2,1)S(1)}, bf16[4,24,128]{2,1,0:T(8,128)(2,1)S(1)}, bf16[4,256,128]{2,1,0:T(8,128)...) custom-call(s32[2]{0:T(128)S(1)} %pad_add_fusion.refs_0_, ...), custom_call_target="tpu_custom_call" | custom-call | flops 51539607552 | bytes 25165824 | tf_op jit(solution)/shard_map/sweep/pallas_call | solution.py:364
  84.1 0.8 copy-done.2
  84.9 1.8 %collective-permute-start.3 = (bf16[4,256,128]{2,1,0:T(8,128)(2,1)S(1)}, bf16[4,256,128]{2,1,0:T(8,128)(2,1)S(1)}, u32[]{:S(2)}, u32[]{:S(2)}) collective-permute-start(bf16[4,256,128]{2,1,0:T(8,128)(2,1)S(1)} %get-tuple-element.18), channel_id=1, source_target_pairs={{0,16},{16,0},{1,17},{17,1},{2,18},{18,2},{3,19},{19,3},{4,20},{20... | collective-permute-start | bytes 786440 | tf_op jit(solution)/shard_map/ppermute | solution.py:472
  86.7 4.0 %collective-permute-start.5 = (bf16[4,40,128]{2,1,0:T(8,128)(2,1)S(1)}, bf16[4,40,128]{2,1,0:T(8,128)(2,1)S(1)}, u32[]{:S(2)}, u32[]{:S(2)}) collective-permute-start(bf16[4,40,128]{2,1,0:T(8,128)(2,1)S(1)} %get-tuple-element.20), channel_id=1, source_target_pairs={{0,15},{1,0},{2,1},{3,2},{4,3},{5,4},{6,5},{7,6},{8,7},{9,8},{10,9... | collective-permute-start | bytes 122888 | tf_op jit(solution)/shard_map/ppermute | solution.py:474
  90.7 0.5 collective-permute-start.7
  91.3 1.2 %collective-permute-start.6 = (bf16[4,24,128]{2,1,0:T(8,128)(2,1)S(1)}, bf16[4,24,128]{2,1,0:T(8,128)(2,1)S(1)}, u32[]{:S(2)}, u32[]{:S(2)}) collective-permute-start(bf16[4,24,128]{2,1,0:T(8,128)(2,1)S(1)} %get-tuple-element.21), channel_id=1, source_target_pairs={{0,17},{1,18},{2,19},{3,20},{4,21},{5,22},{6,23},{7,24},{8,25},{9,... | collective-permute-start | bytes 73736 | tf_op jit(solution)/shard_map/ppermute | solution.py:475
  92.5 4.7 %collective-permute-done.4.own_start = bf16[4,24,128]{2,1,0:T(8,128)(2,1)S(1)} collective-permute-done((bf16[4,24,128]{2,1,0:T(8,128)(2,1)S(1)}, bf16[4,24,128]{2,1,0:T(8,128)(2,1)S(1)}, u32[]{:S(2)}, u32[]{:S(2)}) %collective-permute-start.4) | collective-permute-done | bytes 24608 | tf_op jit(solution)/shard_map/ppermute | solution.py:473
  97.2 1.3 %collective-permute-done.6.peer_start = bf16[4,24,128]{2,1,0:T(8,128)(2,1)S(1)} collective-permute-done((bf16[4,24,128]{2,1,0:T(8,128)(2,1)S(1)}, bf16[4,24,128]{2,1,0:T(8,128)(2,1)S(1)}, u32[]{:S(2)}, u32[]{:S(2)}) %collective-permute-start.6) | collective-permute-done | bytes 24608 | tf_op jit(solution)/shard_map/ppermute | solution.py:475
  98.5 0.5 copy-done.10
  99.1 0.1 copy-done.3
  99.2 2.0 %finish.1 = f32[4,256,128]{2,1,0:T(8,128)} custom-call(f32[4,256,128]{2,1,0:T(8,128)} %copy-done.2, bf16[4,256,128]{2,1,0:T(8,128)(2,1)} %copy-done.3, bf16[4,24,128]{2,1,0:T(8,128)(2,1)} %copy-done.9, bf16[4,40,128]{2,1,0:T(8,128)(2,1)} %copy-done.7, bf16[4,24,128]{2,1,0:T(8,128)(2,1)} %copy-done.10, bf16[4,40,128]{2,1,0:T(8,128)(2,1)} %copy-done.8), custom_call_target="tpu_custom_call" | custom-call | tf_op jit(solution)/shard_map/finish/pallas_call | solution.py:478
  (41 shorter events, 0.5 us)
Async XLA Ops:
  0.0 7.0 %copy-start.4 = (bf16[3,3,3,32,32]{4,3,2,1,0:T(8,128)(2,1)S(1)}, bf16[3,3,3,32,32]{4,3,2,1,0:T(8,128)(2,1)}, u32[]{:S(2)}) copy-start(bf16[3,3,3,32,32]{4,3,2,1,0:T(8,128)(2,1)} %param.12) | copy-start | bytes 165892
  0.0 7.0 %copy-start.5 = (bf16[3,3,3,32,32]{4,3,2,1,0:T(8,128)(2,1)S(1)}, bf16[3,3,3,32,32]{4,3,2,1,0:T(8,128)(2,1)}, u32[]{:S(2)}) copy-start(bf16[3,3,3,32,32]{4,3,2,1,0:T(8,128)(2,1)} %param.13) | copy-start | bytes 165892
  2.3 12.4 %collective-permute-start = (bf16[3,256,256]{2,1,0:T(8,128)(2,1)}, bf16[3,256,256]{2,1,0:T(8,128)(2,1)S(1)}, u32[]{:S(2)}, u32[]{:S(2)}) collective-permute-start(bf16[3,256,256]{2,1,0:T(8,128)(2,1)} %get-tuple-element.14), channel_id=1, source_target_pairs={{0,16},{16,0},{1,17},{17,1},{2,18},{18,2},{3,19},{19,3},{4,20},{20... | collective-permute-start | bytes 1179656 | tf_op jit(solution)/shard_map/ppermute | solution.py:440
  5.3 8.8 %collective-permute-start.2 = (bf16[64,8,256]{2,1,0:T(8,128)(2,1)}, bf16[64,8,256]{2,1,0:T(8,128)(2,1)S(1)}, u32[]{:S(2)}, u32[]{:S(2)}) collective-permute-start(bf16[64,8,256]{2,1,0:T(8,128)(2,1)} %get-tuple-element.16), channel_id=1, source_target_pairs={{0,1},{1,2},{2,3},{3,4},{4,5},{5,6},{6,7},{7,8},{8,9},{9,10},{10,1... | collective-permute-start | bytes 786440 | tf_op jit(solution)/shard_map/ppermute | solution.py:461
  5.3 8.8 %collective-permute-start.1 = (bf16[2,8,256]{2,1,0:T(8,128)(2,1)}, bf16[2,8,256]{2,1,0:T(8,128)(2,1)S(1)}, u32[]{:S(2)}, u32[]{:S(2)}) collective-permute-start(bf16[2,8,256]{2,1,0:T(8,128)(2,1)} %get-tuple-element.15), channel_id=1, source_target_pairs={{0,17},{1,18},{2,19},{3,20},{4,21},{5,22},{6,23},{7,24},{8,25},{9,... | collective-permute-start | bytes 24584 | tf_op jit(solution)/shard_map/ppermute | solution.py:441
  7.7 0.9 copy-start.12
  7.7 0.9 copy-start.11
  7.7 0.9 copy-start.13
  7.8 1.1 %copy-start.6 = (f32[4,64,8,8]{1,3,2,0:T(8,128)S(1)}, f32[4,64,8,8]{1,3,2,0:T(8,128)}, u32[]{:S(2)}) copy-start(f32[4,64,8,8]{1,3,2,0:T(8,128)} %param.14) | copy-start | bytes 196612
  14.7 3.4 %copy-start = (bf16[64,256,256]{2,1,0:T(8,128)(2,1)S(1)}, bf16[64,256,256]{2,1,0:T(8,128)(2,1)}, u32[]{:S(2)}) copy-start(bf16[64,256,256]{2,1,0:T(8,128)(2,1)} %refs_11_.1) | copy-start | bytes 25165828
  18.0 3.4 %copy-start.1 = (bf16[64,256,256]{2,1,0:T(8,128)(2,1)S(1)}, bf16[64,256,256]{2,1,0:T(8,128)(2,1)}, u32[]{:S(2)}) copy-start(bf16[64,256,256]{2,1,0:T(8,128)(2,1)} %refs_12_.1) | copy-start | bytes 25165828
  84.1 0.8 copy-start.2
  84.9 13.6 %collective-permute-start.3 = (bf16[4,256,128]{2,1,0:T(8,128)(2,1)S(1)}, bf16[4,256,128]{2,1,0:T(8,128)(2,1)S(1)}, u32[]{:S(2)}, u32[]{:S(2)}) collective-permute-start(bf16[4,256,128]{2,1,0:T(8,128)(2,1)S(1)} %get-tuple-element.18), channel_id=1, source_target_pairs={{0,16},{16,0},{1,17},{17,1},{2,18},{18,2},{3,19},{19,3},{4,20},{20... | collective-permute-start | bytes 786440 | tf_op jit(solution)/shard_map/ppermute | solution.py:472
  86.7 11.8 %collective-permute-start.5 = (bf16[4,40,128]{2,1,0:T(8,128)(2,1)S(1)}, bf16[4,40,128]{2,1,0:T(8,128)(2,1)S(1)}, u32[]{:S(2)}, u32[]{:S(2)}) collective-permute-start(bf16[4,40,128]{2,1,0:T(8,128)(2,1)S(1)} %get-tuple-element.20), channel_id=1, source_target_pairs={{0,15},{1,0},{2,1},{3,2},{4,3},{5,4},{6,5},{7,6},{8,7},{9,8},{10,9... | collective-permute-start | bytes 122888 | tf_op jit(solution)/shard_map/ppermute | solution.py:474
  90.7 7.8 %collective-permute-start.7 = (bf16[4,40,128]{2,1,0:T(8,128)(2,1)S(1)}, bf16[4,40,128]{2,1,0:T(8,128)(2,1)S(1)}, u32[]{:S(2)}, u32[]{:S(2)}) collective-permute-start(bf16[4,40,128]{2,1,0:T(8,128)(2,1)S(1)} %get-tuple-element.22), channel_id=1, source_target_pairs={{0,31},{1,16},{2,17},{3,18},{4,19},{5,20},{6,21},{7,22},{8,23},{9,... | collective-permute-start | bytes 122888 | tf_op jit(solution)/shard_map/ppermute | solution.py:476
  91.3 5.9 %collective-permute-start.4 = (bf16[4,24,128]{2,1,0:T(8,128)(2,1)S(1)}, bf16[4,24,128]{2,1,0:T(8,128)(2,1)S(1)}, u32[]{:S(2)}, u32[]{:S(2)}) collective-permute-start(bf16[4,24,128]{2,1,0:T(8,128)(2,1)S(1)} %get-tuple-element.19), channel_id=1, source_target_pairs={{0,1},{1,2},{2,3},{3,4},{4,5},{5,6},{6,7},{7,8},{8,9},{9,10},{10,1... | collective-permute-start | bytes 73736 | tf_op jit(solution)/shard_map/ppermute | solution.py:473
  91.3 7.2 %collective-permute-start.6 = (bf16[4,24,128]{2,1,0:T(8,128)(2,1)S(1)}, bf16[4,24,128]{2,1,0:T(8,128)(2,1)S(1)}, u32[]{:S(2)}, u32[]{:S(2)}) collective-permute-start(bf16[4,24,128]{2,1,0:T(8,128)(2,1)S(1)} %get-tuple-element.21), channel_id=1, source_target_pairs={{0,17},{1,18},{2,19},{3,20},{4,21},{5,22},{6,23},{7,24},{8,25},{9,... | collective-permute-start | bytes 73736 | tf_op jit(solution)/shard_map/ppermute | solution.py:475
  97.2 1.3 %copy-start.9 = (bf16[4,24,128]{2,1,0:T(8,128)(2,1)}, bf16[4,24,128]{2,1,0:T(8,128)(2,1)S(1)}, u32[]{:S(2)}) copy-start(bf16[4,24,128]{2,1,0:T(8,128)(2,1)S(1)} %collective-permute-done.4.own_start) | copy-start | bytes 73732
  98.5 0.6 copy-start.10
  98.5 0.6 copy-start.7
  98.5 0.6 copy-start.8
  98.5 0.7 copy-start.3

commit v5 on v4

--- a/solution.py
+++ b/solution.py
@@ -94,12 +94,8 @@
         padded[16 - HALO : 16] = side[0:HALO].astype(F32)
         store_taps(padded, taps_one, slot, 9, wide)
 
-    def masked(cot, saved):
-        return jnp.where(saved > 0, cot, jnp.zeros_like(cot))
-
     def gated(v, first_sphere):
-        place = inside(v, first_sphere, ref.cot.shape[0])
-        return masked(ref.cot[place], ref.second[place])
+        return ref.second[inside(v, first_sphere, ref.second.shape[0])]
 
     def inside(v, first_sphere, count):
         start = block_start(flip, first_sphere, count, spheres)
@@ -212,8 +208,7 @@
                 gate_second(ref.low_rim[1 - index], ref.low_corner[1 - index], index, 2 + index)
         for index in range(2):
             place = inner(index)
-            grad = masked(ref.cot_zero[place], ref.second_zero[place])
-            gate_second(grad, side_of(index), 2 + index, index)
+            gate_second(ref.second_zero[place], side_of(index), 2 + index, index)
         order = (2, 3, 0, 1)
         for index in range(2):
             if index == 0 and paired:
@@ -306,8 +301,8 @@
 
 
 def sweep(info, volumes, tables, row_count, cameras, paired):
-    cot, second, first = volumes
-    spheres, columns, merged = cot.shape
+    second, first = volumes
+    spheres, columns, merged = second.shape
     groups = spheres // GROUP
     wide = columns + 16
     extended = columns + LEFT + RIGHT
@@ -329,10 +324,8 @@
     block = UNROLL * GROUP
     inputs = {name: (array, whole(array.shape)) for name, array in tables.items()}
     inputs.update(
-        cot=(cot, spheres_from(lambda g: block * g + 2, block)),
         second=(second, spheres_from(lambda g: block * g + 2, block)),
         first=(first, spheres_from(lambda g: block * g + 1, block)),
-        cot_zero=(cot, spheres_from(lambda g: 0, 2, pipeline_mode=once)),
         second_zero=(second, spheres_from(lambda g: 0, 2, pipeline_mode=once)),
         first_zero=(first, spheres_from(lambda g: 0, 1, pipeline_mode=once)),
     )
@@ -372,10 +365,10 @@
         ),
         out_shape=[jax.ShapeDtypeStruct(shape, kind) for shape, kind in outputs.values()],
         compiler_params=pltpu.CompilerParams(
-            dimension_semantics=(pltpu.ARBITRARY,), vmem_limit_bytes=30 * 2**20
+            dimension_semantics=(pltpu.ARBITRARY,), vmem_limit_bytes=46 * 2**20
         ),
         cost_estimate=pl.CostEstimate(
-            flops=flops, bytes_accessed=3 * cot.size * 2, transcendentals=0
+            flops=flops, bytes_accessed=2 * second.size * 2, transcendentals=0
         ),
         name="sweep",
     )(info, *[array for array, _ in inputs.values()])
@@ -464,7 +457,8 @@
         row_table=jnp.transpose(row_resample, (1, 0, 2, 3)).reshape(spheres, 1, -1),
         tap_table=table.reshape(cameras * SLOT, spheres).astype(BF16),
     )
-    parts = sweep(info, (cot, second, first), tables, row_count, cameras, paired)
+    second_grad = jnp.where(second > 0, cot, jnp.zeros_like(cot))
+    parts = sweep(info, (second_grad, first), tables, row_count, cameras, paired)
 
     if paired:
         swap = stride(1)

time: 102 us -> 99.2 us (0.973)
  other arithmetic: 0.17 us -> 9.14 us
  local copies, waits for them, and re-layouts: 9.98 us -> 3.21 us
  waiting for transfers between devices: 11.6 us -> 6.37 us
  Pallas kernels: 66.9 us -> 69.8 us
  starting transfers between devices: 12.3 us -> 10.1 us
    select_n x0 -> x1, other arithmetic: none -> 8.97 us  [body(): second_grad = jnp.where(second > 0, cot, jnp.zeros_like(cot))]
    unnamed x42 -> x38, local copies, waits for them, and re-layouts: 9.41 us -> 2.64 us
    ppermute x1, waiting for transfers between devices: 4.96 us -> 0.01 us  [send(): return (right, got_rim, lax.ppermute(corner, both, joint(pairs, forward)))]
    pallas_call x1, Pallas kernels: 62.7 us -> 65.6 us  [sweep(): pl.pallas_call(functools.partial(sweep_kernel, names, row_count, paired),...]
    ppermute x1, starting transfers between devices: 3 us -> 0.51 us  [send(): got_rim = lax.ppermute(rim, 'depth', pairs)]
    ppermute x1, starting transfers between devices: 3.98 us -> 2.34 us  [body(): lax.ppermute(parts.own_left, 'azim', backward)]
    ppermute x1, starting transfers between devices: 0.01 us -> 1.6 us  [body(): lax.ppermute(right, 'azim', forward)]
  transfers between devices with their start and end apart: 8 -> 8, of which waited for: 4 -> 2; matrix products, arithmetic and copies ran while one was open for 2% -> 11% of each run, Pallas kernels for 0% -> 0%
where the time goes in v5:
time: 99.2 us; the launch traced here: 99 us
  Pallas kernels  69.8 us (70%)
  starting transfers between devices  10.1 us (10%)
  other arithmetic  9.14 us (9%)
  waiting for transfers between devices  6.37 us (6%)
  local copies, waits for them, and re-layouts  3.21 us (3%)
    pallas_call x1, Pallas kernels, sweep(): pl.pallas_call(functools.partial(sweep_kernel, names, row_count, paired),...  65.6 us
    select_n x1, other arithmetic, body(): second_grad = jnp.where(second > 0, cot, jnp.zeros_like(cot))  8.97 us
    ppermute x1, waiting for transfers between devices, body(): lax.ppermute(parts.own_right, 'azim', forward)  5.01 us
    unnamed x38, local copies, waits for them, and re-layouts  2.64 us
    ppermute x1, starting transfers between devices, send(): return (right, got_rim, lax.ppermute(corner, both, joint(pairs, forward)))  2.43 us
    ppermute x1, starting transfers between devices, body(): lax.ppermute(parts.own_left, 'azim', backward)  2.34 us
    pallas_call x1, Pallas kernels, edges(): pl.pallas_call(edge_kernel, grid_spec=pltpu.PrefetchScalarGridSpec(num_sc...  2.2 us
    pallas_call x1, Pallas kernels, body(): pl.pallas_call(finish_kernel, out_shape=jax.ShapeDtypeStruct(parts.own.sh...  2.02 us
  transfers between devices with their start and end apart: 8, of which 2 were waited for; matrix products, arithmetic and copies ran while one was open for 11% of the time, Pallas kernels for 0%

profile of v5, /device:TPU:0, one launch (start us, length us, event | category | flops | bytes accessed | tf_op | source)
XLA Modules:
  0.0 99.0 jit_solution(4049885460880262452)
XLA Ops:
  0.0 2.2 %edges.1 = (bf16[64,8,256]{2,1,0:T(8,128)(2,1)}, bf16[3,256,256]{2,1,0:T(8,128)(2,1)}, bf16[2,8,256]{2,1,0:T(8,128)(2,1)}) custom-call(s32[1]{0:T(128)} %bitcast.1.side, bf16[64,256,256]{2,1,0:T(8,128)(2,1)} %cot_rim.1, bf16[64,256,256]{2,1,0:T(8,128)(2,1)} %second_rim.1, bf16[64,256,256]{2,1,0:T(8,128)(2,1)} %refs_11_.1, bf16[64,256,256]{2,1,0:T(8,128)(2,1)} %cot_rim.1, ...), custom_call_target="tpu_custom_call" | custom-call | tf_op jit(solution)/shard_map/edges/pallas_call | solution.py:50
  2.2 2.4 %collective-permute-start.1 = (bf16[2,8,256]{2,1,0:T(8,128)(2,1)}, bf16[2,8,256]{2,1,0:T(8,128)(2,1)S(1)}, u32[]{:S(2)}, u32[]{:S(2)}) collective-permute-start(bf16[2,8,256]{2,1,0:T(8,128)(2,1)} %get-tuple-element.15), channel_id=1, source_target_pairs={{0,17},{1,18},{2,19},{3,20},{4,21},{5,22},{6,23},{7,24},{8,25},{9,... | collective-permute-start | bytes 24584 | tf_op jit(solution)/shard_map/ppermute | solution.py:434
  4.6 1.6 %collective-permute-start.2 = (bf16[64,8,256]{2,1,0:T(8,128)(2,1)}, bf16[64,8,256]{2,1,0:T(8,128)(2,1)S(1)}, u32[]{:S(2)}, u32[]{:S(2)}) collective-permute-start(bf16[64,8,256]{2,1,0:T(8,128)(2,1)} %get-tuple-element.16), channel_id=1, source_target_pairs={{0,1},{1,2},{2,3},{3,4},{4,5},{5,6},{6,7},{7,8},{8,9},{9,10},{10,1... | collective-permute-start | bytes 786440 | tf_op jit(solution)/shard_map/ppermute | solution.py:454
  6.2 0.5 collective-permute-start
  6.7 9.0 %compare_select_fusion.refs_8_.refs_10_ = bf16[64,256,256]{2,1,0:T(8,128)(2,1)} fusion(bf16[64,256,256]{2,1,0:T(8,128)(2,1)} %cot_rim.1, bf16[64,256,256]{2,1,0:T(8,128)(2,1)} %second_rim.1), kind=kLoop, calls=%fused_computation | loop fusion | flops 8388608 | bytes 25165824 | tf_op jit(solution)/shard_map/jit(_where)/select_n | solution.py:460
  15.8 0.1 copy.36
  16.0 0.1 copy.28
  16.1 0.1 fusion.1
  16.3 0.1 fusion.5
  16.4 0.1 fusion.7
  16.5 0.1 fusion.9
  16.7 0.1 fusion.13
  16.8 0.1 fusion.15
  16.9 0.1 fusion.17
  17.0 0.1 fusion.21
  17.1 0.1 fusion.23
  17.2 0.1 fusion.25
  17.4 0.1 fusion.29
  17.5 0.1 fusion.31
  17.6 0.1 pad_add_fusion.refs_0_
  17.7 0.1 copy.45.refs_6_
  17.8 65.6 %sweep.1 = (f32[4,256,128]{2,1,0:T(8,128)S(1)}, bf16[4,40,128]{2,1,0:T(8,128)(2,1)S(1)}, bf16[4,24,128]{2,1,0:T(8,128)(2,1)S(1)}, bf16[4,256,128]{2,1,0:T(8,128)...) custom-call(s32[2]{0:T(128)S(1)} %pad_add_fusion.refs_0_, ...), custom_call_target="tpu_custom_call" | custom-call | flops 51539607552 | bytes 16777216 | tf_op jit(solution)/shard_map/sweep/pallas_call | solution.py:357
  83.5 0.8 copy-done
  84.3 1.5 %collective-permute-start.3 = (bf16[4,256,128]{2,1,0:T(8,128)(2,1)S(1)}, bf16[4,256,128]{2,1,0:T(8,128)(2,1)S(1)}, u32[]{:S(2)}, u32[]{:S(2)}) collective-permute-start(bf16[4,256,128]{2,1,0:T(8,128)(2,1)S(1)} %get-tuple-element.18), channel_id=1, source_target_pairs={{0,16},{16,0},{1,17},{17,1},{2,18},{18,2},{3,19},{19,3},{4,20},{20... | collective-permute-start | bytes 786440 | tf_op jit(solution)/shard_map/ppermute | solution.py:466
  85.8 2.3 %collective-permute-start.5 = (bf16[4,40,128]{2,1,0:T(8,128)(2,1)S(1)}, bf16[4,40,128]{2,1,0:T(8,128)(2,1)S(1)}, u32[]{:S(2)}, u32[]{:S(2)}) collective-permute-start(bf16[4,40,128]{2,1,0:T(8,128)(2,1)S(1)} %get-tuple-element.20), channel_id=1, source_target_pairs={{0,15},{1,0},{2,1},{3,2},{4,3},{5,4},{6,5},{7,6},{8,7},{9,8},{10,9... | collective-permute-start | bytes 122888 | tf_op jit(solution)/shard_map/ppermute | solution.py:468
  88.1 0.8 collective-permute-start.7
  88.9 0.9 collective-permute-start.6
  89.9 5.0 %collective-permute-done.4.own_start = bf16[4,24,128]{2,1,0:T(8,128)(2,1)S(1)} collective-permute-done((bf16[4,24,128]{2,1,0:T(8,128)(2,1)S(1)}, bf16[4,24,128]{2,1,0:T(8,128)(2,1)S(1)}, u32[]{:S(2)}, u32[]{:S(2)}) %collective-permute-start.4) | collective-permute-done | bytes 24608 | tf_op jit(solution)/shard_map/ppermute | solution.py:467
  94.9 1.3 %collective-permute-done.6.peer_start = bf16[4,24,128]{2,1,0:T(8,128)(2,1)S(1)} collective-permute-done((bf16[4,24,128]{2,1,0:T(8,128)(2,1)S(1)}, bf16[4,24,128]{2,1,0:T(8,128)(2,1)S(1)}, u32[]{:S(2)}, u32[]{:S(2)}) %collective-permute-start.6) | collective-permute-done | bytes 24608 | tf_op jit(solution)/shard_map/ppermute | solution.py:469
  96.3 0.5 copy-done.8
  96.9 0.1 copy-done.1
  97.0 2.0 %finish.1 = f32[4,256,128]{2,1,0:T(8,128)} custom-call(f32[4,256,128]{2,1,0:T(8,128)} %copy-done, bf16[4,256,128]{2,1,0:T(8,128)(2,1)} %copy-done.1, bf16[4,24,128]{2,1,0:T(8,128)(2,1)} %copy-done.7, bf16[4,40,128]{2,1,0:T(8,128)(2,1)} %copy-done.5, bf16[4,24,128]{2,1,0:T(8,128)(2,1)} %copy-done.8, bf16[4,40,128]{2,1,0:T(8,128)(2,1)} %copy-done.6), custom_call_target="tpu_custom_call" | custom-call | tf_op jit(solution)/shard_map/finish/pallas_call | solution.py:472
  (38 shorter events, 0.3 us)
Async XLA Ops:
  2.2 15.6 %collective-permute-start.1 = (bf16[2,8,256]{2,1,0:T(8,128)(2,1)}, bf16[2,8,256]{2,1,0:T(8,128)(2,1)S(1)}, u32[]{:S(2)}, u32[]{:S(2)}) collective-permute-start(bf16[2,8,256]{2,1,0:T(8,128)(2,1)} %get-tuple-element.15), channel_id=1, source_target_pairs={{0,17},{1,18},{2,19},{3,20},{4,21},{5,22},{6,23},{7,24},{8,25},{9,... | collective-permute-start | bytes 24584 | tf_op jit(solution)/shard_map/ppermute | solution.py:434
  4.6 13.2 %collective-permute-start.2 = (bf16[64,8,256]{2,1,0:T(8,128)(2,1)}, bf16[64,8,256]{2,1,0:T(8,128)(2,1)S(1)}, u32[]{:S(2)}, u32[]{:S(2)}) collective-permute-start(bf16[64,8,256]{2,1,0:T(8,128)(2,1)} %get-tuple-element.16), channel_id=1, source_target_pairs={{0,1},{1,2},{2,3},{3,4},{4,5},{5,6},{6,7},{7,8},{8,9},{9,10},{10,1... | collective-permute-start | bytes 786440 | tf_op jit(solution)/shard_map/ppermute | solution.py:454
  6.2 9.5 %copy-start.10 = (s32[4,64]{1,0:T(4,128)S(1)}, s32[4,64]{1,0:T(4,128)}, u32[]{:S(2)}) copy-start(s32[4,64]{1,0:T(4,128)} %param.17) | copy-start | bytes 3076
  6.2 9.5 %copy-start.2 = (bf16[3,3,3,32,32]{4,3,2,1,0:T(8,128)(2,1)S(1)}, bf16[3,3,3,32,32]{4,3,2,1,0:T(8,128)(2,1)}, u32[]{:S(2)}) copy-start(bf16[3,3,3,32,32]{4,3,2,1,0:T(8,128)(2,1)} %param.12) | copy-start | bytes 165892
  6.2 9.5 %copy-start.3 = (bf16[3,3,3,32,32]{4,3,2,1,0:T(8,128)(2,1)S(1)}, bf16[3,3,3,32,32]{4,3,2,1,0:T(8,128)(2,1)}, u32[]{:S(2)}) copy-start(bf16[3,3,3,32,32]{4,3,2,1,0:T(8,128)(2,1)} %param.13) | copy-start | bytes 165892
  6.2 11.6 %collective-permute-start = (bf16[3,256,256]{2,1,0:T(8,128)(2,1)}, bf16[3,256,256]{2,1,0:T(8,128)(2,1)S(1)}, u32[]{:S(2)}, u32[]{:S(2)}) collective-permute-start(bf16[3,256,256]{2,1,0:T(8,128)(2,1)} %get-tuple-element.14), channel_id=1, source_target_pairs={{0,16},{16,0},{1,17},{17,1},{2,18},{18,2},{3,19},{19,3},{4,20},{20... | collective-permute-start | bytes 1179656 | tf_op jit(solution)/shard_map/ppermute | solution.py:433
  16.4 1.0 %copy-start.9 = (f32[4,64,8]{1,2,0:T(8,128)S(1)}, f32[4,64,8]{1,2,0:T(8,128)}, u32[]{:S(2)}) copy-start(f32[4,64,8]{1,2,0:T(8,128)} %param.15) | copy-start | bytes 24580
  16.4 1.0 %copy-start.11 = (s32[4,64]{1,0:T(4,128)S(1)}, s32[4,64]{1,0:T(4,128)}, u32[]{:S(2)}) copy-start(s32[4,64]{1,0:T(4,128)} %param.16) | copy-start | bytes 3076
  16.7 1.0 %copy-start.4 = (f32[4,64,8,8]{1,3,2,0:T(8,128)S(1)}, f32[4,64,8,8]{1,3,2,0:T(8,128)}, u32[]{:S(2)}) copy-start(f32[4,64,8,8]{1,3,2,0:T(8,128)} %param.14) | copy-start | bytes 196612
  83.5 0.8 copy-start
  84.3 12.0 %collective-permute-start.3 = (bf16[4,256,128]{2,1,0:T(8,128)(2,1)S(1)}, bf16[4,256,128]{2,1,0:T(8,128)(2,1)S(1)}, u32[]{:S(2)}, u32[]{:S(2)}) collective-permute-start(bf16[4,256,128]{2,1,0:T(8,128)(2,1)S(1)} %get-tuple-element.18), channel_id=1, source_target_pairs={{0,16},{16,0},{1,17},{17,1},{2,18},{18,2},{3,19},{19,3},{4,20},{20... | collective-permute-start | bytes 786440 | tf_op jit(solution)/shard_map/ppermute | solution.py:466
  85.8 10.4 %collective-permute-start.5 = (bf16[4,40,128]{2,1,0:T(8,128)(2,1)S(1)}, bf16[4,40,128]{2,1,0:T(8,128)(2,1)S(1)}, u32[]{:S(2)}, u32[]{:S(2)}) collective-permute-start(bf16[4,40,128]{2,1,0:T(8,128)(2,1)S(1)} %get-tuple-element.20), channel_id=1, source_target_pairs={{0,15},{1,0},{2,1},{3,2},{4,3},{5,4},{6,5},{7,6},{8,7},{9,8},{10,9... | collective-permute-start | bytes 122888 | tf_op jit(solution)/shard_map/ppermute | solution.py:468
  88.1 8.1 %collective-permute-start.7 = (bf16[4,40,128]{2,1,0:T(8,128)(2,1)S(1)}, bf16[4,40,128]{2,1,0:T(8,128)(2,1)S(1)}, u32[]{:S(2)}, u32[]{:S(2)}) collective-permute-start(bf16[4,40,128]{2,1,0:T(8,128)(2,1)S(1)} %get-tuple-element.22), channel_id=1, source_target_pairs={{0,31},{1,16},{2,17},{3,18},{4,19},{5,20},{6,21},{7,22},{8,23},{9,... | collective-permute-start | bytes 122888 | tf_op jit(solution)/shard_map/ppermute | solution.py:470
  88.9 5.9 %collective-permute-start.4 = (bf16[4,24,128]{2,1,0:T(8,128)(2,1)S(1)}, bf16[4,24,128]{2,1,0:T(8,128)(2,1)S(1)}, u32[]{:S(2)}, u32[]{:S(2)}) collective-permute-start(bf16[4,24,128]{2,1,0:T(8,128)(2,1)S(1)} %get-tuple-element.19), channel_id=1, source_target_pairs={{0,1},{1,2},{2,3},{3,4},{4,5},{5,6},{6,7},{7,8},{8,9},{9,10},{10,1... | collective-permute-start | bytes 73736 | tf_op jit(solution)/shard_map/ppermute | solution.py:467
  88.9 7.3 %collective-permute-start.6 = (bf16[4,24,128]{2,1,0:T(8,128)(2,1)S(1)}, bf16[4,24,128]{2,1,0:T(8,128)(2,1)S(1)}, u32[]{:S(2)}, u32[]{:S(2)}) collective-permute-start(bf16[4,24,128]{2,1,0:T(8,128)(2,1)S(1)} %get-tuple-element.21), channel_id=1, source_target_pairs={{0,17},{1,18},{2,19},{3,20},{4,21},{5,22},{6,23},{7,24},{8,25},{9,... | collective-permute-start | bytes 73736 | tf_op jit(solution)/shard_map/ppermute | solution.py:469
  94.9 1.4 %copy-start.7 = (bf16[4,24,128]{2,1,0:T(8,128)(2,1)}, bf16[4,24,128]{2,1,0:T(8,128)(2,1)S(1)}, u32[]{:S(2)}) copy-start(bf16[4,24,128]{2,1,0:T(8,128)(2,1)S(1)} %collective-permute-done.4.own_start) | copy-start | bytes 73732
  96.2 0.6 copy-start.8
  96.2 0.6 copy-start.5
  96.2 0.6 copy-start.6
  96.3 0.7 copy-start.1

commit v6 on v5

--- a/solution.py
+++ b/solution.py
@@ -58,6 +58,29 @@
         out_shape=[jax.ShapeDtypeStruct(s, BF16) for s in shapes],
         name="edges",
     )(side, cot, second, first, cot, second, first)
+
+
+def gate_kernel(cot, second, out):
+    size = cot.shape[0]
+    place = pl.ds(pl.program_id(0) * size, size)
+    out[place] = jnp.where(second[...] > 0, cot[...], jnp.zeros_like(cot))
+
+
+def gate_all(cot, second):
+    spheres, columns, merged = cot.shape
+    block = pl.BlockSpec((GROUP, columns, merged), lambda g: (g, 0, 0))
+    return pl.pallas_call(
+        gate_kernel,
+        grid=(spheres // GROUP,),
+        in_specs=[block, block],
+        out_specs=pl.BlockSpec(memory_space=pltpu.VMEM),
+        out_shape=pltpu.VMEM(cot.shape, BF16),
+        compiler_params=pltpu.CompilerParams(vmem_limit_bytes=48 * 2**20),
+        cost_estimate=pl.CostEstimate(
+            flops=cot.size, bytes_accessed=6 * cot.size, transcendentals=0
+        ),
+        name="gate",
+    )(cot, second)
 
 
 def block_start(flip, sphere, count, spheres):
@@ -365,7 +388,7 @@
         ),
         out_shape=[jax.ShapeDtypeStruct(shape, kind) for shape, kind in outputs.values()],
         compiler_params=pltpu.CompilerParams(
-            dimension_semantics=(pltpu.ARBITRARY,), vmem_limit_bytes=46 * 2**20
+            dimension_semantics=(pltpu.ARBITRARY,), vmem_limit_bytes=36 * 2**20
         ),
         cost_estimate=pl.CostEstimate(
             flops=flops, bytes_accessed=2 * second.size * 2, transcendentals=0
@@ -457,7 +480,7 @@
         row_table=jnp.transpose(row_resample, (1, 0, 2, 3)).reshape(spheres, 1, -1),
         tap_table=table.reshape(cameras * SLOT, spheres).astype(BF16),
     )
-    second_grad = jnp.where(second > 0, cot, jnp.zeros_like(cot))
+    second_grad = gate_all(cot, second)
     parts = sweep(info, (second_grad, first), tables, row_count, cameras, paired)
 
     if paired:

time: 99.2 us -> 98.6 us (level)
  other arithmetic: 9.14 us -> 0.17 us
  Pallas kernels: 69.8 us -> 77.9 us
    pallas_call x0 -> x1, Pallas kernels: none -> 10.9 us  [gate_all(): pl.pallas_call(gate_kernel, grid=(spheres // GROUP,), in_specs=[block, bl...]
    select_n x1 -> x0, other arithmetic: 8.97 us -> none  [body(): second_grad = jnp.where(second > 0, cot, jnp.zeros_like(cot))]
    pallas_call x1, Pallas kernels: 65.6 us -> 62.8 us  [sweep(): pl.pallas_call(functools.partial(sweep_kernel, names, row_count, paired),...]
  transfers between devices with their start and end apart: 8 -> 8, of which waited for: 2 -> 2; matrix products, arithmetic and copies ran while one was open for 11% -> 2% of each run, Pallas kernels for 0% -> 11%
where the time goes in v6:
time: 98.6 us; the launch traced here: 98.2 us
  Pallas kernels  77.9 us (79%)
  starting transfers between devices  10.1 us (10%)
  waiting for transfers between devices  6.45 us (7%)
  local copies, waits for them, and re-layouts  3.21 us (3%)
    pallas_call x1, Pallas kernels, sweep(): pl.pallas_call(functools.partial(sweep_kernel, names, row_count, paired),...  62.8 us
    pallas_call x1, Pallas kernels, gate_all(): pl.pallas_call(gate_kernel, grid=(spheres // GROUP,), in_specs=[block, bl...  10.9 us
    ppermute x1, waiting for transfers between devices, body(): lax.ppermute(parts.own_right, 'azim', forward)  5.04 us
    unnamed x38, local copies, waits for them, and re-layouts  2.64 us
    ppermute x1, starting transfers between devices, send(): return (right, got_rim, lax.ppermute(corner, both, joint(pairs, forward)))  2.45 us
    ppermute x1, starting transfers between devices, body(): lax.ppermute(parts.own_left, 'azim', backward)  2.27 us
    pallas_call x1, Pallas kernels, edges(): pl.pallas_call(edge_kernel, grid_spec=pltpu.PrefetchScalarGridSpec(num_sc...  2.23 us
    pallas_call x1, Pallas kernels, body(): pl.pallas_call(finish_kernel, out_shape=jax.ShapeDtypeStruct(parts.own.sh...  2.02 us
  transfers between devices with their start and end apart: 8, of which 2 were waited for; matrix products, arithmetic and copies ran while one was open for 2% of the time, Pallas kernels for 11%

profile of v6, /device:TPU:0, one launch (start us, length us, event | category | flops | bytes accessed | tf_op | source)
XLA Modules:
  0.0 98.2 jit_solution(7957827881999008062)
XLA Ops:
  0.0 2.2 %edges.1 = (bf16[64,8,256]{2,1,0:T(8,128)(2,1)}, bf16[3,256,256]{2,1,0:T(8,128)(2,1)}, bf16[2,8,256]{2,1,0:T(8,128)(2,1)}) custom-call(s32[1]{0:T(128)} %bitcast.1.side, bf16[64,256,256]{2,1,0:T(8,128)(2,1)} %cot.1, bf16[64,256,256]{2,1,0:T(8,128)(2,1)} %second.1, bf16[64,256,256]{2,1,0:T(8,128)(2,1)} %refs_11_.1, bf16[64,256,256]{2,1,0:T(8,128)(2,1)} %cot.1, ...), custom_call_target="tpu_custom_call" | custom-call | tf_op jit(solution)/shard_map/edges/pallas_call | solution.py:50
  2.2 2.4 %collective-permute-start.1 = (bf16[2,8,256]{2,1,0:T(8,128)(2,1)}, bf16[2,8,256]{2,1,0:T(8,128)(2,1)S(1)}, u32[]{:S(2)}, u32[]{:S(2)}) collective-permute-start(bf16[2,8,256]{2,1,0:T(8,128)(2,1)} %get-tuple-element.15), channel_id=1, source_target_pairs={{0,17},{1,18},{2,19},{3,20},{4,21},{5,22},{6,23},{7,24},{8,25},{9,... | collective-permute-start | bytes 24584 | tf_op jit(solution)/shard_map/ppermute | solution.py:457
  4.7 1.6 %collective-permute-start.2 = (bf16[64,8,256]{2,1,0:T(8,128)(2,1)}, bf16[64,8,256]{2,1,0:T(8,128)(2,1)S(1)}, u32[]{:S(2)}, u32[]{:S(2)}) collective-permute-start(bf16[64,8,256]{2,1,0:T(8,128)(2,1)} %get-tuple-element.16), channel_id=1, source_target_pairs={{0,1},{1,2},{2,3},{3,4},{4,5},{5,6},{6,7},{7,8},{8,9},{9,10},{10,1... | collective-permute-start | bytes 786440 | tf_op jit(solution)/shard_map/ppermute | solution.py:477
  6.3 0.5 collective-permute-start
  6.9 0.1 copy.36
  7.0 0.1 copy.28
  7.2 0.1 fusion.1
  7.3 0.1 fusion.5
  7.5 0.1 fusion.7
  7.6 0.1 fusion.9
  7.7 0.1 fusion.13
  7.8 0.1 fusion.15
  7.9 0.1 fusion.17
  8.1 0.1 fusion.21
  8.2 0.1 fusion.23
  8.3 0.1 fusion.25
  8.5 0.1 fusion.29
  8.6 0.1 fusion.31
  8.7 0.1 pad_add_fusion.refs_0_
  8.8 0.1 copy.45.refs_6_
  8.9 10.9 %gate.1.refs_8_.refs_10_ = bf16[64,256,256]{2,1,0:T(8,128)(2,1)S(1)} custom-call(bf16[64,256,256]{2,1,0:T(8,128)(2,1)} %cot.1, bf16[64,256,256]{2,1,0:T(8,128)(2,1)} %second.1), custom_call_target="tpu_custom_call" | custom-call | flops 4194304 | bytes 25165824 | tf_op jit(solution)/shard_map/gate/pallas_call | solution.py:72
  19.8 62.8 %sweep.1 = (f32[4,256,128]{2,1,0:T(8,128)S(1)}, bf16[4,40,128]{2,1,0:T(8,128)(2,1)S(1)}, bf16[4,24,128]{2,1,0:T(8,128)(2,1)S(1)}, bf16[4,256,128]{2,1,0:T(8,128)...) custom-call(s32[2]{0:T(128)S(1)} %pad_add_fusion.refs_0_, ...), custom_call_target="tpu_custom_call" | custom-call | flops 51539607552 | bytes 16777216 | tf_op jit(solution)/shard_map/sweep/pallas_call | solution.py:380
  82.6 0.8 copy-done
  83.4 1.5 %collective-permute-start.3 = (bf16[4,256,128]{2,1,0:T(8,128)(2,1)S(1)}, bf16[4,256,128]{2,1,0:T(8,128)(2,1)S(1)}, u32[]{:S(2)}, u32[]{:S(2)}) collective-permute-start(bf16[4,256,128]{2,1,0:T(8,128)(2,1)S(1)} %get-tuple-element.18), channel_id=1, source_target_pairs={{0,16},{16,0},{1,17},{17,1},{2,18},{18,2},{3,19},{19,3},{4,20},{20... | collective-permute-start | bytes 786440 | tf_op jit(solution)/shard_map/ppermute | solution.py:489
  85.0 2.3 %collective-permute-start.5 = (bf16[4,40,128]{2,1,0:T(8,128)(2,1)S(1)}, bf16[4,40,128]{2,1,0:T(8,128)(2,1)S(1)}, u32[]{:S(2)}, u32[]{:S(2)}) collective-permute-start(bf16[4,40,128]{2,1,0:T(8,128)(2,1)S(1)} %get-tuple-element.20), channel_id=1, source_target_pairs={{0,15},{1,0},{2,1},{3,2},{4,3},{5,4},{6,5},{7,6},{8,7},{9,8},{10,9... | collective-permute-start | bytes 122888 | tf_op jit(solution)/shard_map/ppermute | solution.py:491
  87.2 0.8 collective-permute-start.7
  88.1 0.9 collective-permute-start.6
  89.0 5.0 %collective-permute-done.4.own_start = bf16[4,24,128]{2,1,0:T(8,128)(2,1)S(1)} collective-permute-done((bf16[4,24,128]{2,1,0:T(8,128)(2,1)S(1)}, bf16[4,24,128]{2,1,0:T(8,128)(2,1)S(1)}, u32[]{:S(2)}, u32[]{:S(2)}) %collective-permute-start.4) | collective-permute-done | bytes 24608 | tf_op jit(solution)/shard_map/ppermute | solution.py:490
  94.0 1.4 %collective-permute-done.6.peer_start = bf16[4,24,128]{2,1,0:T(8,128)(2,1)S(1)} collective-permute-done((bf16[4,24,128]{2,1,0:T(8,128)(2,1)S(1)}, bf16[4,24,128]{2,1,0:T(8,128)(2,1)S(1)}, u32[]{:S(2)}, u32[]{:S(2)}) %collective-permute-start.6) | collective-permute-done | bytes 24608 | tf_op jit(solution)/shard_map/ppermute | solution.py:492
  95.5 0.5 copy-done.8
  96.0 0.1 copy-done.1
  96.1 2.0 %finish.1 = f32[4,256,128]{2,1,0:T(8,128)} custom-call(f32[4,256,128]{2,1,0:T(8,128)} %copy-done, bf16[4,256,128]{2,1,0:T(8,128)(2,1)} %copy-done.1, bf16[4,24,128]{2,1,0:T(8,128)(2,1)} %copy-done.7, bf16[4,40,128]{2,1,0:T(8,128)(2,1)} %copy-done.5, bf16[4,24,128]{2,1,0:T(8,128)(2,1)} %copy-done.8, bf16[4,40,128]{2,1,0:T(8,128)(2,1)} %copy-done.6), custom_call_target="tpu_custom_call" | custom-call | tf_op jit(solution)/shard_map/finish/pallas_call | solution.py:495
  (38 shorter events, 0.3 us)
Async XLA Ops:
  0.0 6.8 %copy-start.10 = (s32[4,64]{1,0:T(4,128)S(1)}, s32[4,64]{1,0:T(4,128)}, u32[]{:S(2)}) copy-start(s32[4,64]{1,0:T(4,128)} %param.17) | copy-start | bytes 3076
  0.0 6.8 %copy-start.2 = (bf16[3,3,3,32,32]{4,3,2,1,0:T(8,128)(2,1)S(1)}, bf16[3,3,3,32,32]{4,3,2,1,0:T(8,128)(2,1)}, u32[]{:S(2)}) copy-start(bf16[3,3,3,32,32]{4,3,2,1,0:T(8,128)(2,1)} %param.12) | copy-start | bytes 165892
  0.0 6.8 %copy-start.3 = (bf16[3,3,3,32,32]{4,3,2,1,0:T(8,128)(2,1)S(1)}, bf16[3,3,3,32,32]{4,3,2,1,0:T(8,128)(2,1)}, u32[]{:S(2)}) copy-start(bf16[3,3,3,32,32]{4,3,2,1,0:T(8,128)(2,1)} %param.13) | copy-start | bytes 165892
  2.2 17.5 %collective-permute-start.1 = (bf16[2,8,256]{2,1,0:T(8,128)(2,1)}, bf16[2,8,256]{2,1,0:T(8,128)(2,1)S(1)}, u32[]{:S(2)}, u32[]{:S(2)}) collective-permute-start(bf16[2,8,256]{2,1,0:T(8,128)(2,1)} %get-tuple-element.15), channel_id=1, source_target_pairs={{0,17},{1,18},{2,19},{3,20},{4,21},{5,22},{6,23},{7,24},{8,25},{9,... | collective-permute-start | bytes 24584 | tf_op jit(solution)/shard_map/ppermute | solution.py:457
  4.7 15.1 %collective-permute-start.2 = (bf16[64,8,256]{2,1,0:T(8,128)(2,1)}, bf16[64,8,256]{2,1,0:T(8,128)(2,1)S(1)}, u32[]{:S(2)}, u32[]{:S(2)}) collective-permute-start(bf16[64,8,256]{2,1,0:T(8,128)(2,1)} %get-tuple-element.16), channel_id=1, source_target_pairs={{0,1},{1,2},{2,3},{3,4},{4,5},{5,6},{6,7},{7,8},{8,9},{9,10},{10,1... | collective-permute-start | bytes 786440 | tf_op jit(solution)/shard_map/ppermute | solution.py:477
  6.3 13.5 %collective-permute-start = (bf16[3,256,256]{2,1,0:T(8,128)(2,1)}, bf16[3,256,256]{2,1,0:T(8,128)(2,1)S(1)}, u32[]{:S(2)}, u32[]{:S(2)}) collective-permute-start(bf16[3,256,256]{2,1,0:T(8,128)(2,1)} %get-tuple-element.14), channel_id=1, source_target_pairs={{0,16},{16,0},{1,17},{17,1},{2,18},{18,2},{3,19},{19,3},{4,20},{20... | collective-permute-start | bytes 1179656 | tf_op jit(solution)/shard_map/ppermute | solution.py:456
  7.4 1.0 %copy-start.9 = (f32[4,64,8]{1,2,0:T(8,128)S(1)}, f32[4,64,8]{1,2,0:T(8,128)}, u32[]{:S(2)}) copy-start(f32[4,64,8]{1,2,0:T(8,128)} %param.15) | copy-start | bytes 24580
  7.5 1.0 %copy-start.11 = (s32[4,64]{1,0:T(4,128)S(1)}, s32[4,64]{1,0:T(4,128)}, u32[]{:S(2)}) copy-start(s32[4,64]{1,0:T(4,128)} %param.16) | copy-start | bytes 3076
  7.7 1.0 %copy-start.4 = (f32[4,64,8,8]{1,3,2,0:T(8,128)S(1)}, f32[4,64,8,8]{1,3,2,0:T(8,128)}, u32[]{:S(2)}) copy-start(f32[4,64,8,8]{1,3,2,0:T(8,128)} %param.14) | copy-start | bytes 196612
  82.6 0.8 copy-start
  83.4 12.0 %collective-permute-start.3 = (bf16[4,256,128]{2,1,0:T(8,128)(2,1)S(1)}, bf16[4,256,128]{2,1,0:T(8,128)(2,1)S(1)}, u32[]{:S(2)}, u32[]{:S(2)}) collective-permute-start(bf16[4,256,128]{2,1,0:T(8,128)(2,1)S(1)} %get-tuple-element.18), channel_id=1, source_target_pairs={{0,16},{16,0},{1,17},{17,1},{2,18},{18,2},{3,19},{19,3},{4,20},{20... | collective-permute-start | bytes 786440 | tf_op jit(solution)/shard_map/ppermute | solution.py:489
  85.0 10.5 %collective-permute-start.5 = (bf16[4,40,128]{2,1,0:T(8,128)(2,1)S(1)}, bf16[4,40,128]{2,1,0:T(8,128)(2,1)S(1)}, u32[]{:S(2)}, u32[]{:S(2)}) collective-permute-start(bf16[4,40,128]{2,1,0:T(8,128)(2,1)S(1)} %get-tuple-element.20), channel_id=1, source_target_pairs={{0,15},{1,0},{2,1},{3,2},{4,3},{5,4},{6,5},{7,6},{8,7},{9,8},{10,9... | collective-permute-start | bytes 122888 | tf_op jit(solution)/shard_map/ppermute | solution.py:491
  87.2 8.2 %collective-permute-start.7 = (bf16[4,40,128]{2,1,0:T(8,128)(2,1)S(1)}, bf16[4,40,128]{2,1,0:T(8,128)(2,1)S(1)}, u32[]{:S(2)}, u32[]{:S(2)}) collective-permute-start(bf16[4,40,128]{2,1,0:T(8,128)(2,1)S(1)} %get-tuple-element.22), channel_id=1, source_target_pairs={{0,31},{1,16},{2,17},{3,18},{4,19},{5,20},{6,21},{7,22},{8,23},{9,... | collective-permute-start | bytes 122888 | tf_op jit(solution)/shard_map/ppermute | solution.py:493
  88.1 5.9 %collective-permute-start.4 = (bf16[4,24,128]{2,1,0:T(8,128)(2,1)S(1)}, bf16[4,24,128]{2,1,0:T(8,128)(2,1)S(1)}, u32[]{:S(2)}, u32[]{:S(2)}) collective-permute-start(bf16[4,24,128]{2,1,0:T(8,128)(2,1)S(1)} %get-tuple-element.19), channel_id=1, source_target_pairs={{0,1},{1,2},{2,3},{3,4},{4,5},{5,6},{6,7},{7,8},{8,9},{9,10},{10,1... | collective-permute-start | bytes 73736 | tf_op jit(solution)/shard_map/ppermute | solution.py:490
  88.1 7.3 %collective-permute-start.6 = (bf16[4,24,128]{2,1,0:T(8,128)(2,1)S(1)}, bf16[4,24,128]{2,1,0:T(8,128)(2,1)S(1)}, u32[]{:S(2)}, u32[]{:S(2)}) collective-permute-start(bf16[4,24,128]{2,1,0:T(8,128)(2,1)S(1)} %get-tuple-element.21), channel_id=1, source_target_pairs={{0,17},{1,18},{2,19},{3,20},{4,21},{5,22},{6,23},{7,24},{8,25},{9,... | collective-permute-start | bytes 73736 | tf_op jit(solution)/shard_map/ppermute | solution.py:492
  94.0 1.4 %copy-start.7 = (bf16[4,24,128]{2,1,0:T(8,128)(2,1)}, bf16[4,24,128]{2,1,0:T(8,128)(2,1)S(1)}, u32[]{:S(2)}) copy-start(bf16[4,24,128]{2,1,0:T(8,128)(2,1)S(1)} %collective-permute-done.4.own_start) | copy-start | bytes 73732
  95.4 0.6 copy-start.8
  95.4 0.6 copy-start.5
  95.4 0.6 copy-start.6
  95.4 0.7 copy-start.1

commit v7 on v6

--- a/solution.py
+++ b/solution.py
@@ -23,18 +23,22 @@
 F32 = jnp.float32
 
 
-def edge_kernel(
-    side, cot_right, second_right, first_right, cot_rim, second_rim, first_rim, right, rim, corner
-):
-    spheres = cot_right.shape[0]
-    gate = lambda cot, saved: jnp.where(saved > 0, cot, jnp.zeros_like(cot))
+def rim_kernel(side, cot_rim, second_rim, first_rim, rim):
     top = side[0]
     for index in range(2):
         place = top + (1 - 2 * top) * index
-        rim[index] = gate(cot_rim[place], second_rim[place])
+        cot, saved = cot_rim[place], second_rim[place]
+        rim[index] = jnp.where(saved > 0, cot, jnp.zeros_like(cot))
     rim[2] = first_rim[0]
+
+
+def edge_kernel(side, cot_right, second_right, first_right, rim, right, corner):
+    del rim
+    spheres = cot_right.shape[0]
+    top = side[0]
     last = slice(8 - HALO, 8)
-    right[:, 0:HALO] = gate(cot_right[:, last], second_right[:, last])
+    cot, saved = cot_right[:, last], second_right[:, last]
+    right[:, 0:HALO] = jnp.where(saved > 0, cot, jnp.zeros_like(cot))
     right[:, HALO : 2 * HALO] = first_right[:, last]
     for index in range(2):
         corner[index] = right[top * (spheres - 1) + (1 - 2 * top) * index]
@@ -46,18 +50,28 @@
     high = pl.BlockSpec((spheres, 8, merged), lambda g, s: (0, columns // 8 - 1, 0))
     pair = pl.BlockSpec((2, columns, merged), lambda g, s: (s[0] * (pairs - 1), 0, 0))
     one = pl.BlockSpec((1, columns, merged), lambda g, s: (s[0] * (spheres - 1), 0, 0))
-    shapes = ((spheres, 2 * HALO, merged), (3, columns, merged), (2, 2 * HALO, merged))
-    return pl.pallas_call(
-        edge_kernel,
-        grid_spec=pltpu.PrefetchScalarGridSpec(
-            num_scalar_prefetch=1,
-            grid=(1,),
-            in_specs=[high, high, high, pair, pair, one],
-            out_specs=[pl.BlockSpec(s, lambda g, s: (0, 0, 0)) for s in shapes],
-        ),
-        out_shape=[jax.ShapeDtypeStruct(s, BF16) for s in shapes],
-        name="edges",
-    )(side, cot, second, first, cot, second, first)
+
+    def call(kernel, in_specs, shapes, name):
+        return pl.pallas_call(
+            kernel,
+            grid_spec=pltpu.PrefetchScalarGridSpec(
+                num_scalar_prefetch=1,
+                grid=(1,),
+                in_specs=in_specs,
+                out_specs=[pl.BlockSpec(s, lambda g, s: (0, 0, 0)) for s in shapes],
+            ),
+            out_shape=[jax.ShapeDtypeStruct(s, BF16) for s in shapes],
+            name=name,
+        )
+
+    rim_shape = (3, columns, merged)
+    (rim,) = call(rim_kernel, [pair, pair, one], (rim_shape,), "rim")(side, cot, second, first)
+    shapes = ((spheres, 2 * HALO, merged), (2, 2 * HALO, merged))
+    token = pl.BlockSpec((1, 8, merged), lambda g, s: (0, 0, 0))
+    right, corner = call(edge_kernel, [high, high, high, token], shapes, "edges")(
+        side, cot, second, first, rim
+    )
+    return right, rim, corner
 
 
 def gate_kernel(cot, second, out):
@@ -68,14 +82,14 @@
 
 def gate_all(cot, second):
     spheres, columns, merged = cot.shape
-    block = pl.BlockSpec((GROUP, columns, merged), lambda g: (g, 0, 0))
+    block = pl.BlockSpec((4 * GROUP, columns, merged), lambda g: (g, 0, 0))
     return pl.pallas_call(
         gate_kernel,
-        grid=(spheres // GROUP,),
+        grid=(spheres // (4 * GROUP),),
         in_specs=[block, block],
         out_specs=pl.BlockSpec(memory_space=pltpu.VMEM),
         out_shape=pltpu.VMEM(cot.shape, BF16),
-        compiler_params=pltpu.CompilerParams(vmem_limit_bytes=48 * 2**20),
+        compiler_params=pltpu.CompilerParams(vmem_limit_bytes=44 * 2**20),
         cost_estimate=pl.CostEstimate(
             flops=cot.size, bytes_accessed=6 * cot.size, transcendentals=0
         ),

time: 98.6 us -> 97.5 us (0.989)
    pallas_call x2 -> x3, Pallas kernels: 13.1 us -> 10.1 us  [the longest x1 6.4 us: gate_all(): pl.pallas_call(gate_kernel, grid=(spheres // (4 * GROUP),), in_specs=[blo...]
    ppermute x1, starting transfers between devices: 0.51 us -> 3 us  [send(): got_rim = lax.ppermute(rim, 'depth', pairs)]
    ppermute x1, starting transfers between devices: 2.45 us -> 0.01 us  [send(): return (right, got_rim, lax.ppermute(corner, both, joint(pairs, forward)))]
    pallas_call x1, Pallas kernels: 62.8 us -> 64.9 us  [sweep(): pl.pallas_call(functools.partial(sweep_kernel, names, row_count, paired),...]
  transfers between devices with their start and end apart: 8 -> 8, of which waited for: 2 -> 2; matrix products, arithmetic and copies ran while one was open for 2% -> 2% of each run, Pallas kernels for 11% -> 9%
where the time goes in v7:
time: 97.5 us; the launch traced here: 97.3 us
  Pallas kernels  77 us (79%)
  starting transfers between devices  10.4 us (11%)
  waiting for transfers between devices  6.16 us (6%)
  local copies, waits for them, and re-layouts  3.21 us (3%)
    pallas_call x1, Pallas kernels, sweep(): pl.pallas_call(functools.partial(sweep_kernel, names, row_count, paired),...  64.9 us
    pallas_call x1, Pallas kernels, gate_all(): pl.pallas_call(gate_kernel, grid=(spheres // (4 * GROUP),), in_specs=[blo...  6.4 us
    ppermute x1, waiting for transfers between devices, body(): lax.ppermute(parts.own_right, 'azim', forward)  4.71 us
    ppermute x1, starting transfers between devices, send(): got_rim = lax.ppermute(rim, 'depth', pairs)  3 us
    unnamed x38, local copies, waits for them, and re-layouts  2.64 us
    ppermute x1, starting transfers between devices, body(): lax.ppermute(parts.own_left, 'azim', backward)  2.56 us
    pallas_call x1, Pallas kernels, body(): pl.pallas_call(finish_kernel, out_shape=jax.ShapeDtypeStruct(parts.own.sh...  2.02 us
  transfers between devices with their start and end apart: 8, of which 2 were waited for; matrix products, arithmetic and copies ran while one was open for 2% of the time, Pallas kernels for 9%

profile of v7, /device:TPU:0, one launch (start us, length us, event | category | flops | bytes accessed | tf_op | source)
XLA Modules:
  0.0 97.3 jit_solution(8818826070477701112)
XLA Ops:
  0.0 1.8 %rim.1 = bf16[3,256,256]{2,1,0:T(8,128)(2,1)} custom-call(s32[1]{0:T(128)} %bitcast.1.side, bf16[64,256,256]{2,1,0:T(8,128)(2,1)} %cot.1, bf16[64,256,256]{2,1,0:T(8,128)(2,1)} %second.1, bf16[64,256,256]{2,1,0:T(8,128)(2,1)} %refs_11_.1), custom_call_target="tpu_custom_call" | custom-call | tf_op jit(solution)/shard_map/rim/pallas_call | solution.py:68
  1.9 3.0 %collective-permute-start = (bf16[3,256,256]{2,1,0:T(8,128)(2,1)}, bf16[3,256,256]{2,1,0:T(8,128)(2,1)S(1)}, u32[]{:S(2)}, u32[]{:S(2)}) collective-permute-start(bf16[3,256,256]{2,1,0:T(8,128)(2,1)} %rim.1), channel_id=1, source_target_pairs={{0,16},{16,0},{1,17},{17,1},{2,18},{18,2},{3,19},{19,3},{4,20},{20... | collective-permute-start | bytes 1179656 | tf_op jit(solution)/shard_map/ppermute | solution.py:470
  4.8 1.9 %edges.1 = (bf16[64,8,256]{2,1,0:T(8,128)(2,1)}, bf16[2,8,256]{2,1,0:T(8,128)(2,1)}) custom-call(s32[1]{0:T(128)} %bitcast.1.side, bf16[64,256,256]{2,1,0:T(8,128)(2,1)} %cot.1, bf16[64,256,256]{2,1,0:T(8,128)(2,1)} %second.1, bf16[64,256,256]{2,1,0:T(8,128)(2,1)} %refs_11_.1, bf16[3,256,256]{2,1,0:T(8,128)(2,1)} %rim.1), custom_call_target="tpu_custom_call" | custom-call | tf_op jit(solution)/shard_map/edges/pallas_call | solution.py:71
  6.8 1.5 %collective-permute-start.2 = (bf16[64,8,256]{2,1,0:T(8,128)(2,1)}, bf16[64,8,256]{2,1,0:T(8,128)(2,1)S(1)}, u32[]{:S(2)}, u32[]{:S(2)}) collective-permute-start(bf16[64,8,256]{2,1,0:T(8,128)(2,1)} %get-tuple-element.14), channel_id=1, source_target_pairs={{0,1},{1,2},{2,3},{3,4},{4,5},{5,6},{6,7},{7,8},{8,9},{9,10},{10,1... | collective-permute-start | bytes 786440 | tf_op jit(solution)/shard_map/ppermute | solution.py:491
  8.4 0.1 copy.36
  8.5 0.1 copy.28
  8.7 0.1 fusion.1
  8.8 0.1 fusion.5
  9.0 0.1 fusion.7
  9.1 0.1 fusion.9
  9.2 0.1 fusion.13
  9.3 0.1 fusion.15
  9.4 0.1 fusion.17
  9.6 0.1 fusion.21
  9.7 0.1 fusion.23
  9.8 0.1 fusion.25
  10.0 0.1 fusion.29
  10.1 0.1 fusion.31
  10.3 0.1 copy.45.refs_6_
  10.4 6.4 %gate.1.refs_8_.refs_10_ = bf16[64,256,256]{2,1,0:T(8,128)(2,1)S(1)} custom-call(bf16[64,256,256]{2,1,0:T(8,128)(2,1)} %cot.1, bf16[64,256,256]{2,1,0:T(8,128)(2,1)} %second.1), custom_call_target="tpu_custom_call" | custom-call | flops 4194304 | bytes 25165824 | tf_op jit(solution)/shard_map/gate/pallas_call | solution.py:86
  16.8 64.9 %sweep.1 = (f32[4,256,128]{2,1,0:T(8,128)S(1)}, bf16[4,40,128]{2,1,0:T(8,128)(2,1)S(1)}, bf16[4,24,128]{2,1,0:T(8,128)(2,1)S(1)}, bf16[4,256,128]{2,1,0:T(8,128)...) custom-call(s32[2]{0:T(128)S(1)} %pad_add_fusion.refs_0_, ...), custom_call_target="tpu_custom_call" | custom-call | flops 51539607552 | bytes 16777216 | tf_op jit(solution)/shard_map/sweep/pallas_call | solution.py:394
  81.7 0.8 copy-done
  82.5 1.5 %collective-permute-start.3 = (bf16[4,256,128]{2,1,0:T(8,128)(2,1)S(1)}, bf16[4,256,128]{2,1,0:T(8,128)(2,1)S(1)}, u32[]{:S(2)}, u32[]{:S(2)}) collective-permute-start(bf16[4,256,128]{2,1,0:T(8,128)(2,1)S(1)} %get-tuple-element.16), channel_id=1, source_target_pairs={{0,16},{16,0},{1,17},{17,1},{2,18},{18,2},{3,19},{19,3},{4,20},{20... | collective-permute-start | bytes 786440 | tf_op jit(solution)/shard_map/ppermute | solution.py:503
  84.0 2.6 %collective-permute-start.5 = (bf16[4,40,128]{2,1,0:T(8,128)(2,1)S(1)}, bf16[4,40,128]{2,1,0:T(8,128)(2,1)S(1)}, u32[]{:S(2)}, u32[]{:S(2)}) collective-permute-start(bf16[4,40,128]{2,1,0:T(8,128)(2,1)S(1)} %get-tuple-element.18), channel_id=1, source_target_pairs={{0,15},{1,0},{2,1},{3,2},{4,3},{5,4},{6,5},{7,6},{8,7},{9,8},{10,9... | collective-permute-start | bytes 122888 | tf_op jit(solution)/shard_map/ppermute | solution.py:505
  86.6 0.5 collective-permute-start.7
  87.1 0.2 collective-permute-start.4
  87.3 1.1 %collective-permute-start.6 = (bf16[4,24,128]{2,1,0:T(8,128)(2,1)S(1)}, bf16[4,24,128]{2,1,0:T(8,128)(2,1)S(1)}, u32[]{:S(2)}, u32[]{:S(2)}) collective-permute-start(bf16[4,24,128]{2,1,0:T(8,128)(2,1)S(1)} %get-tuple-element.19), channel_id=1, source_target_pairs={{0,17},{1,18},{2,19},{3,20},{4,21},{5,22},{6,23},{7,24},{8,25},{9,... | collective-permute-start | bytes 73736 | tf_op jit(solution)/shard_map/ppermute | solution.py:506
  88.4 4.7 %collective-permute-done.4.own_start = bf16[4,24,128]{2,1,0:T(8,128)(2,1)S(1)} collective-permute-done((bf16[4,24,128]{2,1,0:T(8,128)(2,1)S(1)}, bf16[4,24,128]{2,1,0:T(8,128)(2,1)S(1)}, u32[]{:S(2)}, u32[]{:S(2)}) %collective-permute-start.4) | collective-permute-done | bytes 24608 | tf_op jit(solution)/shard_map/ppermute | solution.py:504
  93.1 1.4 %collective-permute-done.6.peer_start = bf16[4,24,128]{2,1,0:T(8,128)(2,1)S(1)} collective-permute-done((bf16[4,24,128]{2,1,0:T(8,128)(2,1)S(1)}, bf16[4,24,128]{2,1,0:T(8,128)(2,1)S(1)}, u32[]{:S(2)}, u32[]{:S(2)}) %collective-permute-start.6) | collective-permute-done | bytes 24608 | tf_op jit(solution)/shard_map/ppermute | solution.py:506
  94.6 0.5 copy-done.8
  95.1 0.1 copy-done.1
  95.2 2.0 %finish.1 = f32[4,256,128]{2,1,0:T(8,128)} custom-call(f32[4,256,128]{2,1,0:T(8,128)} %copy-done, bf16[4,256,128]{2,1,0:T(8,128)(2,1)} %copy-done.1, bf16[4,24,128]{2,1,0:T(8,128)(2,1)} %copy-done.7, bf16[4,40,128]{2,1,0:T(8,128)(2,1)} %copy-done.5, bf16[4,24,128]{2,1,0:T(8,128)(2,1)} %copy-done.8, bf16[4,40,128]{2,1,0:T(8,128)(2,1)} %copy-done.6), custom_call_target="tpu_custom_call" | custom-call | tf_op jit(solution)/shard_map/finish/pallas_call | solution.py:509
  (39 shorter events, 0.4 us)
Async XLA Ops:
  1.8 6.5 %copy-start.10 = (s32[4,64]{1,0:T(4,128)S(1)}, s32[4,64]{1,0:T(4,128)}, u32[]{:S(2)}) copy-start(s32[4,64]{1,0:T(4,128)} %param.17) | copy-start | bytes 3076
  1.8 6.5 %copy-start.2 = (bf16[3,3,3,32,32]{4,3,2,1,0:T(8,128)(2,1)S(1)}, bf16[3,3,3,32,32]{4,3,2,1,0:T(8,128)(2,1)}, u32[]{:S(2)}) copy-start(bf16[3,3,3,32,32]{4,3,2,1,0:T(8,128)(2,1)} %param.12) | copy-start | bytes 165892
  1.9 6.5 %copy-start.3 = (bf16[3,3,3,32,32]{4,3,2,1,0:T(8,128)(2,1)S(1)}, bf16[3,3,3,32,32]{4,3,2,1,0:T(8,128)(2,1)}, u32[]{:S(2)}) copy-start(bf16[3,3,3,32,32]{4,3,2,1,0:T(8,128)(2,1)} %param.13) | copy-start | bytes 165892
  1.9 15.0 %collective-permute-start = (bf16[3,256,256]{2,1,0:T(8,128)(2,1)}, bf16[3,256,256]{2,1,0:T(8,128)(2,1)S(1)}, u32[]{:S(2)}, u32[]{:S(2)}) collective-permute-start(bf16[3,256,256]{2,1,0:T(8,128)(2,1)} %rim.1), channel_id=1, source_target_pairs={{0,16},{16,0},{1,17},{17,1},{2,18},{18,2},{3,19},{19,3},{4,20},{20... | collective-permute-start | bytes 1179656 | tf_op jit(solution)/shard_map/ppermute | solution.py:470
  6.8 10.0 %collective-permute-start.1 = (bf16[2,8,256]{2,1,0:T(8,128)(2,1)}, bf16[2,8,256]{2,1,0:T(8,128)(2,1)S(1)}, u32[]{:S(2)}, u32[]{:S(2)}) collective-permute-start(bf16[2,8,256]{2,1,0:T(8,128)(2,1)} %get-tuple-element.13), channel_id=1, source_target_pairs={{0,17},{1,18},{2,19},{3,20},{4,21},{5,22},{6,23},{7,24},{8,25},{9,... | collective-permute-start | bytes 24584 | tf_op jit(solution)/shard_map/ppermute | solution.py:471
  6.8 10.0 %collective-permute-start.2 = (bf16[64,8,256]{2,1,0:T(8,128)(2,1)}, bf16[64,8,256]{2,1,0:T(8,128)(2,1)S(1)}, u32[]{:S(2)}, u32[]{:S(2)}) collective-permute-start(bf16[64,8,256]{2,1,0:T(8,128)(2,1)} %get-tuple-element.14), channel_id=1, source_target_pairs={{0,1},{1,2},{2,3},{3,4},{4,5},{5,6},{6,7},{7,8},{8,9},{9,10},{10,1... | collective-permute-start | bytes 786440 | tf_op jit(solution)/shard_map/ppermute | solution.py:491
  8.9 1.0 %copy-start.9 = (f32[4,64,8]{1,2,0:T(8,128)S(1)}, f32[4,64,8]{1,2,0:T(8,128)}, u32[]{:S(2)}) copy-start(f32[4,64,8]{1,2,0:T(8,128)} %param.15) | copy-start | bytes 24580
  9.0 1.0 %copy-start.11 = (s32[4,64]{1,0:T(4,128)S(1)}, s32[4,64]{1,0:T(4,128)}, u32[]{:S(2)}) copy-start(s32[4,64]{1,0:T(4,128)} %param.16) | copy-start | bytes 3076
  9.2 1.0 %copy-start.4 = (f32[4,64,8,8]{1,3,2,0:T(8,128)S(1)}, f32[4,64,8,8]{1,3,2,0:T(8,128)}, u32[]{:S(2)}) copy-start(f32[4,64,8,8]{1,3,2,0:T(8,128)} %param.14) | copy-start | bytes 196612
  81.7 0.8 copy-start
  82.5 12.0 %collective-permute-start.3 = (bf16[4,256,128]{2,1,0:T(8,128)(2,1)S(1)}, bf16[4,256,128]{2,1,0:T(8,128)(2,1)S(1)}, u32[]{:S(2)}, u32[]{:S(2)}) collective-permute-start(bf16[4,256,128]{2,1,0:T(8,128)(2,1)S(1)} %get-tuple-element.16), channel_id=1, source_target_pairs={{0,16},{16,0},{1,17},{17,1},{2,18},{18,2},{3,19},{19,3},{4,20},{20... | collective-permute-start | bytes 786440 | tf_op jit(solution)/shard_map/ppermute | solution.py:503
  84.0 10.5 %collective-permute-start.5 = (bf16[4,40,128]{2,1,0:T(8,128)(2,1)S(1)}, bf16[4,40,128]{2,1,0:T(8,128)(2,1)S(1)}, u32[]{:S(2)}, u32[]{:S(2)}) collective-permute-start(bf16[4,40,128]{2,1,0:T(8,128)(2,1)S(1)} %get-tuple-element.18), channel_id=1, source_target_pairs={{0,15},{1,0},{2,1},{3,2},{4,3},{5,4},{6,5},{7,6},{8,7},{9,8},{10,9... | collective-permute-start | bytes 122888 | tf_op jit(solution)/shard_map/ppermute | solution.py:505
  86.6 7.9 %collective-permute-start.7 = (bf16[4,40,128]{2,1,0:T(8,128)(2,1)S(1)}, bf16[4,40,128]{2,1,0:T(8,128)(2,1)S(1)}, u32[]{:S(2)}, u32[]{:S(2)}) collective-permute-start(bf16[4,40,128]{2,1,0:T(8,128)(2,1)S(1)} %get-tuple-element.20), channel_id=1, source_target_pairs={{0,31},{1,16},{2,17},{3,18},{4,19},{5,20},{6,21},{7,22},{8,23},{9,... | collective-permute-start | bytes 122888 | tf_op jit(solution)/shard_map/ppermute | solution.py:507
  87.1 5.9 %collective-permute-start.4 = (bf16[4,24,128]{2,1,0:T(8,128)(2,1)S(1)}, bf16[4,24,128]{2,1,0:T(8,128)(2,1)S(1)}, u32[]{:S(2)}, u32[]{:S(2)}) collective-permute-start(bf16[4,24,128]{2,1,0:T(8,128)(2,1)S(1)} %get-tuple-element.17), channel_id=1, source_target_pairs={{0,1},{1,2},{2,3},{3,4},{4,5},{5,6},{6,7},{7,8},{8,9},{9,10},{10,1... | collective-permute-start | bytes 73736 | tf_op jit(solution)/shard_map/ppermute | solution.py:504
  87.3 7.2 %collective-permute-start.6 = (bf16[4,24,128]{2,1,0:T(8,128)(2,1)S(1)}, bf16[4,24,128]{2,1,0:T(8,128)(2,1)S(1)}, u32[]{:S(2)}, u32[]{:S(2)}) collective-permute-start(bf16[4,24,128]{2,1,0:T(8,128)(2,1)S(1)} %get-tuple-element.19), channel_id=1, source_target_pairs={{0,17},{1,18},{2,19},{3,20},{4,21},{5,22},{6,23},{7,24},{8,25},{9,... | collective-permute-start | bytes 73736 | tf_op jit(solution)/shard_map/ppermute | solution.py:506
  93.1 1.5 %copy-start.7 = (bf16[4,24,128]{2,1,0:T(8,128)(2,1)}, bf16[4,24,128]{2,1,0:T(8,128)(2,1)S(1)}, u32[]{:S(2)}) copy-start(bf16[4,24,128]{2,1,0:T(8,128)(2,1)S(1)} %collective-permute-done.4.own_start) | copy-start | bytes 73732
  94.5 0.6 copy-start.8
  94.5 0.6 copy-start.5
  94.5 0.6 copy-start.6
  94.5 0.7 copy-start.1

commit v8 on v6

--- a/solution.py
+++ b/solution.py
@@ -68,14 +68,14 @@
 
 def gate_all(cot, second):
     spheres, columns, merged = cot.shape
-    block = pl.BlockSpec((GROUP, columns, merged), lambda g: (g, 0, 0))
+    block = pl.BlockSpec((4 * GROUP, columns, merged), lambda g: (g, 0, 0))
     return pl.pallas_call(
         gate_kernel,
-        grid=(spheres // GROUP,),
+        grid=(spheres // (4 * GROUP),),
         in_specs=[block, block],
         out_specs=pl.BlockSpec(memory_space=pltpu.VMEM),
         out_shape=pltpu.VMEM(cot.shape, BF16),
-        compiler_params=pltpu.CompilerParams(vmem_limit_bytes=48 * 2**20),
+        compiler_params=pltpu.CompilerParams(vmem_limit_bytes=44 * 2**20),
         cost_estimate=pl.CostEstimate(
             flops=cot.size, bytes_accessed=6 * cot.size, transcendentals=0
         ),

time: 98.6 us -> 96.1 us (0.975)
  Pallas kernels: 77.9 us -> 73.7 us
  waiting for transfers between devices: 6.45 us -> 9.16 us
    pallas_call x1, Pallas kernels: 10.9 us -> 6.4 us  [gate_all(): pl.pallas_call(gate_kernel, grid=(spheres // (4 * GROUP),), in_specs=[blo...]
    ppermute x1, waiting for transfers between devices: 0.01 us -> 2.31 us  [send(): got_rim = lax.ppermute(rim, 'depth', pairs)]
    ppermute x1, starting transfers between devices: 0.84 us -> 2.11 us  [body(): lax.ppermute(parts.peer_left, both, joint(swap, backward))]
  transfers between devices with their start and end apart: 8 -> 8, of which waited for: 2 -> 3; matrix products, arithmetic and copies ran while one was open for 2% -> 2% of each run, Pallas kernels for 11% -> 7%
where the time goes in v8:
time: 96.1 us; the launch traced here: 95.9 us
  Pallas kernels  73.7 us (77%)
  starting transfers between devices  9.38 us (10%)
  waiting for transfers between devices  9.16 us (10%)
  local copies, waits for them, and re-layouts  3.21 us (3%)
    pallas_call x1, Pallas kernels, sweep(): pl.pallas_call(functools.partial(sweep_kernel, names, row_count, paired),...  63.1 us
    pallas_call x1, Pallas kernels, gate_all(): pl.pallas_call(gate_kernel, grid=(spheres // (4 * GROUP),), in_specs=[blo...  6.4 us
    ppermute x1, waiting for transfers between devices, body(): lax.ppermute(parts.own_right, 'azim', forward)  5.94 us
    unnamed x38, local copies, waits for them, and re-layouts  2.64 us
    ppermute x1, starting transfers between devices, send(): return (right, got_rim, lax.ppermute(corner, both, joint(pairs, forward)))  2.45 us
    ppermute x1, waiting for transfers between devices, send(): got_rim = lax.ppermute(rim, 'depth', pairs)  2.31 us
    pallas_call x1, Pallas kernels, edges(): pl.pallas_call(edge_kernel, grid_spec=pltpu.PrefetchScalarGridSpec(num_sc...  2.23 us
    ppermute x1, starting transfers between devices, body(): lax.ppermute(parts.peer_left, both, joint(swap, backward))  2.11 us
  transfers between devices with their start and end apart: 8, of which 3 were waited for; matrix products, arithmetic and copies ran while one was open for 2% of the time, Pallas kernels for 7%

profile of v8, /device:TPU:0, one launch (start us, length us, event | category | flops | bytes accessed | tf_op | source)
XLA Modules:
  0.0 95.9 jit_solution(10229493069150239566)
XLA Ops:
  0.0 2.2 %edges.1 = (bf16[64,8,256]{2,1,0:T(8,128)(2,1)}, bf16[3,256,256]{2,1,0:T(8,128)(2,1)}, bf16[2,8,256]{2,1,0:T(8,128)(2,1)}) custom-call(s32[1]{0:T(128)} %bitcast.1.side, bf16[64,256,256]{2,1,0:T(8,128)(2,1)} %cot.1, bf16[64,256,256]{2,1,0:T(8,128)(2,1)} %second.1, bf16[64,256,256]{2,1,0:T(8,128)(2,1)} %refs_11_.1, bf16[64,256,256]{2,1,0:T(8,128)(2,1)} %cot.1, ...), custom_call_target="tpu_custom_call" | custom-call | tf_op jit(solution)/shard_map/edges/pallas_call | solution.py:50
  2.2 2.4 %collective-permute-start.1 = (bf16[2,8,256]{2,1,0:T(8,128)(2,1)}, bf16[2,8,256]{2,1,0:T(8,128)(2,1)S(1)}, u32[]{:S(2)}, u32[]{:S(2)}) collective-permute-start(bf16[2,8,256]{2,1,0:T(8,128)(2,1)} %get-tuple-element.15), channel_id=1, source_target_pairs={{0,17},{1,18},{2,19},{3,20},{4,21},{5,22},{6,23},{7,24},{8,25},{9,... | collective-permute-start | bytes 24584 | tf_op jit(solution)/shard_map/ppermute | solution.py:457
  4.7 1.6 %collective-permute-start.2 = (bf16[64,8,256]{2,1,0:T(8,128)(2,1)}, bf16[64,8,256]{2,1,0:T(8,128)(2,1)S(1)}, u32[]{:S(2)}, u32[]{:S(2)}) collective-permute-start(bf16[64,8,256]{2,1,0:T(8,128)(2,1)} %get-tuple-element.16), channel_id=1, source_target_pairs={{0,1},{1,2},{2,3},{3,4},{4,5},{5,6},{6,7},{7,8},{8,9},{9,10},{10,1... | collective-permute-start | bytes 786440 | tf_op jit(solution)/shard_map/ppermute | solution.py:477
  6.3 0.5 collective-permute-start
  6.9 0.1 copy.36
  7.0 0.1 copy.28
  7.2 0.1 fusion.1
  7.3 0.1 fusion.5
  7.5 0.1 fusion.7
  7.6 0.1 fusion.9
  7.7 0.1 fusion.13
  7.8 0.1 fusion.15
  7.9 0.1 fusion.17
  8.1 0.1 fusion.21
  8.2 0.1 fusion.23
  8.3 0.1 fusion.25
  8.5 0.1 fusion.29
  8.6 0.1 fusion.31
  8.7 0.1 pad_add_fusion.refs_0_
  8.8 0.1 copy.45.refs_6_
  8.9 6.4 %gate.1.refs_8_.refs_10_ = bf16[64,256,256]{2,1,0:T(8,128)(2,1)S(1)} custom-call(bf16[64,256,256]{2,1,0:T(8,128)(2,1)} %cot.1, bf16[64,256,256]{2,1,0:T(8,128)(2,1)} %second.1), custom_call_target="tpu_custom_call" | custom-call | flops 4194304 | bytes 25165824 | tf_op jit(solution)/shard_map/gate/pallas_call | solution.py:72
  15.3 2.3 %collective-permute-done.refs_1_ = bf16[3,256,256]{2,1,0:T(8,128)(2,1)S(1)} collective-permute-done((bf16[3,256,256]{2,1,0:T(8,128)(2,1)}, bf16[3,256,256]{2,1,0:T(8,128)(2,1)S(1)}, u32[]{:S(2)}, u32[]{:S(2)}) %collective-permute-start) | collective-permute-done | bytes 393248 | tf_op jit(solution)/shard_map/ppermute | solution.py:456
  17.6 63.1 %sweep.1 = (f32[4,256,128]{2,1,0:T(8,128)S(1)}, bf16[4,40,128]{2,1,0:T(8,128)(2,1)S(1)}, bf16[4,24,128]{2,1,0:T(8,128)(2,1)S(1)}, bf16[4,256,128]{2,1,0:T(8,128)...) custom-call(s32[2]{0:T(128)S(1)} %pad_add_fusion.refs_0_, ...), custom_call_target="tpu_custom_call" | custom-call | flops 51539607552 | bytes 16777216 | tf_op jit(solution)/shard_map/sweep/pallas_call | solution.py:380
  80.7 0.8 copy-done
  81.5 0.6 collective-permute-start.3
  82.1 2.1 %collective-permute-start.5 = (bf16[4,40,128]{2,1,0:T(8,128)(2,1)S(1)}, bf16[4,40,128]{2,1,0:T(8,128)(2,1)S(1)}, u32[]{:S(2)}, u32[]{:S(2)}) collective-permute-start(bf16[4,40,128]{2,1,0:T(8,128)(2,1)S(1)} %get-tuple-element.20), channel_id=1, source_target_pairs={{0,15},{1,0},{2,1},{3,2},{4,3},{5,4},{6,5},{7,6},{8,7},{9,8},{10,9... | collective-permute-start | bytes 122888 | tf_op jit(solution)/shard_map/ppermute | solution.py:491
  84.2 2.1 %collective-permute-start.7 = (bf16[4,40,128]{2,1,0:T(8,128)(2,1)S(1)}, bf16[4,40,128]{2,1,0:T(8,128)(2,1)S(1)}, u32[]{:S(2)}, u32[]{:S(2)}) collective-permute-start(bf16[4,40,128]{2,1,0:T(8,128)(2,1)S(1)} %get-tuple-element.22), channel_id=1, source_target_pairs={{0,31},{1,16},{2,17},{3,18},{4,19},{5,20},{6,21},{7,22},{8,23},{9,... | collective-permute-start | bytes 122888 | tf_op jit(solution)/shard_map/ppermute | solution.py:493
  86.3 5.9 %collective-permute-done.4.own_start = bf16[4,24,128]{2,1,0:T(8,128)(2,1)S(1)} collective-permute-done((bf16[4,24,128]{2,1,0:T(8,128)(2,1)S(1)}, bf16[4,24,128]{2,1,0:T(8,128)(2,1)S(1)}, u32[]{:S(2)}, u32[]{:S(2)}) %collective-permute-start.4) | collective-permute-done | bytes 24608 | tf_op jit(solution)/shard_map/ppermute | solution.py:490
  92.3 0.9 collective-permute-done.6.peer_start
  93.2 0.5 copy-done.8
  93.8 0.1 copy-done.1
  93.9 2.0 %finish.1 = f32[4,256,128]{2,1,0:T(8,128)} custom-call(f32[4,256,128]{2,1,0:T(8,128)} %copy-done, bf16[4,256,128]{2,1,0:T(8,128)(2,1)} %copy-done.1, bf16[4,24,128]{2,1,0:T(8,128)(2,1)} %copy-done.7, bf16[4,40,128]{2,1,0:T(8,128)(2,1)} %copy-done.5, bf16[4,24,128]{2,1,0:T(8,128)(2,1)} %copy-done.8, bf16[4,40,128]{2,1,0:T(8,128)(2,1)} %copy-done.6), custom_call_target="tpu_custom_call" | custom-call | tf_op jit(solution)/shard_map/finish/pallas_call | solution.py:495
  (38 shorter events, 0.3 us)
Async XLA Ops:
  0.0 6.8 %copy-start.10 = (s32[4,64]{1,0:T(4,128)S(1)}, s32[4,64]{1,0:T(4,128)}, u32[]{:S(2)}) copy-start(s32[4,64]{1,0:T(4,128)} %param.17) | copy-start | bytes 3076
  0.0 6.8 %copy-start.2 = (bf16[3,3,3,32,32]{4,3,2,1,0:T(8,128)(2,1)S(1)}, bf16[3,3,3,32,32]{4,3,2,1,0:T(8,128)(2,1)}, u32[]{:S(2)}) copy-start(bf16[3,3,3,32,32]{4,3,2,1,0:T(8,128)(2,1)} %param.12) | copy-start | bytes 165892
  0.0 6.8 %copy-start.3 = (bf16[3,3,3,32,32]{4,3,2,1,0:T(8,128)(2,1)S(1)}, bf16[3,3,3,32,32]{4,3,2,1,0:T(8,128)(2,1)}, u32[]{:S(2)}) copy-start(bf16[3,3,3,32,32]{4,3,2,1,0:T(8,128)(2,1)} %param.13) | copy-start | bytes 165892
  2.2 13.0 %collective-permute-start.1 = (bf16[2,8,256]{2,1,0:T(8,128)(2,1)}, bf16[2,8,256]{2,1,0:T(8,128)(2,1)S(1)}, u32[]{:S(2)}, u32[]{:S(2)}) collective-permute-start(bf16[2,8,256]{2,1,0:T(8,128)(2,1)} %get-tuple-element.15), channel_id=1, source_target_pairs={{0,17},{1,18},{2,19},{3,20},{4,21},{5,22},{6,23},{7,24},{8,25},{9,... | collective-permute-start | bytes 24584 | tf_op jit(solution)/shard_map/ppermute | solution.py:457
  4.7 10.6 %collective-permute-start.2 = (bf16[64,8,256]{2,1,0:T(8,128)(2,1)}, bf16[64,8,256]{2,1,0:T(8,128)(2,1)S(1)}, u32[]{:S(2)}, u32[]{:S(2)}) collective-permute-start(bf16[64,8,256]{2,1,0:T(8,128)(2,1)} %get-tuple-element.16), channel_id=1, source_target_pairs={{0,1},{1,2},{2,3},{3,4},{4,5},{5,6},{6,7},{7,8},{8,9},{9,10},{10,1... | collective-permute-start | bytes 786440 | tf_op jit(solution)/shard_map/ppermute | solution.py:477
  6.3 11.3 %collective-permute-start = (bf16[3,256,256]{2,1,0:T(8,128)(2,1)}, bf16[3,256,256]{2,1,0:T(8,128)(2,1)S(1)}, u32[]{:S(2)}, u32[]{:S(2)}) collective-permute-start(bf16[3,256,256]{2,1,0:T(8,128)(2,1)} %get-tuple-element.14), channel_id=1, source_target_pairs={{0,16},{16,0},{1,17},{17,1},{2,18},{18,2},{3,19},{19,3},{4,20},{20... | collective-permute-start | bytes 1179656 | tf_op jit(solution)/shard_map/ppermute | solution.py:456
  7.4 1.0 %copy-start.9 = (f32[4,64,8]{1,2,0:T(8,128)S(1)}, f32[4,64,8]{1,2,0:T(8,128)}, u32[]{:S(2)}) copy-start(f32[4,64,8]{1,2,0:T(8,128)} %param.15) | copy-start | bytes 24580
  7.5 1.0 %copy-start.11 = (s32[4,64]{1,0:T(4,128)S(1)}, s32[4,64]{1,0:T(4,128)}, u32[]{:S(2)}) copy-start(s32[4,64]{1,0:T(4,128)} %param.16) | copy-start | bytes 3076
  7.7 1.0 %copy-start.4 = (f32[4,64,8,8]{1,3,2,0:T(8,128)S(1)}, f32[4,64,8,8]{1,3,2,0:T(8,128)}, u32[]{:S(2)}) copy-start(f32[4,64,8,8]{1,3,2,0:T(8,128)} %param.14) | copy-start | bytes 196612
  80.7 0.8 copy-start
  81.5 11.7 %collective-permute-start.3 = (bf16[4,256,128]{2,1,0:T(8,128)(2,1)S(1)}, bf16[4,256,128]{2,1,0:T(8,128)(2,1)S(1)}, u32[]{:S(2)}, u32[]{:S(2)}) collective-permute-start(bf16[4,256,128]{2,1,0:T(8,128)(2,1)S(1)} %get-tuple-element.18), channel_id=1, source_target_pairs={{0,16},{16,0},{1,17},{17,1},{2,18},{18,2},{3,19},{19,3},{4,20},{20... | collective-permute-start | bytes 786440 | tf_op jit(solution)/shard_map/ppermute | solution.py:489
  82.1 11.1 %collective-permute-start.5 = (bf16[4,40,128]{2,1,0:T(8,128)(2,1)S(1)}, bf16[4,40,128]{2,1,0:T(8,128)(2,1)S(1)}, u32[]{:S(2)}, u32[]{:S(2)}) collective-permute-start(bf16[4,40,128]{2,1,0:T(8,128)(2,1)S(1)} %get-tuple-element.20), channel_id=1, source_target_pairs={{0,15},{1,0},{2,1},{3,2},{4,3},{5,4},{6,5},{7,6},{8,7},{9,8},{10,9... | collective-permute-start | bytes 122888 | tf_op jit(solution)/shard_map/ppermute | solution.py:491
  84.2 9.0 %collective-permute-start.7 = (bf16[4,40,128]{2,1,0:T(8,128)(2,1)S(1)}, bf16[4,40,128]{2,1,0:T(8,128)(2,1)S(1)}, u32[]{:S(2)}, u32[]{:S(2)}) collective-permute-start(bf16[4,40,128]{2,1,0:T(8,128)(2,1)S(1)} %get-tuple-element.22), channel_id=1, source_target_pairs={{0,31},{1,16},{2,17},{3,18},{4,19},{5,20},{6,21},{7,22},{8,23},{9,... | collective-permute-start | bytes 122888 | tf_op jit(solution)/shard_map/ppermute | solution.py:493
  86.3 5.9 %collective-permute-start.4 = (bf16[4,24,128]{2,1,0:T(8,128)(2,1)S(1)}, bf16[4,24,128]{2,1,0:T(8,128)(2,1)S(1)}, u32[]{:S(2)}, u32[]{:S(2)}) collective-permute-start(bf16[4,24,128]{2,1,0:T(8,128)(2,1)S(1)} %get-tuple-element.19), channel_id=1, source_target_pairs={{0,1},{1,2},{2,3},{3,4},{4,5},{5,6},{6,7},{7,8},{8,9},{9,10},{10,1... | collective-permute-start | bytes 73736 | tf_op jit(solution)/shard_map/ppermute | solution.py:490
  86.3 6.8 %collective-permute-start.6 = (bf16[4,24,128]{2,1,0:T(8,128)(2,1)S(1)}, bf16[4,24,128]{2,1,0:T(8,128)(2,1)S(1)}, u32[]{:S(2)}, u32[]{:S(2)}) collective-permute-start(bf16[4,24,128]{2,1,0:T(8,128)(2,1)S(1)} %get-tuple-element.21), channel_id=1, source_target_pairs={{0,17},{1,18},{2,19},{3,20},{4,21},{5,22},{6,23},{7,24},{8,25},{9,... | collective-permute-start | bytes 73736 | tf_op jit(solution)/shard_map/ppermute | solution.py:492
  92.3 0.9 copy-start.7
  93.2 0.6 copy-start.8
  93.2 0.6 copy-start.5
  93.2 0.6 copy-start.6
  93.2 0.7 copy-start.1
